TPU v7x, 8 devices: a whole 2x2x1 slice. The times are simulated.
8 devices in a mesh: dp: 1 (over z), sp: 8 (over y, x, core).
Axes of the slice: x: 2, y: 2, z: 1, core: 2. Of those that a mesh axis runs over, the one named last changes fastest.
Arguments:
- x_in: bfloat16 [1, 8192, 3840], P('dp', 'sp')
- dy_in: bfloat16 [1, 8192, 3840], P('dp', 'sp')
- positions: int32 [8192], P(('dp', 'sp'))
- w_q: bfloat16 [3840, 4096], replicated
- w_k: bfloat16 [3840, 2048], replicated
- w_v: bfloat16 [3840, 2048], replicated
- w_o: bfloat16 [4096, 3840], replicated
- w_pre: float32 [3840], replicated
- w_post: float32 [3840], replicated
- q_norm: float32 [256], replicated
- k_norm: float32 [256], replicated
Outputs:
- output 1: bfloat16 [1, 8192, 3840], P('dp', 'sp')
- output 2: bfloat16 [1, 8192, 3840], P('dp', 'sp')
- output 3: bfloat16 [3840, 4096], P('dp')
- output 4: bfloat16 [3840, 2048], P('dp')
- output 5: bfloat16 [3840, 2048], P('dp')
- output 6: bfloat16 [4096, 3840], P('dp')
- output 7: float32 [3840], P('dp')
- output 8: float32 [3840], P('dp')
- output 9: float32 [256], P('dp')
- output 10: float32 [256], P('dp')
All inputs are finite; a program needn't handle non-finite values.
Results may differ from a plain program's by a relative error of at most 0.02.
Values are sent between devices in bfloat16 or wider.
A program may use at most 1 GiB of HBM per device.

v0:
```python
import functools
import jax
import jax.numpy as jnp
from jax import lax
from jax.sharding import PartitionSpec as P

EPS = 1e-6
ROPE_BASE = 1000000.0
ROPE_SCALE = 8.0
NEG_BIG = -1e30
Q_BLOCK = 1024


def rms_scale(x_f32, weight):
    inv_rms = lax.rsqrt(jnp.mean(x_f32 * x_f32, axis=-1, keepdims=True) + EPS)
    return x_f32 * inv_rms * (1.0 + weight)


def pre_norm(x_f32, weight):
    return rms_scale(x_f32, weight).astype(jnp.bfloat16)


def post_norm(proj, weight):
    return rms_scale(proj.astype(jnp.float32), weight)


def rope_tables(positions, head):
    half_dim = head // 2
    inv_freq = ROPE_BASE ** (-jnp.arange(half_dim, dtype=jnp.float32) * 2.0 / head)
    angles = (positions.astype(jnp.float32) / ROPE_SCALE)[:, None] * inv_freq[None, :]
    return jnp.cos(angles), jnp.sin(angles)


def norm_rope(heads_bf, weight, cosines, sines):
    half_dim = heads_bf.shape[-1] // 2
    normed = rms_scale(heads_bf.astype(jnp.float32), weight)
    first = normed[..., :half_dim]
    second = normed[..., half_dim:]
    cos_b = cosines[None, :, None, :]
    sin_b = sines[None, :, None, :]
    rotated = jnp.concatenate([first * cos_b - second * sin_b, second * cos_b + first * sin_b], axis=-1)
    return rotated.astype(jnp.bfloat16)


def causal_mask(start, block, end):
    row_ids = start + jnp.arange(block)
    col_ids = jnp.arange(end)
    return row_ids[:, None] >= col_ids[None, :]


def attention_fwd(q_all, k_all, v_all):
    batch, seq, q_heads, head = q_all.shape
    kv_loc = k_all.shape[2]
    scale = head ** -0.5
    block = min(Q_BLOCK, seq)
    q_grp = q_all.reshape(batch, seq, kv_loc, q_heads // kv_loc, head)
    pieces = []
    row_lse = []
    for index in range(seq // block):
        start = index * block
        end = start + block
        scores = jnp.einsum('bqkgh,bskh->bkgqs', q_grp[:, start:end], k_all[:, :end], preferred_element_type=jnp.float32) * scale
        scores = jnp.where(causal_mask(start, block, end), scores, NEG_BIG)
        row_max = jnp.max(scores, axis=-1, keepdims=True)
        exp_scores = jnp.exp(scores - row_max)
        row_sum = jnp.sum(exp_scores, axis=-1, keepdims=True)
        attn_prob = (exp_scores / row_sum).astype(jnp.bfloat16)
        pieces.append(jnp.einsum('bkgqs,bskh->bqkgh', attn_prob, v_all[:, :end], preferred_element_type=jnp.float32).astype(jnp.bfloat16))
        row_lse.append(row_max + jnp.log(row_sum))
    return jnp.concatenate(pieces, axis=1).reshape(batch, seq, q_heads, head), row_lse


def attention_bwd(q_all, k_all, v_all, row_lse, d_out):
    batch, seq, q_heads, head = q_all.shape
    kv_loc = k_all.shape[2]
    per_kv = q_heads // kv_loc
    scale = head ** -0.5
    block = min(Q_BLOCK, seq)
    q_grp = q_all.reshape(batch, seq, kv_loc, per_kv, head)
    do_grp = d_out.reshape(batch, seq, kv_loc, per_kv, head)
    dk_acc = jnp.zeros(k_all.shape, jnp.float32)
    dv_acc = jnp.zeros(v_all.shape, jnp.float32)
    dq_pieces = []
    for index in range(seq // block):
        start = index * block
        end = start + block
        q_blk = q_grp[:, start:end]
        do_blk = do_grp[:, start:end]
        k_pre = k_all[:, :end]
        v_pre = v_all[:, :end]
        scores = jnp.einsum('bqkgh,bskh->bkgqs', q_blk, k_pre, preferred_element_type=jnp.float32) * scale
        scores = jnp.where(causal_mask(start, block, end), scores, NEG_BIG)
        attn_prob = jnp.exp(scores - row_lse[index])
        d_prob = jnp.einsum('bqkgh,bskh->bkgqs', do_blk, v_pre, preferred_element_type=jnp.float32)
        d_score = (attn_prob * (d_prob - jnp.sum(d_prob * attn_prob, axis=-1, keepdims=True)) * scale).astype(jnp.bfloat16)
        dq_pieces.append(jnp.einsum('bkgqs,bskh->bqkgh', d_score, k_pre, preferred_element_type=jnp.float32).astype(jnp.bfloat16))
        dk_part = jnp.einsum('bkgqs,bqkgh->bskh', d_score, q_blk, preferred_element_type=jnp.float32)
        dv_part = jnp.einsum('bkgqs,bqkgh->bskh', attn_prob.astype(jnp.bfloat16), do_blk, preferred_element_type=jnp.float32)
        dk_acc = lax.dynamic_update_slice(dk_acc, dk_acc[:, :end] + dk_part, (0, 0, 0, 0))
        dv_acc = lax.dynamic_update_slice(dv_acc, dv_acc[:, :end] + dv_part, (0, 0, 0, 0))
    dq_all = jnp.concatenate(dq_pieces, axis=1).reshape(batch, seq, q_heads, head)
    return dq_all, dk_acc.astype(jnp.bfloat16), dv_acc.astype(jnp.bfloat16)


def fold_copies(grad_wide, kv_heads, rep):
    if rep == 1:
        return grad_wide
    batch, seq_loc, wide, head = grad_wide.shape
    summed = jnp.sum(grad_wide.reshape(batch, seq_loc, kv_heads, rep, head), axis=3, dtype=jnp.float32)
    return summed.astype(jnp.bfloat16)


def solution(mesh):
    group = mesh.shape['sp']

    def to_heads(arr):
        return lax.all_to_all(arr, 'sp', 2, 1, tiled=True)

    def to_tokens(arr):
        return lax.all_to_all(arr, 'sp', 1, 2, tiled=True)

    def device_step(x_in, dy_in, positions, w_q, w_k, w_v, w_o, w_pre, w_post, q_norm, k_norm):
        batch, seq_loc, width = x_in.shape
        head = q_norm.shape[0]
        heads = w_q.shape[1] // head
        kv_heads = w_k.shape[1] // head
        rep = max(1, group // kv_heads)
        x_f32 = x_in.astype(jnp.float32)
        normed, pre_pull = jax.vjp(pre_norm, x_f32, w_pre)
        q_proj = jnp.einsum('bsd,dn->bsn', normed, w_q, preferred_element_type=jnp.float32).astype(jnp.bfloat16).reshape(batch, seq_loc, heads, head)
        k_proj = jnp.einsum('bsd,dn->bsn', normed, w_k, preferred_element_type=jnp.float32).astype(jnp.bfloat16).reshape(batch, seq_loc, kv_heads, head)
        v_proj = jnp.einsum('bsd,dn->bsn', normed, w_v, preferred_element_type=jnp.float32).astype(jnp.bfloat16).reshape(batch, seq_loc, kv_heads, head)
        cosines, sines = rope_tables(positions, head)
        q_rot, q_pull = jax.vjp(functools.partial(norm_rope, cosines=cosines, sines=sines), q_proj, q_norm)
        k_rot, k_pull = jax.vjp(functools.partial(norm_rope, cosines=cosines, sines=sines), k_proj, k_norm)
        q_all = to_heads(q_rot)
        k_all = to_heads(jnp.repeat(k_rot, rep, axis=2))
        v_all = to_heads(jnp.repeat(v_proj, rep, axis=2))
        o_all, row_lse = attention_fwd(q_all, k_all, v_all)
        o_flat = to_tokens(o_all).reshape(batch, seq_loc, heads * head)
        proj = jnp.einsum('bsn,nd->bsd', o_flat, w_o, preferred_element_type=jnp.float32).astype(jnp.bfloat16)
        post, post_pull = jax.vjp(post_norm, proj, w_post)
        y_out = (x_f32 + post).astype(jnp.bfloat16)
        dy_f32 = dy_in.astype(jnp.float32)
        d_proj, dw_post = post_pull(dy_f32)
        dw_o = jnp.einsum('bsn,bsd->nd', o_flat, d_proj, preferred_element_type=jnp.float32)
        d_oflat = jnp.einsum('bsd,nd->bsn', d_proj, w_o, preferred_element_type=jnp.float32).astype(jnp.bfloat16)
        d_oall = to_heads(d_oflat.reshape(batch, seq_loc, heads, head))
        dq_all, dk_all, dv_all = attention_bwd(q_all, k_all, v_all, row_lse, d_oall)
        dq_rot = to_tokens(dq_all)
        dk_rot = fold_copies(to_tokens(dk_all), kv_heads, rep)
        dv_proj = fold_copies(to_tokens(dv_all), kv_heads, rep)
        dq_proj, dq_norm = q_pull(dq_rot)
        dk_proj, dk_norm = k_pull(dk_rot)
        dq_flat = dq_proj.reshape(batch, seq_loc, heads * head)
        dk_flat = dk_proj.reshape(batch, seq_loc, kv_heads * head)
        dv_flat = dv_proj.reshape(batch, seq_loc, kv_heads * head)
        dw_q = jnp.einsum('bsd,bsn->dn', normed, dq_flat, preferred_element_type=jnp.float32)
        dw_k = jnp.einsum('bsd,bsn->dn', normed, dk_flat, preferred_element_type=jnp.float32)
        dw_v = jnp.einsum('bsd,bsn->dn', normed, dv_flat, preferred_element_type=jnp.float32)
        d_normed = (jnp.einsum('bsn,dn->bsd', dq_flat, w_q, preferred_element_type=jnp.float32)
                    + jnp.einsum('bsn,dn->bsd', dk_flat, w_k, preferred_element_type=jnp.float32)
                    + jnp.einsum('bsn,dn->bsd', dv_flat, w_v, preferred_element_type=jnp.float32)).astype(jnp.bfloat16)
        dx_norm, dw_pre = pre_pull(d_normed)
        dx_out = (dy_f32 + dx_norm).astype(jnp.bfloat16)
        sums = lax.psum((dw_q, dw_k, dw_v, dw_o, dw_pre, dw_post, dq_norm, dk_norm), 'sp')
        return (y_out, dx_out, sums[0].astype(jnp.bfloat16), sums[1].astype(jnp.bfloat16), sums[2].astype(jnp.bfloat16), sums[3].astype(jnp.bfloat16), sums[4], sums[5], sums[6], sums[7])

    token_spec = P('dp', 'sp', None)
    return jax.shard_map(device_step, mesh=mesh,
                         in_specs=(token_spec, token_spec, P(('dp', 'sp')), P(None, None), P(None, None), P(None, None), P(None, None), P(None), P(None), P(None), P(None)),
                         out_specs=(token_spec, token_spec, P('dp', None), P('dp', None), P('dp', None), P('dp', None), P('dp'), P('dp'), P('dp'), P('dp')),
                         check_vma=False)
```

profile of v0, /device:TPU:0, one launch (start us, length us, event | category | flops | bytes accessed | tf_op | source)
XLA Modules:
  0.0 4548.8 jit_solution(12219907879477430847)
XLA Ops:
  6.8 40.8 convert_convert_fusion
  47.6 15.8 copy.798
  63.4 16.7 copy.623
  130.2 20.6 convert_convert_fusion.1
  159.5 22.1 convolution_convert_fusion.2
  253.3 21.9 all-to-all-done.1
  309.8 17.1 fusion.332
  326.9 19.8 fusion.333
  346.7 23.0 fusion.334
  374.2 26.8 fusion.335
  459.9 15.0 fusion.287
  474.9 16.4 fusion.22
  491.3 17.9 fusion.281
  509.2 19.3 fusion.16
  528.5 20.4 fusion.275
  548.9 18.9 fusion.9
  567.8 22.6 fusion.269
  590.4 29.0 fusion.336
  619.4 21.8 fusion.4
  641.1 25.2 fusion.263
  666.4 21.0 copy.635
  696.7 89.1 %all-to-all-done.3 = bf16[1,8192,2,256]{3,2,0,1:T(2,128)(2,1)} async-done(((bf16[1,8192,2,256]{3,2,0,1:T(2,128)(2,1)}), bf16[1,8192,2,256]{3,2,0,1:T(2,128)(2,1)}, u32[]{:S(2)}, u32[]{:S(2)}) %all-to-all-start.3) | async-done | bytes 8388640 | tf_op jit(solution)/shard_map/all_to_all | solution.py:120
  805.1 40.3 fusion.92
  845.5 17.3 fusion.90
  862.7 56.7 %convolution_convert_fusion = bf16[1024,4096]{1,0:T(8,128)(2,1)} fusion(bf16[4096,3840]{1,0:T(8,128)(2,1)} %param.17, bf16[1024,3840]{1,0:T(8,128)(2,1)} %copy-done.5, bf16[1,1024,3840]{2,1,0:T(8,128)(2,1)} %param.12, f32[1024]{0:T(1024)S(1)} %multiply_multiply_fusion.5, f32[1024]{0:T(1024)S(1)} %fusion.316, f32[3840]{0:T(1024)S(1)} %broadcast_add_fusion), kind=kOutput, calls=%fused_computation.222 | convolution fusion | flops 32247906304 | bytes 55598080 | tf_op jit(solution)/shard_map/bsd,nd->bsn/dot_general | solution.py:147
  943.0 44.1 fusion.317
  987.1 49.9 %all-to-all-done.4 = bf16[1,1024,16,256]{3,1,0,2:T(8,128)(2,1)} async-done(((bf16[1,1024,16,256]{3,1,0,2:T(8,128)(2,1)}), bf16[1,1024,16,256]{3,1,0,2:T(8,128)(2,1)}, u32[]{:S(2)}, u32[]{:S(2)}) %all-to-all-start.4) | async-done | bytes 8388640 | tf_op jit(solution)/shard_map/all_to_all | solution.py:117
  1092.6 18.1 fusion.48
  1125.3 26.6 fusion.27
  1151.9 16.6 fusion.172
  1168.5 32.5 fusion.17
  1201.0 19.2 fusion.162
  1220.2 33.7 fusion.11
  1253.9 23.0 fusion.148
  1276.9 43.0 fusion.5
  1319.9 25.7 fusion.123
  1345.6 49.1 %fusion = (f32[2,1024]{1,0:T(2,128)}, f32[8192,1024,2]{1,0,2:T(8,128)}) fusion(f32[1,1,2,1024,8192]{3,4,2,1,0:T(8,128)} %get-tuple-element.52, f32[2,1024]{1,0:T(2,128)S(1)} %copy-done.26, bf16[8192,256,1]{1,0,2:T(8,128)(2,1)} %bitcast.339, bf16[1,8192,1,2,256]{4,1,3,2,0:T(8,128)(2,1)} %bitcast.1048), kind=kOutput, calls=%fused_computation.3 | convolution fusion | flops 8640264192 | bytes 139476992 | tf_op jit(solution)/shard_map/bqkgh,bskh->bkgqs/dot_general | solution.py:94
  1394.7 27.6 fusion.113
  1422.3 17.7 copy.705
  1440.6 43.6 reduce.37
  1495.5 16.0 fusion.132
  1527.4 15.9 fusion.102
  1563.8 28.3 fusion.76
  1618.0 34.0 fusion.59
  1677.1 40.8 fusion.47
  1717.9 46.7 %fusion.39 = bf16[2,1024,7168]{1,2,0:T(8,128)(2,1)} fusion(f32[7168,1024,2]{1,0,2:T(8,128)} %get-tuple-element.68, f32[1,1,2,1024,7168]{3,4,2,1,0:T(8,128)} %get-tuple-element.50, f32[2,1024]{1,0:T(2,128)S(1)} %copy-done.47, f32[2,1024]{1,0:T(2,128)S(1)} %copy-done.23), kind=kLoop, calls=%fused_computation.73 | loop fusion | flops 73400320 | bytes 146817024 | tf_op jit(solution)/shard_map/reshape.182
  1764.6 53.6 %fusion.26 = bf16[2,1024,8192]{1,2,0:T(8,128)(2,1)} fusion(f32[8192,1024,2]{1,0,2:T(8,128)} %get-tuple-element.70, f32[1,1,2,1024,8192]{3,4,2,1,0:T(8,128)} %get-tuple-element.52, f32[2,1024]{1,0:T(2,128)S(1)} %copy-done.46, f32[2,1024]{1,0:T(2,128)S(1)} %copy-done.27), kind=kLoop, calls=%fused_computation.49 | loop fusion | flops 83886080 | bytes 167788544 | tf_op jit(solution)/shard_map/reshape.190
  1818.3 16.1 fusion.152
  1834.3 17.3 fusion.127
  1851.6 18.8 fusion.116
  1870.4 17.7 copy.684
  1888.2 43.5 reduce.38
  1955.3 15.2 fusion.305
  1970.5 20.5 all-to-all-done.6
  1994.7 17.1 fusion.297
  2011.7 21.0 copy.664
  2076.4 25.4 fusion.322
  2123.2 25.6 fusion.320
  2148.8 22.0 fusion.338
  2170.8 23.4 copy.665
  2231.4 40.9 fusion.337
  2272.2 43.8 fusion.324
  2316.1 27.8 fusion.85
  2355.4 2193.2 %all-reduce.8 = (bf16[3840,4096]{1,0:T(8,128)(2,1)}, bf16[3840,2048]{1,0:T(8,128)(2,1)}, bf16[3840,2048]{1,0:T(8,128)(2,1)}, bf16[4096,3840]{1,0:T(8,128)(2,1)},...) all-reduce(f32[3840,4096]{1,0:T(8,128)} %fusion.324, ...), channel_id=1, replica_groups=mesh['dp'=1,'sp'=8] {'sp'}, use_global_device_ids=true, to_apply=%region_32.33 | all-reduce | flops 47194112 | bytes 283181056 | tf_op jit(solution)/shard_map/psum | solution.py:166
  (337 shorter events, 596.5 us)
Async XLA Ops:
  1.4 158.1 %copy-start.37 = (f32[3840]{0:T(1024)}, f32[3840]{0:T(1024)S(1)}, u32[]{:S(2)}) copy-start(f32[3840]{0:T(1024)S(1)} %broadcast_add_fusion.1) | copy-start | bytes 46084
  6.8 152.7 %copy-start.76 = (f32[1024]{0:T(1024)}, f32[1024]{0:T(1024)S(1)}, u32[]{:S(2)}) copy-start(f32[1024]{0:T(1024)S(1)} %fusion.315) | copy-start | bytes 12292
  63.4 16.7 copy-start.84
  90.9 37.5 copy-start.3
  90.9 37.7 copy-start.1
  123.9 99.0 %all-to-all-start.2 = ((bf16[1,1024,16,256]{3,1,0,2:T(8,128)(2,1)}), bf16[1,1024,16,256]{3,1,0,2:T(8,128)(2,1)}, u32[]{:S(2)}, u32[]{:S(2)}) async-start(bf16[1,1024,16,256]{3,1,0,2:T(8,128)(2,1)} %copy.624), calls=%async_computation.2 | async-start | bytes 16777216 | tf_op jit(solution)/shard_map/all_to_all | solution.py:117
  128.7 60.7 %copy-start.6 = (f32[1024,128]{1,0:T(8,128)}, f32[1024,128]{1,0:T(8,128)S(1)}, u32[]{:S(2)}) copy-start(f32[1024,128]{1,0:T(8,128)S(1)} %copy.620) | copy-start | bytes 1572868
  128.9 60.5 %copy-start.8 = (f32[1024,128]{1,0:T(8,128)}, f32[1024,128]{1,0:T(8,128)S(1)}, u32[]{:S(2)}) copy-start(f32[1024,128]{1,0:T(8,128)S(1)} %copy.619) | copy-start | bytes 1572868
  159.5 26.4 copy-start.28
  222.9 52.3 %all-to-all-start.1 = ((bf16[1,1024,8,256]{3,1,0,2:T(8,128)(2,1)}), bf16[1,1024,8,256]{3,1,0,2:T(8,128)(2,1)}, u32[]{:S(2)}, u32[]{:S(2)}) async-start(bf16[1,1024,8,256]{3,1,0,2:T(8,128)(2,1)} %maximum_bitcast_fusion), calls=%async_computation.1 | async-start | bytes 8388608 | tf_op jit(solution)/shard_map/all_to_all | solution.py:117
  275.2 125.8 %all-to-all-start = ((bf16[1,1024,8,256]{3,1,0,2:T(8,128)(2,1)}), bf16[1,1024,8,256]{3,1,0,2:T(8,128)(2,1)}, u32[]{:S(2)}, u32[]{:S(2)}) async-start(bf16[1,1024,8,256]{3,1,0,2:T(8,128)(2,1)} %copy.615), calls=%async_computation | async-start | bytes 8388608 | tf_op jit(solution)/shard_map/all_to_all | solution.py:117
  285.6 115.4 %copy-start.65 = (f32[2,1024]{1,0:T(2,128)}, f32[2,1024]{1,0:T(2,128)S(1)}, u32[]{:S(2)}) copy-start(f32[2,1024]{1,0:T(2,128)S(1)} %get-tuple-element.37) | copy-start | bytes 24580
  296.3 118.8 %copy-start.42 = (f32[2,1024]{1,0:T(2,128)}, f32[2,1024]{1,0:T(2,128)S(1)}, u32[]{:S(2)}) copy-start(f32[2,1024]{1,0:T(2,128)S(1)} %get-tuple-element.39) | copy-start | bytes 24580
  374.2 26.8 copy-start.67
  435.1 11.7 copy-start.59
  435.1 11.7 copy-start.70
  459.8 15.0 copy-start.72
  459.8 15.0 copy-start.54
  491.3 18.0 copy-start.61
  491.3 17.9 copy-start.56
  528.5 20.4 copy-start.63
  528.5 20.4 copy-start.58
  687.5 98.3 %all-to-all-start.3 = ((bf16[1,8192,2,256]{3,2,0,1:T(2,128)(2,1)}), bf16[1,8192,2,256]{3,2,0,1:T(2,128)(2,1)}, u32[]{:S(2)}, u32[]{:S(2)}) async-start(bf16[1,8192,2,256]{3,2,0,1:T(2,128)(2,1)} %copy.635), calls=%async_computation.3 | async-start | bytes 16777216 | tf_op jit(solution)/shard_map/all_to_all | solution.py:120
  845.4 17.3 copy-start.5
  939.0 97.9 %all-to-all-start.4 = ((bf16[1,1024,16,256]{3,1,0,2:T(8,128)(2,1)}), bf16[1,1024,16,256]{3,1,0,2:T(8,128)(2,1)}, u32[]{:S(2)}, u32[]{:S(2)}) async-start(bf16[1,1024,16,256]{3,1,0,2:T(8,128)(2,1)} %copy.638), calls=%async_computation.4 | async-start | bytes 16777216 | tf_op jit(solution)/shard_map/all_to_all | solution.py:117
  1044.4 14.1 slice-start.18
  1058.5 13.0 slice-start.14
  1058.5 13.0 slice-start.15
  1058.5 13.0 slice-start.16
  1110.6 14.7 copy-start.30
  1151.9 16.6 copy-start.24
  1201.0 19.2 copy-start.18
  1253.9 23.0 copy-start.22
  1319.9 25.7 copy-start.26
  1440.6 50.6 %copy-start.15 = (f32[1,1024,1,256]{1,3,2,0:T(8,128)S(1)}, f32[1,1024,1,256]{1,3,2,0:T(8,128)}, u32[]{:S(2)}) copy-start(f32[1,1024,1,256]{1,3,2,0:T(8,128)} %convolution_bitcast_fusion.7) | copy-start | bytes 3145732
  1495.5 31.8 slice-start.4
  1495.5 31.8 slice-start.5
  1495.5 31.8 slice-start.6
  1495.5 31.8 slice-start.7
  1511.5 15.8 slice-start.8
  1604.0 14.0 copy-start.25
  1604.0 14.0 copy-start.49
  1663.8 13.2 copy-start.19
  1663.8 13.2 copy-start.48
  1677.1 40.8 copy-start.23
  1677.1 40.8 copy-start.47
  1717.9 46.8 %copy-start.27 = (f32[2,1024]{1,0:T(2,128)S(1)}, f32[2,1024]{1,0:T(2,128)}, u32[]{:S(2)}) copy-start(f32[2,1024]{1,0:T(2,128)} %log_add_fusion) | copy-start | bytes 24580
  1717.9 46.7 %copy-start.46 = (f32[2,1024]{1,0:T(2,128)S(1)}, f32[2,1024]{1,0:T(2,128)}, u32[]{:S(2)}) copy-start(f32[2,1024]{1,0:T(2,128)} %get-tuple-element.69) | copy-start | bytes 24580
  1938.6 52.3 %all-to-all-start.6 = ((bf16[8,2,131072]{2,1,0:T(2,128)(2,1)}), bf16[8,2,131072]{2,1,0:T(2,128)(2,1)}, u32[]{:S(2)}, u32[]{:S(2)}) async-start(bf16[8,2,131072]{2,1,0:T(2,128)(2,1)} %reshape.1184), calls=%async_computation.6 | async-start | bytes 8388608 | tf_op jit(solution)/shard_map/all_to_all | solution.py:120
  1991.0 81.7 %all-to-all-start.7 = ((bf16[8,2,131072]{2,1,0:T(2,128)(2,1)}), bf16[8,2,131072]{2,1,0:T(2,128)(2,1)}, u32[]{:S(2)}, u32[]{:S(2)}) async-start(bf16[8,2,131072]{2,1,0:T(2,128)(2,1)} %reshape.1186), calls=%async_computation.7 | async-start | bytes 8388608 | tf_op jit(solution)/shard_map/all_to_all | solution.py:120
  2072.7 98.1 %all-to-all-start.5 = ((bf16[1,8192,2,256]{3,2,0,1:T(2,128)(2,1)}), bf16[1,8192,2,256]{3,2,0,1:T(2,128)(2,1)}, u32[]{:S(2)}, u32[]{:S(2)}) async-start(bf16[1,8192,2,256]{3,2,0,1:T(2,128)(2,1)} %copy.664), calls=%async_computation.5 | async-start | bytes 16777216 | tf_op jit(solution)/shard_map/all_to_all | solution.py:120
  2123.2 25.6 copy-start.11
  2170.8 23.4 copy-start.2
  2170.8 23.4 copy-start.4
  2194.2 14.1 slice-start
  2194.2 14.1 slice-start.1
  2194.2 15.2 slice-start.2
  2194.3 16.4 slice-start.3
  2194.3 16.4 copy-start.14
  2194.3 16.4 copy-start.75
  2272.2 43.8 copy-start.10
  2316.1 27.8 copy-start.41
  2343.9 11.5 copy-start.39
  2343.9 11.5 copy-start.82
  (50 other events, 323.9 us)
where the time goes:
time: 4560 us; the launch traced here: 4550 us
  blocking collectives  2190 us (48%)
  matrix products  1240 us (27%)
  other arithmetic  622 us (14%)
  local copies, waits for them, and re-layouts  280 us (6%)
  waiting for transfers between devices  182 us (4%)
    psum x1, blocking collectives, device_step(): lax.psum((dw_q, dw_k, dw_v, dw_o, dw_pre, dw_post, dq_norm, dk_norm), 'sp')  2190 us
    another operation x10, other arithmetic  247 us
    dot_general x8, matrix products, attention_bwd(): jnp.einsum('bqkgh,bskh->bkgqs', do_blk, v_pre, preferred_element_type=jnp...  223 us
    dot_general x8, matrix products, attention_fwd(): jnp.einsum('bqkgh,bskh->bkgqs', q_grp[:, start:end], k_all[:, :end], pref...  147 us
    dot_general x8, matrix products, attention_bwd(): jnp.einsum('bkgqs,bqkgh->bskh', attn_prob.astype(jnp.bfloat16), do_blk, p...  137 us
    dot_general x8, matrix products, attention_fwd(): jnp.einsum('bkgqs,bskh->bqkgh', attn_prob, v_all[:, :end], preferred_elem...  129 us
    reduce_sum x8, other arithmetic, attention_fwd(): row_sum = jnp.sum(exp_scores, axis=-1, keepdims=True)  112 us
    all_to_all x4, waiting for transfers between devices, to_tokens(): return lax.all_to_all(arr, 'sp', 1, 2, tiled=True)  110 us
  transfers between devices with their start and end apart: 8, of which 5 were waited for; matrix products, arithmetic and copies ran while one was open for 11% of the time, Pallas kernels for 0%

commit v1 on v0

v1 whole, which is shorter than its diff:
```python
import functools
import math
import jax
import jax.numpy as jnp
from jax import lax
from jax.experimental import pallas as pl
from jax.experimental.pallas import tpu as pltpu
from jax.sharding import PartitionSpec as P

EPS = 1e-6
ROPE_BASE = 1000000.0
ROPE_SCALE = 8.0
NEG_BIG = -1e30
LOG2E = 1.4426950408889634
F32 = jnp.float32
BF16 = jnp.bfloat16
NT = (((1,), (1,)), ((), ()))
NN = (((1,), (0,)), ((), ()))
TN = (((0,), (0,)), ((), ()))
VMEM_LIMIT = 60 * 1024 * 1024


def dot(a, b, dims):
    return lax.dot_general(a, b, dims, preferred_element_type=F32)


def rms_scale(x_f32, weight):
    inv_rms = lax.rsqrt(jnp.mean(x_f32 * x_f32, axis=-1, keepdims=True) + EPS)
    return x_f32 * inv_rms * (1.0 + weight)


def pre_norm(x_f32, weight):
    return rms_scale(x_f32, weight).astype(BF16)


def post_norm(proj, weight):
    return rms_scale(proj.astype(F32), weight)


def rope_tables(positions, head):
    half_dim = head // 2
    inv_freq = ROPE_BASE ** (-jnp.arange(half_dim, dtype=F32) * 2.0 / head)
    angles = (positions.astype(F32) / ROPE_SCALE)[:, None] * inv_freq[None, :]
    return jnp.cos(angles), jnp.sin(angles)


def rope_fwd_kernel(n_q, n_k, head, x_ref, cos_ref, sin_ref, wq_ref, wk_ref, q_ref, k_ref):
    half = head // 2
    cosines = cos_ref[...]
    sines = sin_ref[...]
    for h in range(n_q + n_k):
        x = x_ref[:, h * head:(h + 1) * head].astype(F32)
        w_ref, out_ref, at = (wq_ref, q_ref, h) if h < n_q else (wk_ref, k_ref, h - n_q)
        normed = rms_scale(x, w_ref[...])
        first = normed[:, :half]
        second = normed[:, half:]
        out_ref[:, at * head:at * head + half] = (first * cosines - second * sines).astype(BF16)
        out_ref[:, at * head + half:(at + 1) * head] = (second * cosines + first * sines).astype(BF16)


def rope_fwd(qkv, cosines, sines, w_qn, w_kn, n_q, n_k, head):
    seq = qkv.shape[0]
    rows = min(512, seq)
    half = head // 2
    row = lambda width: pl.BlockSpec((rows, width), lambda i: (i, 0))
    whole = pl.BlockSpec((1, head), lambda i: (0, 0))
    return pl.pallas_call(
        functools.partial(rope_fwd_kernel, n_q, n_k, head),
        name='rope_fwd',
        grid=(seq // rows,),
        in_specs=[row((n_q + n_k) * head), row(half), row(half), whole, whole],
        out_specs=[row(n_q * head), row(n_k * head)],
        out_shape=[jax.ShapeDtypeStruct((seq, n_q * head), BF16), jax.ShapeDtypeStruct((seq, n_k * head), BF16)],
        compiler_params=pltpu.CompilerParams(dimension_semantics=('arbitrary',)),
        cost_estimate=pl.CostEstimate(flops=seq * (n_q + n_k) * head * 12, bytes_accessed=seq * (n_q + n_k) * head * 4 + seq * head * 4, transcendentals=0),
    )(qkv, cosines, sines, w_qn, w_kn)


def rope_bwd_kernel(n_q, n_k, head, dq_ref, dk_ref, x_ref, cos_ref, sin_ref, wq_ref, wk_ref, oq_ref, ok_ref, gq_ref, gk_ref):
    half = head // 2
    cosines = cos_ref[...]
    sines = sin_ref[...]

    @pl.when(pl.program_id(0) == 0)
    def _():
        gq_ref[...] = jnp.zeros_like(gq_ref)
        gk_ref[...] = jnp.zeros_like(gk_ref)

    for h in range(n_q + n_k):
        x = x_ref[:, h * head:(h + 1) * head].astype(F32)
        g_in, w_ref, out_ref, sum_ref, at = (dq_ref, wq_ref, oq_ref, gq_ref, h) if h < n_q else (dk_ref, wk_ref, ok_ref, gk_ref, h - n_q)
        d_first = g_in[:, at * head:at * head + half].astype(F32)
        d_second = g_in[:, at * head + half:(at + 1) * head].astype(F32)
        g = jnp.concatenate([d_first * cosines + d_second * sines, d_second * cosines - d_first * sines], axis=1)
        inv_rms = lax.rsqrt(jnp.mean(x * x, axis=-1, keepdims=True) + EPS)
        x_hat = x * inv_rms
        rows = x.shape[0]
        sum_ref[...] += jnp.sum((g * x_hat).reshape(rows // 8, 8, head), axis=0)
        gw = g * (1.0 + w_ref[...])
        out = inv_rms * (gw - x_hat * jnp.mean(gw * x_hat, axis=-1, keepdims=True))
        out_ref[:, at * head:(at + 1) * head] = out.astype(BF16)


def rope_bwd(dq, dk, qkv, cosines, sines, w_qn, w_kn, n_q, n_k, head):
    seq = qkv.shape[0]
    rows = min(512, seq)
    half = head // 2
    row = lambda width: pl.BlockSpec((rows, width), lambda i: (i, 0))
    whole = pl.BlockSpec((1, head), lambda i: (0, 0))
    sums = pl.BlockSpec((8, head), lambda i: (0, 0))
    return pl.pallas_call(
        functools.partial(rope_bwd_kernel, n_q, n_k, head),
        name='rope_bwd',
        grid=(seq // rows,),
        in_specs=[row(n_q * head), row(n_k * head), row((n_q + n_k) * head), row(half), row(half), whole, whole],
        out_specs=[row(n_q * head), row(n_k * head), sums, sums],
        out_shape=[jax.ShapeDtypeStruct((seq, n_q * head), BF16), jax.ShapeDtypeStruct((seq, n_k * head), BF16),
                   jax.ShapeDtypeStruct((8, head), F32), jax.ShapeDtypeStruct((8, head), F32)],
        compiler_params=pltpu.CompilerParams(dimension_semantics=('arbitrary',)),
        cost_estimate=pl.CostEstimate(flops=seq * (n_q + n_k) * head * 20, bytes_accessed=seq * (n_q + n_k) * head * 6 + seq * head * 4, transcendentals=0),
    )(dq, dk, qkv, cosines, sines, w_qn, w_kn)


BQ = 512
BK = 512


def attn_fwd_kernel(per, head, blk, q_ref, k_ref, v_ref, o_ref, lse_ref, m_sc, l_sc, acc_sc):
    i = pl.program_id(0)
    c = LOG2E * head ** -0.5
    m_sc[...] = jnp.full_like(m_sc, -jnp.inf)
    l_sc[...] = jnp.zeros_like(l_sc)
    acc_sc[...] = jnp.zeros_like(acc_sc)

    def step(j, masked):
        at = pl.multiple_of(j * blk, blk)
        k = k_ref[pl.ds(at, blk), :]
        v = v_ref[pl.ds(at, blk), :]
        for h in range(per):
            s = dot(q_ref[:, h * head:(h + 1) * head], k, NT)
            if masked:
                rows = lax.broadcasted_iota(jnp.int32, s.shape, 0)
                cols = lax.broadcasted_iota(jnp.int32, s.shape, 1)
                s = jnp.where(rows >= cols, s, NEG_BIG)
            t = s * c
            m_prev = m_sc[h]
            m_new = jnp.maximum(m_prev, jnp.max(t, axis=1, keepdims=True))
            m_sc[h] = m_new
            p = jnp.exp2(t - jnp.tile(m_new, (1, blk // 128)))
            alpha = jnp.exp2(m_prev - m_new)
            part = p[:, :128]
            for z in range(1, blk // 128):
                part = part + p[:, z * 128:(z + 1) * 128]
            l_sc[h] = l_sc[h] * alpha + part
            acc_sc[h] = acc_sc[h] * jnp.tile(alpha, (1, head // 128)) + dot(p.astype(BF16), v, NN)

    @pl.loop(0, i)
    def _(j):
        step(j, False)

    step(i, True)
    for h in range(per):
        total = jnp.sum(l_sc[h], axis=1, keepdims=True)
        o_ref[:, h * head:(h + 1) * head] = (acc_sc[h] / total).astype(BF16)
        lse = m_sc[h] + jnp.log2(jnp.broadcast_to(total, (blk, 128)))
        lse_ref[h:h + 1, :] = lse.T[0:1, :]


def attn_fwd(q, k, v, per, head):
    seq = q.shape[0]
    blk = min(BQ, seq)
    pairs = seq * (seq + blk) // 2 * per
    row = pl.BlockSpec((blk, per * head), lambda i: (i, 0))
    whole = pl.BlockSpec((seq, head), lambda i: (0, 0))
    return pl.pallas_call(
        functools.partial(attn_fwd_kernel, per, head, blk),
        name='attn_fwd',
        grid=(seq // blk,),
        in_specs=[row, whole, whole],
        out_specs=[row, pl.BlockSpec((per, blk), lambda i: (0, i))],
        out_shape=[jax.ShapeDtypeStruct((seq, per * head), BF16), jax.ShapeDtypeStruct((per, seq), F32)],
        scratch_shapes=[pltpu.VMEM((per, blk, 128), F32), pltpu.VMEM((per, blk, 128), F32), pltpu.VMEM((per, blk, head), F32)],
        compiler_params=pltpu.CompilerParams(dimension_semantics=('arbitrary',), vmem_limit_bytes=VMEM_LIMIT),
        cost_estimate=pl.CostEstimate(flops=4 * pairs * head, bytes_accessed=seq * head * 2 * (2 * per + 2), transcendentals=pairs),
    )(q, k, v)


def attn_bwd_kernel(per, head, blk, q_ref, do_ref, o_ref, lse_ref, k_ref, v_ref, dq_ref, dk_ref, dv_ref, dk_acc, dv_acc, dq_acc, q_sc, do_sc, delta_sc):
    i = pl.program_id(0)
    last = pl.num_programs(0) - 1
    scale = head ** -0.5
    c = LOG2E * scale
    for h in range(per):
        lanes = slice(h * head, (h + 1) * head)
        rows = slice(h * blk, (h + 1) * blk)
        q_sc[rows, :] = q_ref[:, lanes]
        do_sc[rows, :] = do_ref[:, lanes]
        prod = do_ref[:, lanes].astype(F32) * o_ref[:, lanes].astype(F32)
        delta = jnp.broadcast_to(jnp.sum(prod, axis=1, keepdims=True), (blk, 128))
        delta_sc[:, rows] = delta.T[0:1, :]

    def step(j, diag):
        at = pl.multiple_of(j * blk, blk)
        k = k_ref[pl.ds(at, blk), :]
        v = v_ref[pl.ds(at, blk), :]
        dvs = []
        dks = []
        dqs = []
        for h in range(per):
            rows = slice(h * blk, (h + 1) * blk)
            q = q_sc[rows, :]
            d_out = do_sc[rows, :]
            s = dot(k, q, NT)
            p = jnp.exp2(s * c - lse_ref[h:h + 1, :])
            if diag:
                kv_ids = lax.broadcasted_iota(jnp.int32, s.shape, 0)
                q_ids = lax.broadcasted_iota(jnp.int32, s.shape, 1)
                p = jnp.where(q_ids >= kv_ids, p, 0.0)
            dp = dot(v, d_out, NT)
            ds = (p * (dp - delta_sc[:, rows])).astype(BF16)
            dvs.append(dot(p.astype(BF16), d_out, NN))
            dks.append(dot(ds, q, NN))
            dqs.append(dot(ds, k, TN))
        d_v = functools.reduce(jnp.add, dvs)
        d_k = functools.reduce(jnp.add, dks)
        if diag:
            dv_acc[pl.ds(at, blk), :] = d_v
            dk_acc[pl.ds(at, blk), :] = d_k
        else:
            dv_acc[pl.ds(at, blk), :] += d_v
            dk_acc[pl.ds(at, blk), :] += d_k
        for h in range(per):
            rows = slice(h * blk, (h + 1) * blk)
            if diag:
                dq_acc[rows, :] = dqs[h]
            else:
                dq_acc[rows, :] += dqs[h]

    step(i, True)

    @pl.loop(0, i)
    def _(j):
        step(j, False)

    for h in range(per):
        dq_ref[:, h * head:(h + 1) * head] = (dq_acc[h * blk:(h + 1) * blk, :] * scale).astype(BF16)

    @pl.when(i == last)
    def _():
        @pl.loop(0, dk_acc.shape[0] // blk)
        def _(j):
            at = pl.ds(pl.multiple_of(j * blk, blk), blk)
            dk_ref[at, :] = (dk_acc[at, :] * scale).astype(BF16)
            dv_ref[at, :] = dv_acc[at, :].astype(BF16)


def attn_bwd(q, d_out, o, lse, k, v, per, head):
    seq = q.shape[0]
    blk = min(BQ, seq)
    pairs = seq * (seq + blk) // 2 * per
    row = pl.BlockSpec((blk, per * head), lambda i: (i, 0))
    whole = pl.BlockSpec((seq, head), lambda i: (0, 0), pipeline_mode=pl.Buffered(1))
    return pl.pallas_call(
        functools.partial(attn_bwd_kernel, per, head, blk),
        name='attn_bwd',
        grid=(seq // blk,),
        in_specs=[row, row, row, pl.BlockSpec((per, blk), lambda i: (0, i)), whole, whole],
        out_specs=[row, whole, whole],
        out_shape=[jax.ShapeDtypeStruct((seq, per * head), BF16), jax.ShapeDtypeStruct((seq, head), BF16), jax.ShapeDtypeStruct((seq, head), BF16)],
        scratch_shapes=[pltpu.VMEM((seq, head), F32), pltpu.VMEM((seq, head), F32), pltpu.VMEM((per * blk, head), F32),
                        pltpu.VMEM((per * blk, head), BF16), pltpu.VMEM((per * blk, head), BF16), pltpu.VMEM((1, per * blk), F32)],
        compiler_params=pltpu.CompilerParams(dimension_semantics=('arbitrary',), vmem_limit_bytes=VMEM_LIMIT),
        cost_estimate=pl.CostEstimate(flops=10 * pairs * head, bytes_accessed=seq * head * 2 * (4 * per + 4), transcendentals=pairs),
    )(q, d_out, o, lse, k, v)


def solution(mesh):
    group = mesh.shape['sp']

    def gather(arr, axis=0):
        return lax.all_gather(arr, 'sp', axis=axis, tiled=True)

    def device_step(x_in, dy_in, positions, w_q, w_k, w_v, w_o, w_pre, w_post, q_norm, k_norm):
        batch, seq_loc, width = x_in.shape
        head = q_norm.shape[0]
        n_q = w_q.shape[1] // head // group
        n_k = w_k.shape[1] // head // group
        me = lax.axis_index('sp')
        x_f32 = x_in[0].astype(F32)
        normed, pre_pull = jax.vjp(pre_norm, x_f32, w_pre)
        normed_all = gather(normed)
        cosines, sines = rope_tables(gather(positions), head)
        wq_mine = lax.dynamic_slice_in_dim(w_q, me * n_q * head, n_q * head, 1)
        wk_mine = lax.dynamic_slice_in_dim(w_k, me * n_k * head, n_k * head, 1)
        wv_mine = lax.dynamic_slice_in_dim(w_v, me * n_k * head, n_k * head, 1)
        qk = dot(normed_all, jnp.concatenate([wq_mine, wk_mine], axis=1), NN).astype(BF16)
        v_all = dot(normed_all, wv_mine, NN).astype(BF16)
        qn = q_norm[None, :]
        kn = k_norm[None, :]
        q_all, k_all = rope_fwd(qk, cosines, sines, qn, kn, n_q, n_k, head)
        o_all, lse = attn_fwd(q_all, k_all, v_all, n_q // n_k, head)
        o_flat = lax.all_to_all(o_all, 'sp', 0, 1, tiled=True)
        proj = dot(o_flat, w_o, NN).astype(BF16)
        post, post_pull = jax.vjp(post_norm, proj, w_post)
        y_out = (x_f32 + post).astype(BF16)
        dy_f32 = dy_in[0].astype(F32)
        d_proj, dw_post = post_pull(dy_f32)
        d_proj_all = gather(d_proj)
        wo_mine = lax.dynamic_slice_in_dim(w_o, me * n_q * head, n_q * head, 0)
        do_all = dot(d_proj_all, wo_mine, NT).astype(BF16)
        dw_o = gather(dot(o_all, d_proj_all, TN).astype(BF16))
        dq_all, dk_all, dv_all = attn_bwd(q_all, do_all, o_all, lse, k_all, v_all, n_q // n_k, head)
        dq_proj, dk_proj, gq, gk = rope_bwd(dq_all, dk_all, qk, cosines, sines, qn, kn, n_q, n_k, head)
        dq_flat = lax.all_to_all(dq_proj, 'sp', 0, 1, tiled=True)
        dk_flat = lax.all_to_all(dk_proj, 'sp', 0, 1, tiled=True)
        dv_flat = lax.all_to_all(dv_all, 'sp', 0, 1, tiled=True)
        dw_q = gather(dot(normed_all, dq_proj, TN).astype(BF16), 1)
        dw_k = gather(dot(normed_all, dk_proj, TN).astype(BF16), 1)
        dw_v = gather(dot(normed_all, dv_all, TN).astype(BF16), 1)
        d_normed = (dot(dq_flat, w_q, NT) + dot(dk_flat, w_k, NT) + dot(dv_flat, w_v, NT)).astype(BF16)
        dx_norm, dw_pre = pre_pull(d_normed)
        dx_out = (dy_f32 + dx_norm).astype(BF16)
        sums = lax.psum((dw_pre, dw_post, jnp.sum(gq, axis=0), jnp.sum(gk, axis=0)), 'sp')
        return (y_out[None], dx_out[None], dw_q, dw_k, dw_v, dw_o, sums[0], sums[1], sums[2], sums[3])

    token_spec = P('dp', 'sp', None)
    return jax.shard_map(device_step, mesh=mesh,
                         in_specs=(token_spec, token_spec, P(('dp', 'sp')), P(None, None), P(None, None), P(None, None), P(None, None), P(None), P(None), P(None), P(None)),
                         out_specs=(token_spec, token_spec, P('dp', None), P('dp', None), P('dp', None), P('dp', None), P('dp'), P('dp'), P('dp'), P('dp')),
                         check_vma=False)
```

time: 4560 us -> 2100 us (0.46)
  blocking collectives: 2190 us -> 35.9 us
  matrix products: 1240 us -> 405 us
  waiting for transfers between devices: 182 us -> 971 us
  other arithmetic: 622 us -> 68 us
  Pallas kernels: 0 us -> 478 us
  local copies, waits for them, and re-layouts: 280 us -> 110 us
    psum x1, blocking collectives: 2190 us -> 23.6 us  [device_step(): lax.psum((dw_pre, dw_post, jnp.sum(gq, axis=0), jnp.sum(gk, axis=0)), 'sp')]
    dot_general x60 -> x11, matrix products: 1240 us -> 405 us  [dot(): return lax.dot_general(a, b, dims, preferred_element_type=F32)]
    all_gather x0 -> x6, waiting for transfers between devices: none -> 647 us  [gather(): return lax.all_gather(arr, 'sp', axis=axis, tiled=True)]
    pallas_call x0 -> x4, Pallas kernels: none -> 478 us  [the longest x1 269 us: attn_bwd(): pl.pallas_call(functools.partial(attn_bwd_kernel, per, head, blk), name='...]
    another operation x10 -> x0, other arithmetic: 247 us -> none
    all_to_all x8 -> x4, waiting for transfers between devices: 182 us -> 324 us  [the longest x1 105 us: device_step(): dq_flat = lax.all_to_all(dq_proj, 'sp', 0, 1, tiled=True)]
    reduce_sum x8 -> x2, other arithmetic: 112 us -> 0.04 us  [the longest x1 0.02 us: device_step(): jnp.sum(gq, axis=0)]
    unnamed x8 -> x2, other arithmetic: 87.1 us -> 0.01 us
  transfers between devices with their start and end apart: 8 -> 10, of which waited for: 5 -> 7; matrix products, arithmetic and copies ran while one was open for 11% -> 13% of each run, Pallas kernels for 0% -> 0%
where the time goes in v1:
time: 2100 us
  waiting for transfers between devices  971 us (46%)
  Pallas kernels  478 us (23%)
  matrix products  405 us (19%)
  local copies, waits for them, and re-layouts  110 us (5%)
  other arithmetic  68 us (3%)
  blocking collectives  35.9 us (2%)
    all_gather x6, waiting for transfers between devices, gather(): return lax.all_gather(arr, 'sp', axis=axis, tiled=True)  647 us
    dot_general x11, matrix products, dot(): return lax.dot_general(a, b, dims, preferred_element_type=F32)  405 us
    pallas_call x1, Pallas kernels, attn_bwd(): pl.pallas_call(functools.partial(attn_bwd_kernel, per, head, blk), name='...  269 us
    pallas_call x1, Pallas kernels, attn_fwd(): pl.pallas_call(functools.partial(attn_fwd_kernel, per, head, blk), name='...  168 us
    all_to_all x1, waiting for transfers between devices, device_step(): dq_flat = lax.all_to_all(dq_proj, 'sp', 0, 1, tiled=True)  105 us
    all_to_all x1, waiting for transfers between devices, device_step(): o_flat = lax.all_to_all(o_all, 'sp', 0, 1, tiled=True)  94 us
    all_to_all x1, waiting for transfers between devices, device_step(): dk_flat = lax.all_to_all(dk_proj, 'sp', 0, 1, tiled=True)  71.4 us
    unnamed x36, local copies, waits for them, and re-layouts  66 us
  transfers between devices with their start and end apart: 10, of which 7 were waited for; matrix products, arithmetic and copies ran while one was open for 13% of the time, Pallas kernels for 0%

profile of v1, /device:TPU:0, one launch (start us, length us, event | category | flops | bytes accessed | tf_op | source)
XLA Modules:
  0.0 2096.4 jit_solution(15042186273267656279)
XLA Ops:
  7.2 0.0 all-gather.7.cloned.1.call-start
  7.2 4.8 fusion.11
  12.1 0.6 copy-done.4
  12.7 0.7 broadcast_add_fusion.1
  13.4 0.6 copy-done.1
  14.0 9.6 fusion.4
  23.6 0.0 all-gather.7.cloned.1.call-update
  23.6 12.3 all_gather.22
  35.9 2.2 constant_dynamic-slice_fusion
  38.1 5.6 constant_dynamic-slice_fusion.1
  43.7 18.2 multiply_sine_fusion
  61.9 244.0 %all-gather.7.cloned.1.call-done = bf16[8192,3840]{1,0:T(8,128)(2,1)} async-done(((bf16[1024,3840]{1,0:T(8,128)(2,1)}), bf16[8192,3840]{1,0:T(8,128)(2,1)}) %all-gather.7.cloned.1.call-update) | async-done | bytes 62914576 | tf_op jit(solution)/shard_map/all_gather | solution.py:281
  306.0 55.5 %convolution_convert_fusion.x_ref = bf16[8192,768]{1,0:T(8,128)(2,1)} fusion(bf16[8192,3840]{1,0:T(8,128)(2,1)} %all-gather.7.cloned.1.call-done, bf16[3840,256]{1,0:T(8,128)(2,1)S(1)} %constant_dynamic-slice_fusion, bf16[3840,512]{1,0:T(8,128)(2,1)} %constant_dynamic-slice_fusion.1), kind=kOutput, calls=%fused_computation.31 | convolution fusion | flops 48336470016 | bytes 81395712 | tf_op jit(solution)/shard_map/dot_general | solution.py:24
  361.5 18.7 rope_fwd.1
  380.2 28.2 %convolution_convert_fusion.2.v_ref = bf16[8192,256]{1,0:T(8,128)(2,1)} fusion(bf16[8192,3840]{1,0:T(8,128)(2,1)} %all-gather.7.cloned.1.call-done, bf16[3840,2048]{1,0:T(8,128)(2,1)} %param.16, s32[]{:T(128)S(6)} %select_n.9), kind=kOutput, calls=%fused_computation.33 | convolution fusion | flops 16108224512 | bytes 69074944 | tf_op jit(solution)/shard_map/dot_general | solution.py:24
  408.3 167.9 %attn_fwd.1 = (bf16[8192,512]{1,0:T(8,128)(2,1)}, f32[2,8192]{1,0:T(2,128)}) custom-call(bf16[8192,512]{1,0:T(8,128)(2,1)} %get-tuple-element.21.q_ref, bf16[8192,256]{1,0:T(8,128)(2,1)} %get-tuple-element.22.k_ref, bf16[8192,256]{1,0:T(8,128)(2,1)} %convolution_convert_fusion.2.v_ref), custom_call_target="tpu_custom_call" | custom-call | flops 73014444032 | bytes 25165824 | tf_op jit(solution)/shard_map/attn_fwd/pallas_call | solution.py:175
  576.2 11.4 copy.25
  587.6 3.7 all-to-all-start
  591.3 0.0 all-gather.9.cloned.1.call-start
  591.4 94.0 %all-to-all-done = bf16[8,1024,512]{1,2,0:T(8,128)(2,1)} async-done(((bf16[8,1024,512]{1,2,0:T(8,128)(2,1)}), bf16[8,1024,512]{1,2,0:T(8,128)(2,1)}, u32[]{:S(2)}, u32[]{:S(2)}) %all-to-all-start) | async-done | bytes 8388640 | tf_op jit(solution)/shard_map/all_to_all | solution.py:302
  685.3 40.4 %fusion.9 = (f32[1024]{0:T(1024)S(1)}, bf16[1024,3840]{1,0:T(8,128)(2,1)S(1)}) fusion(bf16[1024,4096]{0,1:T(8,128)(2,1)} %bitcast.6, bf16[4096,3840]{1,0:T(8,128)(2,1)} %param.17), kind=kOutput, calls=%fused_computation.25 | convolution fusion | flops 32227983360 | bytes 47714304 | tf_op jit(solution)/shard_map/dot_general | solution.py:24
  725.7 0.0 slice-start
  725.8 0.0 slice-start.1
  725.8 11.5 fusion.8
  737.4 9.8 fusion.6
  747.2 0.0 all-gather.9.cloned.1.call-update
  747.2 0.0 all-gather.13.cloned.1.call-start
  747.3 278.6 %all-gather.9.cloned.1.call-done = bf16[8192,3840]{1,0:T(8,128)(2,1)} async-done(((bf16[1024,3840]{1,0:T(8,128)(2,1)}), bf16[8192,3840]{1,0:T(8,128)(2,1)}) %all-gather.9.cloned.1.call-update) | async-done | bytes 62914576 | tf_op jit(solution)/shard_map/all_gather | solution.py:281
  1025.9 41.6 %convolution_convert_fusion.1.do_ref = bf16[8192,512]{1,0:T(8,128)(2,1)} fusion(bf16[8192,3840]{1,0:T(8,128)(2,1)} %all-gather.9.cloned.1.call-done, bf16[4096,3840]{1,0:T(8,128)(2,1)} %param.17, s32[]{:T(128)S(6)} %select_n.8), kind=kOutput, calls=%fused_computation.32 | convolution fusion | flops 32216449024 | bytes 75235328 | tf_op jit(solution)/shard_map/dot_general | solution.py:24
  1067.5 268.5 %attn_bwd.1 = (bf16[8192,512]{1,0:T(8,128)(2,1)}, bf16[8192,256]{1,0:T(8,128)(2,1)}, bf16[8192,256]{1,0:T(8,128)(2,1)}) custom-call(bf16[8192,512]{1,0:T(8,128)(2,1)} %get-tuple-element.21.q_ref, bf16[8192,512]{1,0:T(8,128)(2,1)} %convolution_convert_fusion.1.do_ref, bf16[8192,512]{1,0:T(8,128)(2,1)} %get-tuple-element.23.o_ref, ...), custom_call_target="tpu_custom_call" | custom-call | flops 182536110080 | bytes 50331648 | tf_op jit(solution)/shard_map/attn_bwd/pallas_call | solution.py:263
  1336.0 22.8 %rope_bwd.1 = (bf16[8192,512]{1,0:T(8,128)(2,1)}, bf16[8192,256]{1,0:T(8,128)(2,1)}, f32[8,256]{1,0:T(8,128)}, f32[8,256]{1,0:T(8,128)}) custom-call(bf16[8192,512]{1,0:T(8,128)(2,1)} %get-tuple-element.25.dq_ref, bf16[8192,256]{1,0:T(8,128)(2,1)} %get-tuple-element.26.dk_ref, bf16[8192,768]{1,0:T(8,128)(2,1)} %convolution_convert_fusion.x_ref, ...), custom_call_target="tpu_custom_call" | custom-call | flops 125829120 | bytes 46137344 | tf_op jit(solution)/shard_map/rope_bwd/pallas_call | solution.py:111
  1358.9 28.7 %convolution_convert_fusion.7 = bf16[3840,256]{1,0:T(8,128)(2,1)} fusion(bf16[8192,3840]{1,0:T(8,128)(2,1)} %all-gather.7.cloned.1.call-done, bf16[8192,256]{1,0:T(8,128)(2,1)} %get-tuple-element.28), kind=kOutput, calls=%fused_computation.45 | convolution fusion | flops 16107110400 | bytes 69074944 | tf_op jit(solution)/shard_map/dot_general | solution.py:24
  1387.5 0.0 all-gather.13.cloned.1.call-update
  1387.6 0.0 all-gather.15.cloned.1.call-start
  1387.6 29.4 %convolution_convert_fusion.6 = bf16[3840,256]{1,0:T(8,128)(2,1)} fusion(bf16[8192,3840]{1,0:T(8,128)(2,1)} %all-gather.7.cloned.1.call-done, bf16[8192,256]{1,0:T(8,128)(2,1)} %get-tuple-element.29), kind=kOutput, calls=%fused_computation.44 | convolution fusion | flops 16107110400 | bytes 69074944 | tf_op jit(solution)/shard_map/dot_general | solution.py:24
  1417.1 0.0 all-gather.15.cloned.1.call-update
  1417.1 0.0 all-gather.17.cloned.1.call-start
  1417.1 43.7 %convolution_convert_fusion.4 = bf16[512,3840]{1,0:T(8,128)(2,1)} fusion(bf16[8192,512]{1,0:T(8,128)(2,1)} %get-tuple-element.23.o_ref, bf16[8192,3840]{1,0:T(8,128)(2,1)} %all-gather.9.cloned.1.call-done), kind=kOutput, calls=%fused_computation.39 | convolution fusion | flops 32214220800 | bytes 75235328 | tf_op jit(solution)/shard_map/dot_general | solution.py:24
  1460.9 0.0 all-gather.17.cloned.1.call-update
  1460.9 0.0 all-gather.11.cloned.1.call-start
  1460.9 41.8 %convolution_convert_fusion.5 = bf16[3840,512]{1,0:T(8,128)(2,1)} fusion(bf16[8192,3840]{1,0:T(8,128)(2,1)} %all-gather.7.cloned.1.call-done, bf16[8192,512]{1,0:T(8,128)(2,1)} %get-tuple-element.27), kind=kOutput, calls=%fused_computation.40 | convolution fusion | flops 32214220800 | bytes 75235328 | tf_op jit(solution)/shard_map/dot_general | solution.py:24
  1502.7 0.0 all-gather.11.cloned.1.call-update
  1502.7 6.5 copy.27
  1509.2 3.3 all-to-all-start.2
  1512.6 11.4 copy.26
  1524.0 71.4 %all-to-all-done.2 = bf16[8,1024,256]{1,2,0:T(8,128)(2,1)} async-done(((bf16[8,1024,256]{1,2,0:T(8,128)(2,1)}), bf16[8,1024,256]{1,2,0:T(8,128)(2,1)}, u32[]{:S(2)}, u32[]{:S(2)}) %all-to-all-start.2) | async-done | bytes 4194336 | tf_op jit(solution)/shard_map/all_to_all | solution.py:315
  1595.4 3.7 all-to-all-start.1
  1599.2 6.4 copy.28
  1605.6 25.0 %fusion.27 = f32[1024,3840]{1,0:T(8,128)} fusion(bf16[1024,2048]{0,1:T(8,128)(2,1)} %bitcast.15, bf16[3840,2048]{1,0:T(8,128)(2,1)} %param.15), kind=kOutput, calls=%fused_computation.64 | convolution fusion | flops 16106127360 | bytes 35651584 | tf_op jit(solution)/shard_map/dot_general | solution.py:24
  1630.6 104.6 %all-to-all-done.1 = bf16[8,1024,512]{1,2,0:T(8,128)(2,1)} async-done(((bf16[8,1024,512]{1,2,0:T(8,128)(2,1)}), bf16[8,1024,512]{1,2,0:T(8,128)(2,1)}, u32[]{:S(2)}, u32[]{:S(2)}) %all-to-all-start.1) | async-done | bytes 8388640 | tf_op jit(solution)/shard_map/all_to_all | solution.py:314
  1735.3 3.7 all-to-all-start.3
  1738.9 0.0 copy-start.2
  1739.0 40.7 %fusion.26 = f32[1024,3840]{1,0:T(8,128)} fusion(bf16[1024,4096]{0,1:T(8,128)(2,1)} %bitcast.12, bf16[3840,4096]{1,0:T(8,128)(2,1)} %param.14), kind=kOutput, calls=%fused_computation.63 | convolution fusion | flops 32212254720 | bytes 55574528 | tf_op jit(solution)/shard_map/dot_general | solution.py:24
  1779.6 53.7 %all-to-all-done.3 = bf16[8,1024,256]{1,2,0:T(8,128)(2,1)} async-done(((bf16[8,1024,256]{1,2,0:T(8,128)(2,1)}), bf16[8,1024,256]{1,2,0:T(8,128)(2,1)}, u32[]{:S(2)}, u32[]{:S(2)}) %all-to-all-start.3) | async-done | bytes 4194336 | tf_op jit(solution)/shard_map/all_to_all | solution.py:316
  1833.3 30.1 %fusion.5 = (f32[3840]{0:T(1024)S(1)}, f32[1024]{0:T(1024)S(1)}, bf16[1024,3840]{1,0:T(8,128)(2,1)}) fusion(bf16[1,1024,3840]{2,1,0:T(8,128)(2,1)} %param.11, f32[1024]{0:T(1024)S(1)} %copy-done.7, f32[3840]{0:T(1024)S(1)} %copy-done.2, bf16[1024,2048]{0,1:T(8,128)(2,1)} %bitcast.18, bf16[3840,2048]{1,0:T(8,128)(2,1)} %param.16, f32[1024,3840]{1,0:T(8,128)} %fusion.26, ...), kind=kOutput, calls=%fused_computation.21 | convolution fusion | flops 16149376000 | bytes 67147776 | tf_op jit(solution)/shard_map/dot_general | solution.py:24
  1863.4 23.6 %all-reduce = (f32[3840]{0:T(1024)}, f32[3840]{0:T(1024)}, f32[256]{0:T(256)}, f32[256]{0:T(256)}) all-reduce(f32[3840]{0:T(1024)S(1)} %get-tuple-element.34, f32[3840]{0:T(1024)S(1)} %copy-done.3, f32[256]{0:T(256)S(1)} %reduce_sum.79, f32[256]{0:T(256)S(1)} %reduce_sum.83), channel_id=1, replica_groups=mesh['dp'=1,'sp'=8] {'sp'}, use_global_device_ids=true, to_apply=%region_5.0 | all-reduce | flops 8192 | bytes 65536 | tf_op jit(solution)/shard_map/psum | solution.py:323
  1887.0 13.2 fusion.15
  1900.2 0.0 all-gather.17.cloned.1.call-done
  1900.3 124.1 %all-gather.11.cloned.1.call-done = bf16[3840,4096]{1,0:T(8,128)(2,1)} async-done(((bf16[3840,512]{1,0:T(8,128)(2,1)}), bf16[3840,4096]{1,0:T(8,128)(2,1)}) %all-gather.11.cloned.1.call-update) | async-done | bytes 31457296 | tf_op jit(solution)/shard_map/all_gather | solution.py:281
  2024.3 21.3 %copy.33 = bf16[3840,4096]{1,0:T(8,128)(2,1)} copy(bf16[3840,4096]{1,0:T(8,128)(2,1)} %all-gather.11.cloned.1.call-done) | data formatting | bytes 62914560
  2045.6 14.4 copy.34
  2060.0 1.5 copy-done
  2061.5 5.8 copy.35
  2067.3 21.8 %copy.36 = bf16[4096,3840]{1,0:T(8,128)(2,1)} copy(bf16[4096,3840]{1,0:T(8,128)(2,1)} %all-gather.17.cloned.1.call-done) | data formatting | bytes 62914560
  (39 shorter events, 0.1 us)
Async XLA Ops:
  7.2 16.4 copy-start.11
  7.2 298.8 %all-gather.7.cloned.1.call-start = ((), (), s32[]{:S(2)}) async-start(), calls=%async_computation.4 | async-start | bytes 70778880 | tf_op jit(solution)/shard_map/all_gather | solution.py:281
  12.1 0.6 copy-start.4
  12.7 0.7 copy-start.6
  13.4 0.6 copy-start.1
  576.2 15.1 copy-start.8
  587.6 97.7 %all-to-all-start = ((bf16[8,1024,512]{1,2,0:T(8,128)(2,1)}), bf16[8,1024,512]{1,2,0:T(8,128)(2,1)}, u32[]{:S(2)}, u32[]{:S(2)}) async-start(bf16[8,1024,512]{1,2,0:T(8,128)(2,1)} %copy.25), calls=%async_computation | async-start | bytes 16777216 | tf_op jit(solution)/shard_map/all_to_all | solution.py:302
  591.3 434.6 %all-gather.9.cloned.1.call-start = ((), (), s32[]{:S(2)}) async-start(), calls=%async_computation.5 | async-start | bytes 70778880 | tf_op jit(solution)/shard_map/all_gather | solution.py:281
  685.3 52.0 %slice-start.2 = ((s8[7864320]{0:T(1024)(128)(4,1)}), s8[4194304]{0:T(1024)(128)(4,1)S(1)}, s32[]{:S(2)}) async-start(s8[7864320]{0:T(1024)(128)(4,1)} %bitcast.58), calls=%async_computation.12 | async-start | bytes 8388608
  685.3 52.0 %slice-start.3 = ((s8[7864320]{0:T(1024)(128)(4,1)}), s8[3670016]{0:T(1024)(128)(4,1)S(1)}, s32[]{:S(2)}) async-start(s8[7864320]{0:T(1024)(128)(4,1)} %bitcast.58), calls=%async_computation.13 | async-start | bytes 7340032
  725.7 11.6 slice-start
  725.8 11.6 slice-start.1
  747.2 1153.0 %all-gather.13.cloned.1.call-start = ((), (), s32[]{:S(2)}) async-start(), calls=%async_computation.7 | async-start | bytes 17694720 | tf_op jit(solution)/shard_map/all_gather | solution.py:281
  1387.6 512.7 %all-gather.15.cloned.1.call-start = ((), (), s32[]{:S(2)}) async-start(), calls=%async_computation.8 | async-start | bytes 17694720 | tf_op jit(solution)/shard_map/all_gather | solution.py:281
  1417.1 483.2 %all-gather.17.cloned.1.call-start = ((), (), s32[]{:S(2)}) async-start(), calls=%async_computation.9 | async-start | bytes 35389440 | tf_op jit(solution)/shard_map/all_gather | solution.py:281
  1460.9 563.4 %all-gather.11.cloned.1.call-start = ((), (), s32[]{:S(2)}) async-start(), calls=%async_computation.6 | async-start | bytes 35389440 | tf_op jit(solution)/shard_map/all_gather | solution.py:281
  1509.2 86.2 %all-to-all-start.2 = ((bf16[8,1024,256]{1,2,0:T(8,128)(2,1)}), bf16[8,1024,256]{1,2,0:T(8,128)(2,1)}, u32[]{:S(2)}, u32[]{:S(2)}) async-start(bf16[8,1024,256]{1,2,0:T(8,128)(2,1)} %copy.27), calls=%async_computation.2 | async-start | bytes 8388608 | tf_op jit(solution)/shard_map/all_to_all | solution.py:315
  1512.6 86.6 %copy-start.10 = (f32[8,256]{1,0:T(8,128)S(1)}, f32[8,256]{1,0:T(8,128)}, u32[]{:S(2)}) copy-start(f32[8,256]{1,0:T(8,128)} %get-tuple-element.30) | copy-start | bytes 24580
  1512.6 86.6 %copy-start.9 = (f32[8,256]{1,0:T(8,128)S(1)}, f32[8,256]{1,0:T(8,128)}, u32[]{:S(2)}) copy-start(f32[8,256]{1,0:T(8,128)} %get-tuple-element.31) | copy-start | bytes 24580
  1595.4 139.8 %all-to-all-start.1 = ((bf16[8,1024,512]{1,2,0:T(8,128)(2,1)}), bf16[8,1024,512]{1,2,0:T(8,128)(2,1)}, u32[]{:S(2)}, u32[]{:S(2)}) async-start(bf16[8,1024,512]{1,2,0:T(8,128)(2,1)} %copy.26), calls=%async_computation.1 | async-start | bytes 16777216 | tf_op jit(solution)/shard_map/all_to_all | solution.py:314
  1735.3 98.1 %all-to-all-start.3 = ((bf16[8,1024,256]{1,2,0:T(8,128)(2,1)}), bf16[8,1024,256]{1,2,0:T(8,128)(2,1)}, u32[]{:S(2)}, u32[]{:S(2)}) async-start(bf16[8,1024,256]{1,2,0:T(8,128)(2,1)} %copy.28), calls=%async_computation.3 | async-start | bytes 8388608 | tf_op jit(solution)/shard_map/all_to_all | solution.py:316
  1738.9 94.4 %copy-start.2 = (f32[3840]{0:T(1024)S(1)}, f32[3840]{0:T(1024)}, u32[]{:S(2)}) copy-start(f32[3840]{0:T(1024)} %copy-done.1) | copy-start | bytes 46084
  1738.9 94.4 %copy-start.7 = (f32[1024]{0:T(1024)S(1)}, f32[1024]{0:T(1024)}, u32[]{:S(2)}) copy-start(f32[1024]{0:T(1024)} %copy-done.6) | copy-start | bytes 12292
  1833.3 30.1 %copy-start.3 = (f32[3840]{0:T(1024)S(1)}, f32[3840]{0:T(1024)}, u32[]{:S(2)}) copy-start(f32[3840]{0:T(1024)} %get-tuple-element.32) | copy-start | bytes 46084
  1833.3 53.7 %copy-start.5 = (f32[1024]{0:T(1024)S(1)}, f32[1024]{0:T(1024)}, u32[]{:S(2)}) copy-start(f32[1024]{0:T(1024)} %copy-done.4) | copy-start | bytes 12292
  2045.6 15.9 copy-start
Sparse Core Ops, SparseCore 0:
  23.7 282.1 all-gather.6
  747.3 278.5 all-gather.8
  1387.7 82.8 all-gather.12
  1472.2 116.5 all-gather.14
  1590.4 278.6 all-gather.16
  1871.4 152.8 all-gather.10

commit v2 on v1

v2 whole, which is shorter than its diff:
```python
import functools
import jax
import jax.numpy as jnp
from jax import lax
from jax.experimental import pallas as pl
from jax.experimental.pallas import tpu as pltpu
from jax.sharding import PartitionSpec as P

EPS = 1e-6
ROPE_BASE = 1000000.0
ROPE_SCALE = 8.0
NEG_BIG = -1e30
LOG2E = 1.4426950408889634
F32 = jnp.float32
BF16 = jnp.bfloat16
NT = (((1,), (1,)), ((), ()))
NN = (((1,), (0,)), ((), ()))
TN = (((0,), (0,)), ((), ()))
VMEM_LIMIT = 60 * 1024 * 1024


def dot(a, b, dims):
    return lax.dot_general(a, b, dims, preferred_element_type=F32)


def rms_scale(x_f32, weight):
    inv_rms = lax.rsqrt(jnp.mean(x_f32 * x_f32, axis=-1, keepdims=True) + EPS)
    return x_f32 * inv_rms * (1.0 + weight)


def pre_norm(x_f32, weight):
    return rms_scale(x_f32, weight).astype(BF16)


def post_norm(proj, weight):
    return rms_scale(proj.astype(F32), weight)


def rope_tables(positions, head):
    half_dim = head // 2
    inv_freq = ROPE_BASE ** (-jnp.arange(half_dim, dtype=F32) * 2.0 / head)
    angles = (positions.astype(F32) / ROPE_SCALE)[:, None] * inv_freq[None, :]
    return jnp.cos(angles), jnp.sin(angles)


def rope_fwd_kernel(n_q, n_k, head, x_ref, cos_ref, sin_ref, wq_ref, wk_ref, *refs):
    q_ref, k_ref, v_ref = refs[-3:]
    half = head // 2
    cosines = cos_ref[...]
    sines = sin_ref[...]
    for h in range(n_q + n_k):
        x = x_ref[:, h * head:(h + 1) * head].astype(F32)
        w_ref, out_ref, at = (wq_ref, q_ref, h) if h < n_q else (wk_ref, k_ref, h - n_q)
        normed = rms_scale(x, w_ref[...])
        first = normed[:, :half]
        second = normed[:, half:]
        out_ref[:, at * head:at * head + half] = (first * cosines - second * sines).astype(BF16)
        out_ref[:, at * head + half:(at + 1) * head] = (second * cosines + first * sines).astype(BF16)
    v_ref[...] = x_ref[:, (n_q + n_k) * head:]


def rope_fwd(z, qkv, cosines, sines, w_qn, w_kn, n_q, n_k, head, kv_so_far):
    seq = cosines.shape[0]
    blk = BLK
    half = head // 2
    row = lambda width: pl.BlockSpec((blk, width), lambda i: (i, 0))
    placed = lambda width: pl.BlockSpec((blk, width), lambda i: (2 * i + z, 0))
    whole = pl.BlockSpec((1, head), lambda i: (0, 0))
    kv_shape = jax.ShapeDtypeStruct((seq, n_k * head), BF16)
    return pl.pallas_call(
        functools.partial(rope_fwd_kernel, n_q, n_k, head),
        name='rope_fwd',
        grid=(qkv.shape[0] // blk,),
        in_specs=[row((n_q + 2 * n_k) * head), placed(half), placed(half), whole, whole] + [pl.BlockSpec(memory_space=pl.ANY)] * len(kv_so_far),
        out_specs=[row(n_q * head), placed(n_k * head), placed(n_k * head)],
        out_shape=[jax.ShapeDtypeStruct((qkv.shape[0], n_q * head), BF16), kv_shape, kv_shape],
        input_output_aliases={5: 1, 6: 2} if kv_so_far else {},
        compiler_params=pltpu.CompilerParams(dimension_semantics=('arbitrary',)),
        cost_estimate=pl.CostEstimate(flops=qkv.size * 40, bytes_accessed=qkv.size * 4 + seq * head * 2, transcendentals=0),
    )(qkv, cosines, sines, w_qn, w_kn, *kv_so_far)


def rope_bwd_kernel(n, head, d_ref, x_ref, cos_ref, sin_ref, w_ref, *refs):
    out_ref, sum_ref = refs[-2:]
    half = head // 2
    cosines = cos_ref[...]
    sines = sin_ref[...]

    @pl.when(pl.program_id(0) == 0)
    def _():
        sum_ref[...] = jnp.zeros_like(sum_ref)

    for h in range(n):
        x = x_ref[:, h * head:(h + 1) * head].astype(F32)
        d_first = d_ref[:, h * head:h * head + half].astype(F32)
        d_second = d_ref[:, h * head + half:(h + 1) * head].astype(F32)
        g = jnp.concatenate([d_first * cosines + d_second * sines, d_second * cosines - d_first * sines], axis=1)
        inv_rms = lax.rsqrt(jnp.mean(x * x, axis=-1, keepdims=True) + EPS)
        x_hat = x * inv_rms
        sum_ref[...] += jnp.sum((g * x_hat).reshape(x.shape[0] // 8, 8, head), axis=0)
        gw = g * (1.0 + w_ref[...])
        out = inv_rms * (gw - x_hat * jnp.mean(gw * x_hat, axis=-1, keepdims=True))
        out_ref[:, h * head:(h + 1) * head] = out.astype(BF16)
    if len(refs) == 3:
        out_ref[:, n * head:] = refs[0][...]


def rope_bwd(z, grad, beside, qkv, lane_block, cosines, sines, w_n, n, head):
    blk = BLK
    half = head // 2
    row = lambda width: pl.BlockSpec((blk, width), lambda i: (i, 0))
    placed = lambda width: pl.BlockSpec((blk, width), lambda i: (2 * i + z, 0))
    rows = qkv.shape[0]
    lanes = n * head + sum(b.shape[1] for b in beside)
    return pl.pallas_call(
        functools.partial(rope_bwd_kernel, n, head),
        name='rope_bwd',
        grid=(rows // blk,),
        in_specs=[placed(n * head) if beside else row(n * head), pl.BlockSpec((blk, n * head), lambda i: (i, lane_block)),
                  placed(half), placed(half), pl.BlockSpec((1, head), lambda i: (0, 0))] + [placed(b.shape[1]) for b in beside],
        out_specs=[row(lanes), pl.BlockSpec((8, head), lambda i: (0, 0))],
        out_shape=[jax.ShapeDtypeStruct((rows, lanes), BF16), jax.ShapeDtypeStruct((8, head), F32)],
        compiler_params=pltpu.CompilerParams(dimension_semantics=('arbitrary',)),
        cost_estimate=pl.CostEstimate(flops=rows * n * head * 60, bytes_accessed=rows * n * head * 6 + rows * head * 4, transcendentals=0),
    )(grad, qkv, cosines, sines, w_n, *beside)


def copy_kernel(x_ref, o_ref):
    o_ref[...] = x_ref[...]


def place(x):
    rows = 256
    spec = pl.BlockSpec((rows, x.shape[1]), lambda i: (i, 0))
    return pl.pallas_call(
        copy_kernel,
        name='place',
        grid=(x.shape[0] // rows,),
        in_specs=[spec],
        out_specs=spec,
        out_shape=jax.ShapeDtypeStruct(x.shape, x.dtype),
        compiler_params=pltpu.CompilerParams(dimension_semantics=('arbitrary',)),
        cost_estimate=pl.CostEstimate(flops=x.size * 16, bytes_accessed=4 * x.size, transcendentals=0),
    )(x)


BLK = 512


def attn_fwd_kernel(z, per, head, blk, q_ref, k_ref, v_ref, o_ref, lse_ref, m_sc, l_sc, acc_sc, s_even, s_odd):
    i = pl.program_id(0)
    c = LOG2E * head ** -0.5
    m_sc[...] = jnp.full_like(m_sc, -jnp.inf)
    l_sc[...] = jnp.zeros_like(l_sc)
    acc_sc[...] = jnp.zeros_like(acc_sc)

    def scores(j, s_ref):
        k = k_ref[pl.ds(pl.multiple_of(j * blk, blk), blk), :]
        for h in range(per):
            s_ref[h] = dot(q_ref[:, h * head:(h + 1) * head], k, NT)

    def update(j, s_ref, masked):
        v = v_ref[pl.ds(pl.multiple_of(j * blk, blk), blk), :]
        for h in range(per):
            s = s_ref[h]
            if masked:
                rows = lax.broadcasted_iota(jnp.int32, s.shape, 0)
                cols = lax.broadcasted_iota(jnp.int32, s.shape, 1)
                s = jnp.where(rows >= cols, s, NEG_BIG)
            t = s * c
            m_prev = m_sc[h]
            m_new = jnp.maximum(m_prev, jnp.max(t, axis=1, keepdims=True))
            m_sc[h] = m_new
            p = jnp.exp2(t - jnp.tile(m_new, (1, blk // 128)))
            alpha = jnp.exp2(m_prev - m_new)
            part = p[:, :128]
            for y in range(1, blk // 128):
                part = part + p[:, y * 128:(y + 1) * 128]
            l_sc[h] = l_sc[h] * alpha + part
            acc_sc[h] = acc_sc[h] * jnp.tile(alpha, (1, head // 128)) + dot(p.astype(BF16), v, NN)

    scores(0, s_even)

    @pl.loop(0, i)
    def _(j):
        scores(2 * j + 1, s_odd)
        update(2 * j, s_even, False)
        scores(2 * j + 2, s_even)
        update(2 * j + 1, s_odd, False)

    if z == 0:
        update(2 * i, s_even, True)
    else:
        scores(2 * i + 1, s_odd)
        update(2 * i, s_even, False)
        update(2 * i + 1, s_odd, True)
    for h in range(per):
        total = jnp.sum(l_sc[h], axis=1, keepdims=True)
        o_ref[:, h * head:(h + 1) * head] = (acc_sc[h] / total).astype(BF16)
        lse = m_sc[h] + jnp.log2(jnp.broadcast_to(total, (blk, 128)))
        lse_ref[h:h + 1, :] = lse.T[0:1, :]


def attn_fwd(z, q, k, v, per, head):
    rows = q.shape[0]
    seq = k.shape[0]
    blk = BLK
    pairs = rows * (seq + blk) // 2 * per
    row = pl.BlockSpec((blk, per * head), lambda i: (i, 0))
    whole = pl.BlockSpec((seq, head), lambda i: (0, 0), pipeline_mode=pl.Buffered(1))
    return pl.pallas_call(
        functools.partial(attn_fwd_kernel, z, per, head, blk),
        name='attn_fwd',
        grid=(rows // blk,),
        in_specs=[row, whole, whole],
        out_specs=[row, pl.BlockSpec((per, blk), lambda i: (0, i))],
        out_shape=[jax.ShapeDtypeStruct((rows, per * head), BF16), jax.ShapeDtypeStruct((per, rows), F32)],
        scratch_shapes=[pltpu.VMEM((per, blk, 128), F32), pltpu.VMEM((per, blk, 128), F32), pltpu.VMEM((per, blk, head), F32),
                        pltpu.VMEM((per, blk, blk), F32), pltpu.VMEM((per, blk, blk), F32)],
        compiler_params=pltpu.CompilerParams(dimension_semantics=('arbitrary',), vmem_limit_bytes=VMEM_LIMIT),
        cost_estimate=pl.CostEstimate(flops=4 * pairs * head, bytes_accessed=rows * head * 4 * per + seq * head * 4, transcendentals=pairs),
    )(q, k, v)


def attn_bwd_kernel(z, per, head, blk, q_ref, do_ref, o_ref, lse_ref, k_ref, v_ref, *refs):
    if z == 0:
        dq_ref, dk_ref, dv_ref, dk_acc, dv_acc, dq_acc, q_sc, do_sc, delta_sc, sems = refs
    else:
        dk_in, dv_in, dq_ref, dk_ref, dv_ref, dk_acc, dv_acc, dq_acc, q_sc, do_sc, delta_sc, sems = refs
    i = pl.program_id(0)
    last = pl.num_programs(0) - 1
    scale = head ** -0.5
    c = LOG2E * scale

    @pl.when(i == 0)
    def _():
        if z == 0:
            dk_acc[...] = jnp.zeros_like(dk_acc)
            dv_acc[...] = jnp.zeros_like(dv_acc)
        else:
            loads = [pltpu.make_async_copy(dk_in, dk_acc, sems.at[0]), pltpu.make_async_copy(dv_in, dv_acc, sems.at[1])]
            for load in loads:
                load.start()
            for load in loads:
                load.wait()

    for h in range(per):
        lanes = slice(h * head, (h + 1) * head)
        rows = slice(h * blk, (h + 1) * blk)
        q_sc[rows, :] = q_ref[:, lanes]
        do_sc[rows, :] = do_ref[:, lanes]
        prod = do_ref[:, lanes].astype(F32) * o_ref[:, lanes].astype(F32)
        delta = jnp.broadcast_to(jnp.sum(prod, axis=1, keepdims=True), (blk, 128))
        delta_sc[:, rows] = delta.T[0:1, :]

    def step(j, diag):
        at = pl.ds(pl.multiple_of(j * blk, blk), blk)
        k = k_ref[at, :]
        v = v_ref[at, :]
        dvs = []
        dks = []
        dqs = []
        for h in range(per):
            rows = slice(h * blk, (h + 1) * blk)
            q = q_sc[rows, :]
            d_out = do_sc[rows, :]
            s = dot(k, q, NT)
            p = jnp.exp2(s * c - lse_ref[h:h + 1, :])
            if diag:
                kv_ids = lax.broadcasted_iota(jnp.int32, s.shape, 0)
                q_ids = lax.broadcasted_iota(jnp.int32, s.shape, 1)
                p = jnp.where(q_ids >= kv_ids, p, 0.0)
            dp = dot(v, d_out, NT)
            ds = (p * (dp - delta_sc[:, rows])).astype(BF16)
            dvs.append(dot(p.astype(BF16), d_out, NN))
            dks.append(dot(ds, q, NN))
            dqs.append(dot(ds, k, TN))
        dv_acc[at, :] += functools.reduce(jnp.add, dvs)
        dk_acc[at, :] += functools.reduce(jnp.add, dks)
        for h in range(per):
            rows = slice(h * blk, (h + 1) * blk)
            if diag:
                dq_acc[rows, :] = dqs[h]
            else:
                dq_acc[rows, :] += dqs[h]

    step(2 * i + z, True)

    @pl.loop(0, 2 * i + z)
    def _(j):
        step(j, False)

    for h in range(per):
        dq_ref[:, h * head:(h + 1) * head] = (dq_acc[h * blk:(h + 1) * blk, :] * scale).astype(BF16)

    @pl.when(i == last)
    def _():
        if z == 0:
            stores = [pltpu.make_async_copy(dk_acc, dk_ref, sems.at[0]), pltpu.make_async_copy(dv_acc, dv_ref, sems.at[1])]
            for store in stores:
                store.start()
            for store in stores:
                store.wait()
        else:
            @pl.loop(0, dk_acc.shape[0] // blk)
            def _(j):
                at = pl.ds(pl.multiple_of(j * blk, blk), blk)
                dk_ref[at, :] = (dk_acc[at, :] * scale).astype(BF16)
                dv_ref[at, :] = dv_acc[at, :].astype(BF16)


def attn_bwd(z, q, d_out, o, lse, k, v, per, head, partial):
    rows = q.shape[0]
    seq = k.shape[0]
    blk = BLK
    pairs = rows * (seq + blk) // 2 * per
    row = pl.BlockSpec((blk, per * head), lambda i: (i, 0))
    once = lambda n: pl.BlockSpec((n, head), lambda i: (0, 0), pipeline_mode=pl.Buffered(1))
    anywhere = pl.BlockSpec(memory_space=pl.ANY)
    dq_shape = jax.ShapeDtypeStruct((rows, per * head), BF16)
    if z == 0:
        out_specs = [row, anywhere, anywhere]
        out_shape = [dq_shape, jax.ShapeDtypeStruct((seq, head), F32), jax.ShapeDtypeStruct((seq, head), F32)]
    else:
        out_specs = [row, once(seq), once(seq)]
        out_shape = [dq_shape, jax.ShapeDtypeStruct((seq, head), BF16), jax.ShapeDtypeStruct((seq, head), BF16)]
    return pl.pallas_call(
        functools.partial(attn_bwd_kernel, z, per, head, blk),
        name='attn_bwd',
        grid=(rows // blk,),
        in_specs=[row, row, row, pl.BlockSpec((per, blk), lambda i: (0, i)), once(seq), once(seq)] + [anywhere] * len(partial),
        out_specs=out_specs,
        out_shape=out_shape,
        scratch_shapes=[pltpu.VMEM((seq, head), F32), pltpu.VMEM((seq, head), F32), pltpu.VMEM((per * blk, head), F32),
                        pltpu.VMEM((per * blk, head), BF16), pltpu.VMEM((per * blk, head), BF16), pltpu.VMEM((1, per * blk), F32),
                        pltpu.SemaphoreType.DMA((2,))],
        compiler_params=pltpu.CompilerParams(dimension_semantics=('arbitrary',), vmem_limit_bytes=VMEM_LIMIT),
        cost_estimate=pl.CostEstimate(flops=10 * pairs * head, bytes_accessed=rows * head * 8 * per + seq * head * 16, transcendentals=pairs),
    )(q, d_out, o, lse, k, v, *partial)


def solution(mesh):
    group = mesh.shape['sp']

    def gather(arr, axis=0):
        return lax.all_gather(arr, 'sp', axis=axis, tiled=True)

    def exchange(arr):
        return lax.all_to_all(arr.reshape(group, -1, arr.shape[1]), 'sp', 0, 0, tiled=True)

    def device_step(x_in, dy_in, positions, w_q, w_k, w_v, w_o, w_pre, w_post, q_norm, k_norm):
        _, _, width = x_in.shape
        head = q_norm.shape[0]
        n_q = w_q.shape[1] // head // group
        n_k = w_k.shape[1] // head // group
        per = n_q // n_k
        me = lax.axis_index('sp')
        halves = [slice(z * BLK, (z + 1) * BLK) for z in range(2)]
        dy_half = [dy_in[0, rows] for rows in halves]
        x_half = [x_in[0, rows] for rows in halves]

        def mine(w, n, axis):
            return lax.dynamic_slice_in_dim(w, me * n * head, n * head, axis)

        x_f32, normed, pre_pull, normed_all = [], [], [], []
        for z in range(2):
            if z == 1:
                x_half[1], normed[0] = lax.optimization_barrier((x_half[1], normed[0]))
                normed_all.append(gather(normed[0]))
            x_f32.append(x_half[z].astype(F32))
            out, pull = jax.vjp(pre_norm, x_f32[z], w_pre)
            normed.append(out)
            pre_pull.append(pull)
        normed_all.append(gather(normed[1]))
        cosines, sines = rope_tables(gather(positions), head)
        w_mine = jnp.concatenate([mine(w_q, n_q, 1), mine(w_k, n_k, 1), mine(w_v, n_k, 1)], axis=1)
        qn = q_norm[None, :]
        kn = k_norm[None, :]
        qkv, q_all, kv = [], [], ()
        for z in range(2):
            qkv.append(dot(normed_all[z], w_mine, NN).astype(BF16))
            q, *kv = rope_fwd(z, qkv[z], cosines, sines, qn, kn, n_q, n_k, head, kv)
            q_all.append(q)
        k_all, v_all = kv

        w_o3 = w_o.reshape(group, n_q * head, width)
        o_all, lse, y_out, dy_f32, d_proj_all, dw_post = [], [], [], [], [], []
        for z in range(2):
            o, row_lse = attn_fwd(z, q_all[z], k_all, v_all, per, head)
            o_all.append(o)
            lse.append(row_lse)
        o_mine = [exchange(o) for o in o_all]
        for z in range(2):
            proj = jnp.einsum('gtn,gnd->td', o_mine[z], w_o3, preferred_element_type=F32).astype(BF16)
            post, post_pull = jax.vjp(post_norm, proj, w_post)
            y_out.append((x_f32[z] + post).astype(BF16))
            dy_f32.append(dy_half[z].astype(F32))
            d_proj, dw = post_pull(dy_f32[z])
            dw_post.append(dw)
            if z == 0:
                dy_half[1], d_proj = lax.optimization_barrier((dy_half[1], d_proj))
            d_proj_all.append(gather(d_proj))

        wo_mine = mine(w_o, n_q, 0)
        do_0 = dot(d_proj_all[0], wo_mine, NT).astype(BF16)
        dq_0, *partial = attn_bwd(0, q_all[0], do_0, o_all[0], lse[0], k_all, v_all, per, head, ())
        dq_proj_0, gq_0 = rope_bwd(0, dq_0, (), qkv[0], 0, cosines, sines, qn, n_q, head)
        do_1 = dot(d_proj_all[1], wo_mine, NT).astype(BF16)
        dw_o = (dot(o_all[0], d_proj_all[0], TN) + dot(o_all[1], d_proj_all[1], TN)).astype(BF16)
        do_1, dw_o, dq_proj_0, partial = lax.optimization_barrier((do_1, dw_o, dq_proj_0, partial))
        dw_o = gather(dw_o)
        dq_flat_0 = exchange(dq_proj_0)
        dq_1, dk_all, dv_all = attn_bwd(1, q_all[1], do_1, o_all[1], lse[1], k_all, v_all, per, head, partial)
        dq_1, dk_all, dv_all, dq_flat_0 = lax.optimization_barrier((dq_1, dk_all, dv_all, dq_flat_0))
        dq_proj_1, gq_1 = rope_bwd(1, dq_1, (), qkv[1], 0, cosines, sines, qn, n_q, head)
        dkv, gk = [], []
        for z in range(2):
            out, sums = rope_bwd(z, dk_all, (dv_all,), qkv[z], n_q, cosines, sines, kn, n_k, head)
            dkv.append(out)
            gk.append(sums)
        dq_flat = [dq_flat_0, exchange(dq_proj_1)]
        dq_proj_1, dkv = lax.optimization_barrier((dq_proj_1, dkv))

        def weight_grad(grads):
            return (dot(normed_all[0], grads[0], TN) + dot(normed_all[1], grads[1], TN)).astype(BF16)

        dw_q = weight_grad((dq_proj_0, dq_proj_1))
        dw_q, dw_o, dq_flat[1], dkv = lax.optimization_barrier((dw_q, dw_o, dq_flat[1], dkv))
        dw_q = gather(dw_q, 1)
        dkv_flat = [exchange(dkv[0])]
        dw_kv = weight_grad(dkv)
        dw_kv, dkv_flat[0], dkv[1] = lax.optimization_barrier((dw_kv, dkv_flat[0], dkv[1]))
        dw_k = gather(dw_kv[:, :n_k * head], 1)
        dw_v = gather(dw_kv[:, n_k * head:], 1)
        dkv_flat.append(exchange(dkv[1]))
        dw_o = place(dw_o)

        def back(flat, w):
            return jnp.einsum('gtn,dgn->td', flat, w.reshape(width, group, -1), preferred_element_type=F32)

        dx_out, dw_pre = [], []
        for z in range(2):
            dk_flat = dkv_flat[z][:, :, :n_k * head]
            dv_flat = dkv_flat[z][:, :, n_k * head:]
            d_normed = (back(dq_flat[z], w_q) + back(dk_flat, w_k) + back(dv_flat, w_v)).astype(BF16)
            dx_norm, dw = pre_pull[z](d_normed)
            dw_pre.append(dw)
            dx_out.append((dy_f32[z] + dx_norm).astype(BF16))
        dw_pre = dw_pre[0] + dw_pre[1]
        dw_pre, dw_o = lax.optimization_barrier((dw_pre, dw_o))
        sums = lax.psum((dw_pre, dw_post[0] + dw_post[1], jnp.sum(gq_0 + gq_1, axis=0), jnp.sum(gk[0] + gk[1], axis=0)), 'sp')
        dw_q, sums = lax.optimization_barrier((dw_q, sums))
        return (jnp.concatenate(y_out)[None], jnp.concatenate(dx_out)[None], place(dw_q), place(dw_k), dw_v, dw_o, sums[0], sums[1], sums[2], sums[3])

    token_spec = P('dp', 'sp', None)
    return jax.shard_map(device_step, mesh=mesh,
                         in_specs=(token_spec, token_spec, P(('dp', 'sp')), P(None, None), P(None, None), P(None, None), P(None, None), P(None), P(None), P(None), P(None)),
                         out_specs=(token_spec, token_spec, P('dp', None), P('dp', None), P('dp', None), P('dp', None), P('dp'), P('dp'), P('dp'), P('dp')),
                         check_vma=False)
```

time: 2100 us -> 1690 us (0.80)
  waiting for transfers between devices: 971 us -> 389 us
  blocking collectives: 35.9 us -> 135 us
  Pallas kernels: 478 us -> 563 us
  local copies, waits for them, and re-layouts: 110 us -> 36.5 us
  matrix products: 405 us -> 430 us
  other arithmetic: 68 us -> 91.8 us
    all_gather x6 -> x8, waiting for transfers between devices: 647 us -> 313 us  [gather(): return lax.all_gather(arr, 'sp', axis=axis, tiled=True)]
    all_to_all x4 -> x5, waiting for transfers between devices: 324 us -> 74.6 us  [exchange(): lax.all_to_all(arr.reshape(group, -1, arr.shape[1]), 'sp', 0, 0, tiled=True)]
    dot_general x0 -> x8, matrix products: none -> 164 us  [the longest x6 120 us: back(): jnp.einsum('gtn,dgn->td', flat, w.reshape(width, group, -1), preferred_el...]
    dot_general x11 -> x10, matrix products: 405 us -> 266 us  [dot(): return lax.dot_general(a, b, dims, preferred_element_type=F32)]
    all_to_all x0 -> x1, blocking collectives: none -> 97 us  [exchange(): lax.all_to_all(arr.reshape(group, -1, arr.shape[1]), 'sp', 0, 0, tiled=True)]
    pallas_call x3 -> x11, Pallas kernels: 459 us -> 542 us  [the longest x2 289 us: attn_bwd(): pl.pallas_call(functools.partial(attn_bwd_kernel, z, per, head, blk), nam...]
    unnamed x36 -> x71, local copies, waits for them, and re-layouts: 66 us -> 15.4 us
    all_to_all x4 -> x0, local copies, waits for them, and re-layouts: 35.7 us -> none  [the longest x1 11.4 us: device_step(): dq_flat = lax.all_to_all(dq_proj, 'sp', 0, 1, tiled=True)]
  transfers between devices with their start and end apart: 10 -> 13, of which waited for: 7 -> 6; matrix products, arithmetic and copies ran while one was open for 13% -> 24% of each run, Pallas kernels for 0% -> 27%
where the time goes in v2:
time: 1690 us; the launch traced here: 1680 us
  Pallas kernels  563 us (33%)
  matrix products  430 us (25%)
  waiting for transfers between devices  389 us (23%)
  blocking collectives  135 us (8%)
  other arithmetic  91.8 us (5%)
  local copies, waits for them, and re-layouts  36.5 us (2%)
  starting transfers between devices  18.2 us (1%)
    all_gather x8, waiting for transfers between devices, gather(): return lax.all_gather(arr, 'sp', axis=axis, tiled=True)  313 us
    pallas_call x2, Pallas kernels, attn_bwd(): pl.pallas_call(functools.partial(attn_bwd_kernel, z, per, head, blk), nam...  289 us
    dot_general x10, matrix products, dot(): return lax.dot_general(a, b, dims, preferred_element_type=F32)  266 us
    pallas_call x2, Pallas kernels, attn_fwd(): pl.pallas_call(functools.partial(attn_fwd_kernel, z, per, head, blk), nam...  144 us
    dot_general x6, matrix products, back(): jnp.einsum('gtn,dgn->td', flat, w.reshape(width, group, -1), preferred_el...  120 us
    all_to_all x1, blocking collectives, exchange(): lax.all_to_all(arr.reshape(group, -1, arr.shape[1]), 'sp', 0, 0, tiled=True)  97 us
    all_to_all x5, waiting for transfers between devices, exchange(): lax.all_to_all(arr.reshape(group, -1, arr.shape[1]), 'sp', 0, 0, tiled=True)  74.6 us
    pallas_call x3, Pallas kernels, place(): pl.pallas_call(copy_kernel, name='place', grid=(x.shape[0] // rows,), in_...  69.5 us
  transfers between devices with their start and end apart: 13, of which 6 were waited for; matrix products, arithmetic and copies ran while one was open for 24% of the time, Pallas kernels for 27%

profile of v2, /device:TPU:0, one launch (start us, length us, event | category | flops | bytes accessed | tf_op | source)
XLA Modules:
  0.0 1678.8 jit_solution(2983223245038973589)
XLA Ops:
  7.2 3.1 fusion.43
  10.4 4.6 slice_bitcast_fusion.1
  15.6 3.3 fusion.26
  19.0 3.0 fusion.40
  23.1 5.8 fusion.27
  28.9 13.4 all_gather.28
  42.3 4.3 constant_dynamic-slice_fusion.2
  46.6 3.7 constant_dynamic-slice_fusion
  50.3 18.5 %multiply_sine_fusion = (f32[8192,128]{1,0:T(8,128)}, f32[8192,128]{1,0:T(8,128)}) fusion(f32[128]{0:T(128)S(1)} %multiply_power_fusion, f32[8192]{0:T(1024)S(1)} %convert_multiply_fusion.24), kind=kLoop, calls=%fused_computation.94 | loop fusion | flops 1048576 | bytes 8421888 | tf_op jit(solution)/shard_map/sin | solution.py:43
  68.8 99.4 %all-gather.9.cloned.1.call-done = bf16[4096,3840]{1,0:T(8,128)(2,1)} async-done(((bf16[512,3840]{1,0:T(8,128)(2,1)}), bf16[4096,3840]{1,0:T(8,128)(2,1)}) %all-gather.9.cloned.1.call-update) | async-done | bytes 31457296 | tf_op jit(solution)/shard_map/all_gather | solution.py:346
  168.2 39.3 %convolution_convert_fusion.1.x_ref = bf16[4096,1024]{1,0:T(8,128)(2,1)} fusion(bf16[4096,3840]{1,0:T(8,128)(2,1)} %all-gather.9.cloned.1.call-done, bf16[3840,256]{1,0:T(8,128)(2,1)S(1)} %get-tuple-element.148, bf16[3840,256]{1,0:T(8,128)(2,1)} %get-tuple-element.149, bf16[3840,512]{1,0:T(8,128)(2,1)} %constant_dynamic-slice_fusion.2), kind=kOutput, calls=%fused_computation.93 | convolution fusion | flops 32240041984 | bytes 47710208 | tf_op jit(solution)/shard_map/dot_general | solution.py:23
  207.4 10.9 rope_fwd.2
  218.3 98.5 %all-gather.11.cloned.1.call-done = bf16[4096,3840]{1,0:T(8,128)(2,1)} async-done(((bf16[512,3840]{1,0:T(8,128)(2,1)}), bf16[4096,3840]{1,0:T(8,128)(2,1)}) %all-gather.11.cloned.1.call-update) | async-done | bytes 31457296 | tf_op jit(solution)/shard_map/all_gather | solution.py:346
  316.8 39.3 %convolution_convert_fusion.x_ref = bf16[4096,1024]{1,0:T(8,128)(2,1)} fusion(bf16[4096,3840]{1,0:T(8,128)(2,1)} %all-gather.11.cloned.1.call-done, bf16[3840,256]{1,0:T(8,128)(2,1)S(1)} %get-tuple-element.148, bf16[3840,256]{1,0:T(8,128)(2,1)} %get-tuple-element.149, bf16[3840,512]{1,0:T(8,128)(2,1)} %constant_dynamic-slice_fusion.2), kind=kOutput, calls=%fused_computation.92 | convolution fusion | flops 32240041984 | bytes 47710208 | tf_op jit(solution)/shard_map/dot_general | solution.py:23
  356.1 10.9 rope_fwd.3
  367.0 67.2 %attn_fwd.2 = (bf16[4096,512]{1,0:T(8,128)(2,1)}, f32[2,4096]{1,0:T(2,128)}) custom-call(bf16[4096,512]{1,0:T(8,128)(2,1)} %get-tuple-element.66.q_ref, bf16[8192,256]{1,0:T(8,128)(2,1)} %get-tuple-element.70.k_ref, bf16[8192,256]{1,0:T(8,128)(2,1)} %get-tuple-element.71.v_ref), custom_call_target="tpu_custom_call" | custom-call | flops 36507222016 | bytes 16777216 | tf_op jit(solution)/shard_map/attn_fwd/pallas_call | solution.py:211
  434.2 3.6 all-to-all-start
  437.8 4.2 slice_bitcast_fusion
  442.1 44.8 %all-to-all-done = bf16[8,512,512]{2,1,0:T(8,128)(2,1)} async-done(((bf16[8,512,512]{2,1,0:T(8,128)(2,1)}), bf16[8,512,512]{2,1,0:T(8,128)(2,1)}, u32[]{:S(2)}, u32[]{:S(2)}) %all-to-all-start) | async-done | bytes 4194336 | tf_op jit(solution)/shard_map/all_to_all | solution.py:349
  486.9 22.3 %fusion.36 = (f32[512]{0:T(512)S(1)}, bf16[512,3840]{1,0:T(8,128)(2,1)S(1)}) fusion(bf16[8,512,512]{2,1,0:T(8,128)(2,1)} %all-to-all-done, bf16[8,512,3840]{2,1,0:T(8,128)(2,1)} %bitcast.123), kind=kOutput, calls=%fused_computation.68 | convolution fusion | flops 16113991680 | bytes 39585792 | tf_op jit(solution)/shard_map/gtn,gnd->td/dot_general | solution.py:394
  509.2 8.2 fusion.35
  517.5 3.9 fusion.30
  521.4 76.6 %attn_fwd.3 = (bf16[4096,512]{1,0:T(8,128)(2,1)}, f32[2,4096]{1,0:T(2,128)}) custom-call(bf16[4096,512]{1,0:T(8,128)(2,1)} %get-tuple-element.73.q_ref, bf16[8192,256]{1,0:T(8,128)(2,1)} %get-tuple-element.70.k_ref, bf16[8192,256]{1,0:T(8,128)(2,1)} %get-tuple-element.71.v_ref), custom_call_target="tpu_custom_call" | custom-call | flops 36507222016 | bytes 16777216 | tf_op jit(solution)/shard_map/attn_fwd/pallas_call | solution.py:211
  598.0 97.0 %all_to_all.30 = bf16[8,512,512]{2,1,0:T(8,128)(2,1)S(1)} all-to-all(bf16[8,512,512]{2,1,0:T(8,128)(2,1)} %bitcast.105), channel_id=1, replica_groups=mesh['dp'=1,'sp'=8] {'sp'}, dimensions={0} | all-to-all | bytes 8388608 | tf_op jit(solution)/shard_map/all_to_all | solution.py:349
  695.0 21.1 %fusion.38 = (f32[512]{0:T(512)S(1)}, bf16[512,3840]{1,0:T(8,128)(2,1)S(1)}) fusion(bf16[8,512,512]{2,1,0:T(8,128)(2,1)S(1)} %all_to_all.30, bf16[8,512,3840]{2,1,0:T(8,128)(2,1)} %bitcast.124), kind=kOutput, calls=%fused_computation.70 | convolution fusion | flops 16113991680 | bytes 39585792 | tf_op jit(solution)/shard_map/gtn,gnd->td/dot_general | solution.py:394
  716.2 5.3 fusion.32
  721.5 6.0 fusion.33
  728.0 25.5 %convolution_convert_fusion.2.do_ref = bf16[4096,512]{1,0:T(8,128)(2,1)} fusion(bf16[4096,3840]{1,0:T(8,128)(2,1)} %all-gather.15.cloned.1.call-done, bf16[4096,3840]{1,0:T(8,128)(2,1)} %param.17, s32[]{:T(128)S(6)} %select_n.8), kind=kOutput, calls=%fused_computation.96 | convolution fusion | flops 16108224512 | bytes 39583748 | tf_op jit(solution)/shard_map/dot_general | solution.py:23
  753.5 134.5 %attn_bwd.2 = (bf16[4096,512]{1,0:T(8,128)(2,1)}, f32[8192,256]{1,0:T(8,128)}, f32[8192,256]{1,0:T(8,128)}) custom-call(bf16[4096,512]{1,0:T(8,128)(2,1)} %get-tuple-element.66.q_ref, bf16[4096,512]{1,0:T(8,128)(2,1)} %convolution_convert_fusion.2.do_ref, bf16[4096,512]{1,0:T(8,128)(2,1)} %get-tuple-element.72.o_ref, f32[2,4096]{1,0:T(2,128)} %get-tuple-element.77.lse_ref, ...), custom_call_target="tpu_custom_call" | custom-call | flops 91268055040 | bytes 50331648 | tf_op jit(solution)/shard_map/attn_bwd/pallas_call | solution.py:327
  888.0 10.6 rope_bwd.4
  898.5 24.1 %fusion.67 = f32[512,3840]{1,0:T(8,128)} fusion(bf16[4096,512]{1,0:T(8,128)(2,1)} %get-tuple-element.72.o_ref, bf16[4096,3840]{1,0:T(8,128)(2,1)} %all-gather.15.cloned.1.call-done), kind=kOutput, calls=%fused_computation.132 | convolution fusion | flops 16106127360 | bytes 43515904 | tf_op jit(solution)/shard_map/dot_general | solution.py:23
  922.7 23.4 %convolution_convert_fusion.3.do_ref = bf16[4096,512]{1,0:T(8,128)(2,1)} fusion(bf16[4096,3840]{1,0:T(8,128)(2,1)} %all-gather.13.cloned.1.call-done, bf16[4096,3840]{1,0:T(8,128)(2,1)} %param.17, s32[]{:T(128)S(6)} %select_n.8), kind=kOutput, calls=%fused_computation.97 | convolution fusion | flops 16108224512 | bytes 39583748 | tf_op jit(solution)/shard_map/dot_general | solution.py:23
  946.1 22.8 %add_convert_fusion.2 = bf16[512,3840]{1,0:T(8,128)(2,1)} fusion(f32[512,3840]{1,0:T(8,128)S(1)} %copy-done.32, bf16[4096,512]{1,0:T(8,128)(2,1)S(1)} %copy-done.5, bf16[4096,3840]{1,0:T(8,128)(2,1)} %all-gather.13.cloned.1.call-done), kind=kOutput, calls=%fused_computation.91 | convolution fusion | flops 16110059520 | bytes 47448064 | tf_op jit(solution)/shard_map/dot_general | solution.py:23
  969.0 3.3 all-to-all-start.2
  972.3 154.6 %attn_bwd.3 = (bf16[4096,512]{1,0:T(8,128)(2,1)}, bf16[8192,256]{1,0:T(8,128)(2,1)}, bf16[8192,256]{1,0:T(8,128)(2,1)}) custom-call(bf16[4096,512]{1,0:T(8,128)(2,1)} %get-tuple-element.73.q_ref, bf16[4096,512]{1,0:T(8,128)(2,1)} %convolution_convert_fusion.3.do_ref, bf16[4096,512]{1,0:T(8,128)(2,1)} %get-tuple-element.74.o_ref, ...), custom_call_target="tpu_custom_call" | custom-call | flops 91268055040 | bytes 50331648 | tf_op jit(solution)/shard_map/attn_bwd/pallas_call | solution.py:327
  1126.9 10.8 rope_bwd.5
  1137.7 3.7 all-to-all-start.3
  1141.4 23.8 %fusion.68 = f32[3840,512]{1,0:T(8,128)} fusion(bf16[4096,3840]{1,0:T(8,128)(2,1)} %all-gather.9.cloned.1.call-done, bf16[4096,512]{1,0:T(8,128)(2,1)} %get-tuple-element.89), kind=kOutput, calls=%fused_computation.133 | convolution fusion | flops 16106127360 | bytes 43515904 | tf_op jit(solution)/shard_map/dot_general | solution.py:23
  1165.2 9.0 rope_bwd.7
  1174.2 9.0 rope_bwd.6
  1183.2 24.0 %add_convert_fusion.1 = bf16[3840,512]{1,0:T(8,128)(2,1)} fusion(f32[3840,512]{1,0:T(8,128)} %fusion.68, bf16[4096,3840]{1,0:T(8,128)(2,1)} %all-gather.11.cloned.1.call-done, bf16[4096,512]{1,0:T(8,128)(2,1)} %get-tuple-element.97), kind=kOutput, calls=%fused_computation.90 | convolution fusion | flops 16110059520 | bytes 47448064 | tf_op jit(solution)/shard_map/dot_general | solution.py:23
  1207.2 3.3 all-to-all-start.4
  1210.6 21.5 %fusion.69 = f32[3840,512]{1,0:T(8,128)S(1)} fusion(bf16[4096,3840]{1,0:T(8,128)(2,1)} %all-gather.9.cloned.1.call-done, bf16[4096,512]{1,0:T(8,128)(2,1)} %get-tuple-element.101), kind=kOutput, calls=%fused_computation.134 | convolution fusion | flops 16106127360 | bytes 43515904 | tf_op jit(solution)/shard_map/dot_general | solution.py:23
  1232.1 22.3 %add_convert_fusion = bf16[3840,512]{1,0:T(8,128)(2,1)} fusion(f32[3840,512]{1,0:T(8,128)S(1)} %fusion.69, bf16[4096,3840]{1,0:T(8,128)(2,1)} %all-gather.11.cloned.1.call-done, bf16[4096,512]{1,0:T(8,128)(2,1)S(1)} %copy-done.4), kind=kOutput, calls=%fused_computation.89 | convolution fusion | flops 16110059520 | bytes 47448064 | tf_op jit(solution)/shard_map/dot_general | solution.py:23
  1254.5 5.1 all-to-all-done.4
  1259.6 4.4 fusion.66
  1264.8 0.7 all-gather.19.cloned.1.call-update
  1267.3 24.7 %fusion.2 = f32[512,3840,1]{1,0,2:T(8,128)} fusion(bf16[8,512,512]{2,1,0:T(8,128)(2,1)} %all-to-all-done.2, bf16[480,8,8,512]{3,2,1,0:T(8,128)(2,1)} %bitcast.109), kind=kOutput, calls=%fused_computation.2 | convolution fusion | flops 16106127360 | bytes 43515904 | tf_op jit(solution)/shard_map/gtn,dgn->td/dot_general | solution.py:439
  1292.0 3.5 all-to-all-start.5
  1295.6 25.5 %fusion = f32[512,3840,1]{1,0,2:T(8,128)} fusion(bf16[8,512,512]{2,1,0:T(8,128)(2,1)} %all-to-all-done.3, bf16[480,8,8,512]{3,2,1,0:T(8,128)(2,1)} %bitcast.110), kind=kOutput, calls=%fused_computation | convolution fusion | flops 16106127360 | bytes 43515904 | tf_op jit(solution)/shard_map/gtn,dgn->td/dot_general | solution.py:439
  1321.0 25.9 %place.3 = bf16[4096,3840]{1,0:T(8,128)(2,1)} custom-call(bf16[4096,3840]{1,0:T(8,128)(2,1)} %all-gather.17.cloned.1.call-done.x_ref), custom_call_target="tpu_custom_call" | custom-call | flops 251658240 | bytes 62914560 | tf_op jit(solution)/shard_map/place/pallas_call | solution.py:135
  1347.0 14.8 fusion.8
  1361.8 24.7 %all-to-all-done.5 = bf16[8,512,512]{2,1,0:T(8,128)(2,1)} async-done(((bf16[8,512,512]{2,1,0:T(8,128)(2,1)}), bf16[8,512,512]{2,1,0:T(8,128)(2,1)}, u32[]{:S(2)}, u32[]{:S(2)}) %all-to-all-start.5) | async-done | bytes 4194336 | tf_op jit(solution)/shard_map/all_to_all | solution.py:349
  1386.5 14.8 fusion.6
  1401.3 18.3 %fusion.46 = bf16[512,3840]{1,0:T(8,128)(2,1)} fusion(f32[512,3840,1]{1,0,2:T(8,128)} %fusion.6, f32[512,3840,1]{1,0,2:T(8,128)} %fusion, bf16[480,8,8,256]{3,2,1,0:T(8,128)(2,1)} %bitcast.113, bf16[8,512,512]{2,1,0:T(8,128)(2,1)} %all-to-all-done.5), kind=kOutput, calls=%fused_computation.82 | convolution fusion | flops 8058961920 | bytes 37486592 | tf_op jit(solution)/shard_map/gtn,dgn->td/dot_general | solution.py:439
  1419.7 22.1 %fusion.28 = (f32[3840]{0:T(1024)S(1)}, f32[512]{0:T(512)S(1)}, f32[512]{0:T(512)S(1)}, f32[3840]{0:T(1024)S(1)}, bf16[512,3840]{1,0:T(8,128)(2,1)}) fusion(f32[512]{0:T(512)S(1)} %copy-done.20, bf16[1,1024,3840]{2,1,0:T(8,128)(2,1)} %param.11, f32[3840]{0:T(1024)S(1)} %copy-done.9, bf16[512,3840]{1,0:T(8,128)(2,1)} %fusion.46, f32[512]{0:T(512)S(1)} %copy-done.22, ...), kind=kOutput, calls=%fused_computation.60 | convolution fusion | flops 8090409984 | bytes 49337344 | tf_op jit(solution)/shard_map/gtn,dgn->td/dot_general | solution.py:439
  1441.8 24.9 %all-reduce = (f32[3840]{0:T(1024)}, f32[3840]{0:T(1024)}, f32[256]{0:T(256)}, f32[256]{0:T(256)}) all-reduce(f32[3840]{0:T(1024)S(1)} %add.128, f32[3840]{0:T(1024)S(1)} %copy-done.12, f32[256]{0:T(256)S(1)} %copy-done.31, f32[256]{0:T(256)S(1)} %copy-done.30), channel_id=1, replica_groups=mesh['dp'=1,'sp'=8] {'sp'}, use_global_device_ids=true, to_apply=%region_10.0 | all-reduce | flops 8192 | bytes 65536 | tf_op jit(solution)/shard_map/psum | solution.py:451
  1466.7 17.0 %fusion.34 = (bf16[512,3840]{1,0:T(8,128)(2,1)}, bf16[512,3840]{1,0:T(8,128)(2,1)}, bf16[512,3840]{1,0:T(8,128)(2,1)}) fusion(bf16[512,3840]{1,0:T(8,128)(2,1)} %get-tuple-element.147, f32[512]{0:T(512)S(1)} %multiply_multiply_fusion.1, f32[3840]{0:T(1024)S(1)} %copy-done.9, f32[512]{0:T(512)S(1)} %copy-done.20, bf16[1,1024,3840]{2,1,0:T(8,128)(2,1)} %param.12, ...), kind=kLoop, calls=%fused_computation.66 | loop fusion | flops 49152000 | bytes 39362560 | tf_op jit(solution)/shard_map/convert_element_type | solution.py:448
  1483.8 8.5 maximum_bitcast_fusion.1
  1492.3 7.3 maximum_bitcast_fusion
  1499.7 17.1 %place.5 = bf16[3840,2048]{1,0:T(8,128)(2,1)} custom-call(bf16[3840,2048]{1,0:T(8,128)(2,1)} %all-gather.21.cloned.1.call-done.x_ref), custom_call_target="tpu_custom_call" | custom-call | flops 125829120 | bytes 31457280 | tf_op jit(solution)/shard_map/place/pallas_call | solution.py:135
  1516.7 114.8 %all-gather.19.cloned.1.call-done.x_ref = bf16[3840,4096]{1,0:T(8,128)(2,1)} async-done(((bf16[3840,512]{1,0:T(8,128)(2,1)}), bf16[3840,4096]{1,0:T(8,128)(2,1)}) %all-gather.19.cloned.1.call-update) | async-done | bytes 31457296 | tf_op jit(solution)/shard_map/all_gather | solution.py:346
  1631.5 26.5 %place.4 = bf16[3840,4096]{1,0:T(8,128)(2,1)} custom-call(bf16[3840,4096]{1,0:T(8,128)(2,1)} %all-gather.19.cloned.1.call-done.x_ref), custom_call_target="tpu_custom_call" | custom-call | flops 251658240 | bytes 62914560 | tf_op jit(solution)/shard_map/place/pallas_call | solution.py:135
  1658.0 13.5 copy.71
  (109 shorter events, 5.3 us)
Async XLA Ops:
  7.2 7.8 copy-start.23
  7.2 161.0 %all-gather.9.cloned.1.call-start = ((), (), s32[]{:S(2)}) async-start(), calls=%async_computation.6 | async-start | bytes 35389440 | tf_op jit(solution)/shard_map/all_gather | solution.py:346
  7.2 8.3 copy-start.3
  10.4 4.6 copy-start.15
  14.9 7.6 copy-start.8
  15.0 0.6 copy-start.19
  18.9 10.0 copy-start.29
  18.9 297.9 %all-gather.11.cloned.1.call-start = ((), (), s32[]{:S(2)}) async-start(), calls=%async_computation.7 | async-start | bytes 35389440 | tf_op jit(solution)/shard_map/all_gather | solution.py:346
  21.9 0.6 copy-start.17
  22.5 0.6 copy-start.21
  434.2 3.7 copy-start.24
  434.2 52.7 %all-to-all-start = ((bf16[8,512,512]{2,1,0:T(8,128)(2,1)}), bf16[8,512,512]{2,1,0:T(8,128)(2,1)}, u32[]{:S(2)}, u32[]{:S(2)}) async-start(bf16[8,512,512]{2,1,0:T(8,128)(2,1)} %bitcast.104), calls=%async_computation | async-start | bytes 8388608 | tf_op jit(solution)/shard_map/all_to_all | solution.py:349
  437.8 290.2 %all-gather.15.cloned.1.call-start = ((), (), s32[]{:S(2)}) async-start(), calls=%async_computation.9 | async-start | bytes 35389440 | tf_op jit(solution)/shard_map/all_gather | solution.py:346
  437.8 283.6 %copy-start.6 = (f32[3840]{0:T(1024)}, f32[3840]{0:T(1024)S(1)}, u32[]{:S(2)}) copy-start(f32[3840]{0:T(1024)S(1)} %broadcast_add_fusion) | copy-start | bytes 46084
  486.9 30.6 %slice-start = ((s8[7864320]{0:T(1024)(128)(4,1)}), s8[4194304]{0:T(1024)(128)(4,1)S(1)}, s32[]{:S(2)}) async-start(s8[7864320]{0:T(1024)(128)(4,1)} %bitcast.101), calls=%async_computation.14 | async-start | bytes 8388608
  486.9 30.6 %slice-start.1 = ((s8[7864320]{0:T(1024)(128)(4,1)}), s8[3670016]{0:T(1024)(128)(4,1)S(1)}, s32[]{:S(2)}) async-start(s8[7864320]{0:T(1024)(128)(4,1)} %bitcast.101), calls=%async_computation.15 | async-start | bytes 7340032
  509.2 8.3 copy-start.2
  509.2 8.2 copy-start.13
  521.4 401.3 %all-gather.13.cloned.1.call-start = ((), (), s32[]{:S(2)}) async-start(), calls=%async_computation.8 | async-start | bytes 35389440 | tf_op jit(solution)/shard_map/all_gather | solution.py:346
  695.0 21.1 %copy-start.1 = (bf16[512,3840]{1,0:T(8,128)(2,1)S(1)}, bf16[512,3840]{1,0:T(8,128)(2,1)}, u32[]{:S(2)}) copy-start(bf16[512,3840]{1,0:T(8,128)(2,1)} %slice_bitcast_fusion) | copy-start | bytes 11796484
  716.1 5.3 copy-start
  727.5 479.7 %all-gather.17.cloned.1.call-start = ((), (), s32[]{:S(2)}) async-start(), calls=%async_computation.10 | async-start | bytes 35389440 | tf_op jit(solution)/shard_map/all_gather | solution.py:346
  922.6 23.4 %copy-start.5 = (bf16[4096,512]{1,0:T(8,128)(2,1)S(1)}, bf16[4096,512]{1,0:T(8,128)(2,1)}, u32[]{:S(2)}) copy-start(bf16[4096,512]{1,0:T(8,128)(2,1)} %get-tuple-element.74.o_ref) | copy-start | bytes 12582916
  922.7 23.4 %copy-start.32 = (f32[512,3840]{1,0:T(8,128)S(1)}, f32[512,3840]{1,0:T(8,128)}, u32[]{:S(2)}) copy-start(f32[512,3840]{1,0:T(8,128)} %fusion.67) | copy-start | bytes 23592964
  969.0 157.9 %all-to-all-start.2 = ((bf16[8,512,512]{2,1,0:T(8,128)(2,1)}), bf16[8,512,512]{2,1,0:T(8,128)(2,1)}, u32[]{:S(2)}, u32[]{:S(2)}) async-start(bf16[8,512,512]{2,1,0:T(8,128)(2,1)} %bitcast.106), calls=%async_computation.2 | async-start | bytes 8388608 | tf_op jit(solution)/shard_map/all_to_all | solution.py:349
  1137.7 69.5 %all-to-all-start.3 = ((bf16[8,512,512]{2,1,0:T(8,128)(2,1)}), bf16[8,512,512]{2,1,0:T(8,128)(2,1)}, u32[]{:S(2)}, u32[]{:S(2)}) async-start(bf16[8,512,512]{2,1,0:T(8,128)(2,1)} %bitcast.108), calls=%async_computation.3 | async-start | bytes 8388608 | tf_op jit(solution)/shard_map/all_to_all | solution.py:349
  1207.2 52.4 %all-to-all-start.4 = ((bf16[8,512,512]{2,1,0:T(8,128)(2,1)}), bf16[8,512,512]{2,1,0:T(8,128)(2,1)}, u32[]{:S(2)}, u32[]{:S(2)}) async-start(bf16[8,512,512]{2,1,0:T(8,128)(2,1)} %bitcast.107), calls=%async_computation.4 | async-start | bytes 8388608 | tf_op jit(solution)/shard_map/all_to_all | solution.py:349
  1210.5 289.2 %all-gather.23.cloned.1.call-start = ((), (), s32[]{:S(2)}) async-start(), calls=%async_computation.13 | async-start | bytes 17694720 | tf_op jit(solution)/shard_map/all_gather | solution.py:346
  1210.5 21.6 %copy-start.4 = (bf16[4096,512]{1,0:T(8,128)(2,1)S(1)}, bf16[4096,512]{1,0:T(8,128)(2,1)}, u32[]{:S(2)}) copy-start(bf16[4096,512]{1,0:T(8,128)(2,1)} %get-tuple-element.105) | copy-start | bytes 12582916
  1254.5 11.1 copy-start.10
  1254.5 11.1 copy-start.11
  1254.5 11.7 copy-start.27
  1254.5 11.7 copy-start.28
  1254.5 12.3 copy-start.25
  1254.5 12.3 copy-start.26
  1264.0 235.7 %all-gather.21.cloned.1.call-start = ((), (), s32[]{:S(2)}) async-start(), calls=%async_computation.12 | async-start | bytes 17694720 | tf_op jit(solution)/shard_map/all_gather | solution.py:346
  1264.8 366.7 %all-gather.19.cloned.1.call-start = ((), (), s32[]{:S(2)}) async-start(), calls=%async_computation.11 | async-start | bytes 35389440 | tf_op jit(solution)/shard_map/all_gather | solution.py:346
  1292.0 94.4 %all-to-all-start.5 = ((bf16[8,512,512]{2,1,0:T(8,128)(2,1)}), bf16[8,512,512]{2,1,0:T(8,128)(2,1)}, u32[]{:S(2)}, u32[]{:S(2)}) async-start(bf16[8,512,512]{2,1,0:T(8,128)(2,1)} %bitcast.103), calls=%async_computation.5 | async-start | bytes 8388608 | tf_op jit(solution)/shard_map/all_to_all | solution.py:349
  1401.3 18.3 %copy-start.9 = (f32[3840]{0:T(1024)S(1)}, f32[3840]{0:T(1024)}, u32[]{:S(2)}) copy-start(f32[3840]{0:T(1024)} %copy-done.8) | copy-start | bytes 46084
  1401.3 18.3 %copy-start.20 = (f32[512]{0:T(512)S(1)}, f32[512]{0:T(512)}, u32[]{:S(2)}) copy-start(f32[512]{0:T(512)} %copy-done.19) | copy-start | bytes 6148
  1401.3 18.3 %copy-start.22 = (f32[512]{0:T(512)S(1)}, f32[512]{0:T(512)}, u32[]{:S(2)}) copy-start(f32[512]{0:T(512)} %copy-done.21) | copy-start | bytes 6148
  1419.6 22.2 %copy-start.12 = (f32[3840]{0:T(1024)S(1)}, f32[3840]{0:T(1024)}, u32[]{:S(2)}) copy-start(f32[3840]{0:T(1024)} %add.129) | copy-start | bytes 46084
  1419.6 22.2 %copy-start.30 = (f32[256]{0:T(256)S(1)}, f32[256]{0:T(256)}, u32[]{:S(2)}) copy-start(f32[256]{0:T(256)} %add_reduce_fusion) | copy-start | bytes 3076
  1419.6 22.2 %copy-start.31 = (f32[256]{0:T(256)S(1)}, f32[256]{0:T(256)}, u32[]{:S(2)}) copy-start(f32[256]{0:T(256)} %add_reduce_fusion.1) | copy-start | bytes 3076
  1419.6 47.1 %copy-start.18 = (f32[512]{0:T(512)S(1)}, f32[512]{0:T(512)}, u32[]{:S(2)}) copy-start(f32[512]{0:T(512)} %copy-done.17) | copy-start | bytes 6148
  1419.6 47.1 %copy-start.16 = (f32[512]{0:T(512)S(1)}, f32[512]{0:T(512)}, u32[]{:S(2)}) copy-start(f32[512]{0:T(512)} %copy-done.15) | copy-start | bytes 6148
  1419.6 47.1 %copy-start.7 = (f32[3840]{0:T(1024)S(1)}, f32[3840]{0:T(1024)}, u32[]{:S(2)}) copy-start(f32[3840]{0:T(1024)} %copy-done.6) | copy-start | bytes 46084
  1419.6 47.1 %copy-start.14 = (f32[512]{0:T(512)S(1)}, f32[512]{0:T(512)}, u32[]{:S(2)}) copy-start(f32[512]{0:T(512)} %copy-done.13) | copy-start | bytes 6148
Sparse Core Ops, SparseCore 0:
  19.0 149.1 all-gather.8
  170.6 146.2 all-gather.10
  521.5 190.2 all-gather.14
  727.6 145.3 all-gather.12
  969.1 193.1 all-gather.16
  1264.1 122.8 all-gather.22
  1388.9 88.2 all-gather.20
  1479.0 152.4 all-gather.18

commit v3 on v2

--- a/solution.py
+++ b/solution.py
@@ -371,17 +371,20 @@
             out, pull = jax.vjp(pre_norm, x_f32[z], w_pre)
             normed.append(out)
             pre_pull.append(pull)
-        normed_all.append(gather(normed[1]))
         cosines, sines = rope_tables(gather(positions), head)
         w_mine = jnp.concatenate([mine(w_q, n_q, 1), mine(w_k, n_k, 1), mine(w_v, n_k, 1)], axis=1)
         qn = q_norm[None, :]
         kn = k_norm[None, :]
-        qkv, q_all, kv = [], [], ()
-        for z in range(2):
-            qkv.append(dot(normed_all[z], w_mine, NN).astype(BF16))
+        local = [dot(normed[1], w, NN).astype(BF16).reshape(BLK, group, -1) for w in (w_k, w_v, w_q)]
+        local = jnp.concatenate([local[2], local[0], local[1]], axis=2).swapaxes(0, 1)
+        local = lax.all_to_all(local, 'sp', 0, 0, tiled=True)
+        qkv = [dot(normed_all[0], w_mine, NN).astype(BF16), local.reshape(group * BLK, -1)]
+        q_all, kv = [], ()
+        for z in range(2):
             q, *kv = rope_fwd(z, qkv[z], cosines, sines, qn, kn, n_q, n_k, head, kv)
             q_all.append(q)
-        k_all, v_all = kv
+        k_all, v_all, to_gather = lax.optimization_barrier((*kv, normed[1]))
+        normed_all.append(gather(to_gather))
 
         w_o3 = w_o.reshape(group, n_q * head, width)
         o_all, lse, y_out, dy_f32, d_proj_all, dw_post = [], [], [], [], [], []
@@ -389,7 +392,9 @@
             o, row_lse = attn_fwd(z, q_all[z], k_all, v_all, per, head)
             o_all.append(o)
             lse.append(row_lse)
-        o_mine = [exchange(o) for o in o_all]
+        o_mine = [exchange(o_all[0])]
+        o_mine[0], o_all[1] = lax.optimization_barrier((o_mine[0], o_all[1]))
+        o_mine.append(exchange(o_all[1]))
         for z in range(2):
             proj = jnp.einsum('gtn,gnd->td', o_mine[z], w_o3, preferred_element_type=F32).astype(BF16)
             post, post_pull = jax.vjp(post_norm, proj, w_post)
@@ -398,7 +403,7 @@
             d_proj, dw = post_pull(dy_f32[z])
             dw_post.append(dw)
             if z == 0:
-                dy_half[1], d_proj = lax.optimization_barrier((dy_half[1], d_proj))
+                dy_half[1], d_proj, o_mine[1], normed_all[1] = lax.optimization_barrier((dy_half[1], d_proj, o_mine[1], normed_all[1]))
             d_proj_all.append(gather(d_proj))
 
         wo_mine = mine(w_o, n_q, 0)
@@ -407,26 +412,24 @@
         dq_proj_0, gq_0 = rope_bwd(0, dq_0, (), qkv[0], 0, cosines, sines, qn, n_q, head)
         do_1 = dot(d_proj_all[1], wo_mine, NT).astype(BF16)
         dw_o = (dot(o_all[0], d_proj_all[0], TN) + dot(o_all[1], d_proj_all[1], TN)).astype(BF16)
-        do_1, dw_o, dq_proj_0, partial = lax.optimization_barrier((do_1, dw_o, dq_proj_0, partial))
+        dq_flat_0 = exchange(dq_proj_0)
+        do_1, dw_o, dq_flat_0, partial = lax.optimization_barrier((do_1, dw_o, dq_flat_0, partial))
         dw_o = gather(dw_o)
-        dq_flat_0 = exchange(dq_proj_0)
         dq_1, dk_all, dv_all = attn_bwd(1, q_all[1], do_1, o_all[1], lse[1], k_all, v_all, per, head, partial)
-        dq_1, dk_all, dv_all, dq_flat_0 = lax.optimization_barrier((dq_1, dk_all, dv_all, dq_flat_0))
         dq_proj_1, gq_1 = rope_bwd(1, dq_1, (), qkv[1], 0, cosines, sines, qn, n_q, head)
+        dq_flat = [dq_flat_0, exchange(dq_proj_1)]
+
+        def weight_grad(grads):
+            return (dot(normed_all[0], grads[0], TN) + dot(normed_all[1], grads[1], TN)).astype(BF16)
+
+        dw_q = weight_grad((dq_proj_0, dq_proj_1))
+        dw_q, dw_o, dq_flat[1], dk_all, dv_all = lax.optimization_barrier((dw_q, dw_o, dq_flat[1], dk_all, dv_all))
+        dw_q = gather(dw_q, 1)
         dkv, gk = [], []
         for z in range(2):
             out, sums = rope_bwd(z, dk_all, (dv_all,), qkv[z], n_q, cosines, sines, kn, n_k, head)
             dkv.append(out)
             gk.append(sums)
-        dq_flat = [dq_flat_0, exchange(dq_proj_1)]
-        dq_proj_1, dkv = lax.optimization_barrier((dq_proj_1, dkv))
-
-        def weight_grad(grads):
-            return (dot(normed_all[0], grads[0], TN) + dot(normed_all[1], grads[1], TN)).astype(BF16)
-
-        dw_q = weight_grad((dq_proj_0, dq_proj_1))
-        dw_q, dw_o, dq_flat[1], dkv = lax.optimization_barrier((dw_q, dw_o, dq_flat[1], dkv))
-        dw_q = gather(dw_q, 1)
         dkv_flat = [exchange(dkv[0])]
         dw_kv = weight_grad(dkv)
         dw_kv, dkv_flat[0], dkv[1] = lax.optimization_barrier((dw_kv, dkv_flat[0], dkv[1]))

time: 1690 us -> 1670 us (0.988)
  waiting for transfers between devices: 389 us -> 300 us
  blocking collectives: 135 us -> 190 us
    all_gather x1, blocking collectives: 13.4 us -> 165 us  [gather(): return lax.all_gather(arr, 'sp', axis=axis, tiled=True)]
    all_to_all x1 -> x0, blocking collectives: 97 us -> none  [exchange(): lax.all_to_all(arr.reshape(group, -1, arr.shape[1]), 'sp', 0, 0, tiled=True)]
    all_gather x8, waiting for transfers between devices: 313 us -> 224 us  [gather(): return lax.all_gather(arr, 'sp', axis=axis, tiled=True)]
    dot_general x10 -> x12, matrix products: 266 us -> 271 us  [dot(): return lax.dot_general(a, b, dims, preferred_element_type=F32)]
    all_to_all x5 -> x6, waiting for transfers between devices: 74.6 us -> 74.9 us  [exchange(): lax.all_to_all(arr.reshape(group, -1, arr.shape[1]), 'sp', 0, 0, tiled=True)]
  transfers between devices with their start and end apart: 13 -> 15, of which waited for: 6 -> 6; matrix products, arithmetic and copies ran while one was open for 24% -> 32% of each run, Pallas kernels for 27% -> 31%
where the time goes in v3:
time: 1670 us
  Pallas kernels  563 us (34%)
  matrix products  439 us (26%)
  waiting for transfers between devices  300 us (18%)
  blocking collectives  190 us (11%)
  other arithmetic  95.5 us (6%)
  local copies, waits for them, and re-layouts  39.1 us (2%)
  starting transfers between devices  26.3 us (2%)
    pallas_call x2, Pallas kernels, attn_bwd(): pl.pallas_call(functools.partial(attn_bwd_kernel, z, per, head, blk), nam...  289 us
    dot_general x12, matrix products, dot(): return lax.dot_general(a, b, dims, preferred_element_type=F32)  271 us
    all_gather x8, waiting for transfers between devices, gather(): return lax.all_gather(arr, 'sp', axis=axis, tiled=True)  224 us
    all_gather x1, blocking collectives, gather(): return lax.all_gather(arr, 'sp', axis=axis, tiled=True)  165 us
    pallas_call x2, Pallas kernels, attn_fwd(): pl.pallas_call(functools.partial(attn_fwd_kernel, z, per, head, blk), nam...  143 us
    dot_general x6, matrix products, back(): jnp.einsum('gtn,dgn->td', flat, w.reshape(width, group, -1), preferred_el...  121 us
    all_to_all x6, waiting for transfers between devices, exchange(): lax.all_to_all(arr.reshape(group, -1, arr.shape[1]), 'sp', 0, 0, tiled=True)  74.9 us
    pallas_call x3, Pallas kernels, place(): pl.pallas_call(copy_kernel, name='place', grid=(x.shape[0] // rows,), in_...  69.5 us
  transfers between devices with their start and end apart: 15, of which 6 were waited for; matrix products, arithmetic and copies ran while one was open for 32% of the time, Pallas kernels for 31%

profile of v3, /device:TPU:0, one launch (start us, length us, event | category | flops | bytes accessed | tf_op | source)
XLA Modules:
  0.0 1667.1 jit_solution(9898537976616341034)
XLA Ops:
  10.4 4.6 slice_bitcast_fusion.1
  15.5 3.3 fusion.26
  23.0 5.8 fusion.27
  28.8 23.7 %convolution_convert_fusion.2 = bf16[512,4096]{1,0:T(8,128)(2,1)S(1)} fusion(bf16[512,3840]{1,0:T(8,128)(2,1)} %fusion.27, bf16[3840,4096]{1,0:T(8,128)(2,1)} %param.14), kind=kOutput, calls=%fused_computation.103 | convolution fusion | flops 16108224512 | bytes 39583744 | tf_op jit(solution)/shard_map/dot_general | solution.py:23
  54.6 12.1 convolution_convert_fusion.4
  66.8 8.5 convolution_convert_fusion.3
  75.7 4.4 maximum_bitcast_fusion
  80.1 5.2 all-to-all-start
  85.4 4.2 constant_dynamic-slice_fusion.2
  89.6 3.7 constant_dynamic-slice_fusion
  93.4 165.0 %all_gather.28 = s32[8192]{0:T(1024)S(1)} all-gather(s32[1024]{0:T(1024)S(1)} %copy-done.29), channel_id=1, replica_groups=mesh['dp'=1,'sp'=8] {'sp'}, dimensions={0}, use_global_device_ids=true | all-gather | bytes 36864 | tf_op jit(solution)/shard_map/all_gather | solution.py:346
  258.4 18.2 %multiply_sine_fusion = (f32[8192,128]{1,0:T(8,128)}, f32[8192,128]{1,0:T(8,128)}) fusion(f32[128]{0:T(128)S(1)} %multiply_power_fusion, f32[8192]{0:T(1024)S(1)} %convert_multiply_fusion.24), kind=kLoop, calls=%fused_computation.99 | loop fusion | flops 1048576 | bytes 8421888 | tf_op jit(solution)/shard_map/sin | solution.py:43
  276.6 39.3 %fusion.54.x_ref = bf16[4096,1024]{1,0:T(8,128)(2,1)} fusion(bf16[4096,3840]{1,0:T(8,128)(2,1)} %all-gather.9.cloned.1.call-done, bf16[3840,256]{1,0:T(8,128)(2,1)S(1)} %get-tuple-element.148, bf16[3840,256]{1,0:T(8,128)(2,1)} %get-tuple-element.149, bf16[3840,512]{1,0:T(8,128)(2,1)} %constant_dynamic-slice_fusion.2), kind=kOutput, calls=%fused_computation.98 | convolution fusion | flops 32240041984 | bytes 47710208 | tf_op jit(solution)/shard_map/dot_general | solution.py:23
  315.9 10.9 rope_fwd.2
  326.7 10.9 rope_fwd.3
  337.6 67.2 %attn_fwd.2 = (bf16[4096,512]{1,0:T(8,128)(2,1)}, f32[2,4096]{1,0:T(2,128)}) custom-call(bf16[4096,512]{1,0:T(8,128)(2,1)} %get-tuple-element.66.q_ref, bf16[8192,256]{1,0:T(8,128)(2,1)} %get-tuple-element.72.k_ref, bf16[8192,256]{1,0:T(8,128)(2,1)} %get-tuple-element.73.v_ref), custom_call_target="tpu_custom_call" | custom-call | flops 36507222016 | bytes 16777216 | tf_op jit(solution)/shard_map/attn_fwd/pallas_call | solution.py:211
  404.8 3.6 all-to-all-start.1
  408.5 4.4 slice_bitcast_fusion
  412.8 76.1 %attn_fwd.3 = (bf16[4096,512]{1,0:T(8,128)(2,1)}, f32[2,4096]{1,0:T(2,128)}) custom-call(bf16[4096,512]{1,0:T(8,128)(2,1)} %get-tuple-element.75.q_ref, bf16[8192,256]{1,0:T(8,128)(2,1)} %get-tuple-element.72.k_ref, bf16[8192,256]{1,0:T(8,128)(2,1)} %get-tuple-element.73.v_ref), custom_call_target="tpu_custom_call" | custom-call | flops 36507222016 | bytes 16777216 | tf_op jit(solution)/shard_map/attn_fwd/pallas_call | solution.py:211
  488.9 14.0 all-to-all-done.1
  502.9 3.3 all-to-all-start.2
  506.2 22.3 %fusion.36 = (f32[512]{0:T(512)S(1)}, bf16[512,3840]{1,0:T(8,128)(2,1)S(1)}) fusion(bf16[8,512,512]{2,1,0:T(8,128)(2,1)} %all-to-all-done.1, bf16[8,512,3840]{2,1,0:T(8,128)(2,1)} %bitcast.147), kind=kOutput, calls=%fused_computation.69 | convolution fusion | flops 16113991680 | bytes 39585792 | tf_op jit(solution)/shard_map/gtn,gnd->td/dot_general | solution.py:399
  528.6 8.2 fusion.35
  536.9 3.9 fusion.30
  540.7 30.7 %all-to-all-done.2 = bf16[8,512,512]{2,1,0:T(8,128)(2,1)} async-done(((bf16[8,512,512]{2,1,0:T(8,128)(2,1)}), bf16[8,512,512]{2,1,0:T(8,128)(2,1)}, u32[]{:S(2)}, u32[]{:S(2)}) %all-to-all-start.2) | async-done | bytes 4194336 | tf_op jit(solution)/shard_map/all_to_all | solution.py:349
  571.5 25.0 %fusion.38 = (f32[512]{0:T(512)S(1)}, bf16[512,3840]{1,0:T(8,128)(2,1)S(1)}) fusion(bf16[8,512,512]{2,1,0:T(8,128)(2,1)} %all-to-all-done.2, bf16[8,512,3840]{2,1,0:T(8,128)(2,1)} %bitcast.148), kind=kOutput, calls=%fused_computation.71 | convolution fusion | flops 16113991680 | bytes 39585792 | tf_op jit(solution)/shard_map/gtn,gnd->td/dot_general | solution.py:399
  596.5 5.3 fusion.32
  601.8 6.0 fusion.33
  607.8 109.1 %all-gather.15.cloned.1.call-done = bf16[4096,3840]{1,0:T(8,128)(2,1)} async-done(((bf16[512,3840]{1,0:T(8,128)(2,1)}), bf16[4096,3840]{1,0:T(8,128)(2,1)}) %all-gather.15.cloned.1.call-update) | async-done | bytes 31457296 | tf_op jit(solution)/shard_map/all_gather | solution.py:346
  717.0 23.5 %convolution_convert_fusion.do_ref = bf16[4096,512]{1,0:T(8,128)(2,1)} fusion(bf16[4096,3840]{1,0:T(8,128)(2,1)} %all-gather.15.cloned.1.call-done, bf16[4096,3840]{1,0:T(8,128)(2,1)} %param.17, s32[]{:T(128)S(6)} %select_n.8), kind=kOutput, calls=%fused_computation.101 | convolution fusion | flops 16108224512 | bytes 39583748 | tf_op jit(solution)/shard_map/dot_general | solution.py:23
  740.4 134.6 %attn_bwd.2 = (bf16[4096,512]{1,0:T(8,128)(2,1)}, f32[8192,256]{1,0:T(8,128)}, f32[8192,256]{1,0:T(8,128)}) custom-call(bf16[4096,512]{1,0:T(8,128)(2,1)} %get-tuple-element.66.q_ref, bf16[4096,512]{1,0:T(8,128)(2,1)} %convolution_convert_fusion.do_ref, bf16[4096,512]{1,0:T(8,128)(2,1)} %get-tuple-element.74.o_ref, f32[2,4096]{1,0:T(2,128)} %get-tuple-element.83.lse_ref, ...), custom_call_target="tpu_custom_call" | custom-call | flops 91268055040 | bytes 50331648 | tf_op jit(solution)/shard_map/attn_bwd/pallas_call | solution.py:327
  875.0 10.6 rope_bwd.4
  888.9 24.1 %fusion.75 = f32[512,3840]{1,0:T(8,128)} fusion(bf16[4096,512]{1,0:T(8,128)(2,1)} %get-tuple-element.74.o_ref, bf16[4096,3840]{1,0:T(8,128)(2,1)} %all-gather.15.cloned.1.call-done), kind=kOutput, calls=%fused_computation.142 | convolution fusion | flops 16106127360 | bytes 43515904 | tf_op jit(solution)/shard_map/dot_general | solution.py:23
  913.1 24.2 %add_convert_fusion.2 = bf16[512,3840]{1,0:T(8,128)(2,1)} fusion(f32[512,3840]{1,0:T(8,128)} %fusion.75, bf16[4096,512]{1,0:T(8,128)(2,1)} %get-tuple-element.78.o_ref, bf16[4096,3840]{1,0:T(8,128)(2,1)} %all-gather.13.cloned.1.call-done), kind=kOutput, calls=%fused_computation.97 | convolution fusion | flops 16110059520 | bytes 47448064 | tf_op jit(solution)/shard_map/dot_general | solution.py:23
  937.2 23.5 %convolution_convert_fusion.1.do_ref = bf16[4096,512]{1,0:T(8,128)(2,1)} fusion(bf16[4096,3840]{1,0:T(8,128)(2,1)} %all-gather.13.cloned.1.call-done, bf16[4096,3840]{1,0:T(8,128)(2,1)} %param.17, s32[]{:T(128)S(6)} %select_n.8), kind=kOutput, calls=%fused_computation.102 | convolution fusion | flops 16108224512 | bytes 39583748 | tf_op jit(solution)/shard_map/dot_general | solution.py:23
  960.8 154.7 %attn_bwd.3 = (bf16[4096,512]{1,0:T(8,128)(2,1)}, bf16[8192,256]{1,0:T(8,128)(2,1)}, bf16[8192,256]{1,0:T(8,128)(2,1)}) custom-call(bf16[4096,512]{1,0:T(8,128)(2,1)} %get-tuple-element.75.q_ref, bf16[4096,512]{1,0:T(8,128)(2,1)} %convolution_convert_fusion.1.do_ref, bf16[4096,512]{1,0:T(8,128)(2,1)} %get-tuple-element.78.o_ref, ...), custom_call_target="tpu_custom_call" | custom-call | flops 91268055040 | bytes 50331648 | tf_op jit(solution)/shard_map/attn_bwd/pallas_call | solution.py:327
  1115.5 10.5 rope_bwd.5
  1126.0 3.8 all-to-all-start.4
  1129.8 21.4 %fusion.76 = f32[3840,512]{1,0:T(8,128)S(1)} fusion(bf16[4096,3840]{1,0:T(8,128)(2,1)} %all-gather.9.cloned.1.call-done, bf16[4096,512]{1,0:T(8,128)(2,1)} %get-tuple-element.85), kind=kOutput, calls=%fused_computation.143 | convolution fusion | flops 16106127360 | bytes 43515904 | tf_op jit(solution)/shard_map/dot_general | solution.py:23
  1151.2 22.5 %add_convert_fusion.1 = bf16[3840,512]{1,0:T(8,128)(2,1)} fusion(f32[3840,512]{1,0:T(8,128)S(1)} %fusion.76, bf16[4096,3840]{1,0:T(8,128)(2,1)} %all-gather.11.cloned.1.call-done, bf16[4096,512]{1,0:T(8,128)(2,1)S(1)} %copy-done.5), kind=kOutput, calls=%fused_computation.96 | convolution fusion | flops 16110059520 | bytes 47448064 | tf_op jit(solution)/shard_map/dot_general | solution.py:23
  1173.7 5.2 all-to-all-done.4
  1178.9 9.0 rope_bwd.6
  1187.9 3.3 all-to-all-start.5
  1191.3 24.0 %fusion.77 = f32[3840,512]{1,0:T(8,128)} fusion(bf16[4096,3840]{1,0:T(8,128)(2,1)} %all-gather.9.cloned.1.call-done, bf16[4096,512]{1,0:T(8,128)(2,1)} %get-tuple-element.101), kind=kOutput, calls=%fused_computation.144 | convolution fusion | flops 16106127360 | bytes 43515904 | tf_op jit(solution)/shard_map/dot_general | solution.py:23
  1215.3 9.1 rope_bwd.7
  1224.3 24.1 %add_convert_fusion = bf16[3840,512]{1,0:T(8,128)(2,1)} fusion(f32[3840,512]{1,0:T(8,128)} %fusion.77, bf16[4096,3840]{1,0:T(8,128)(2,1)} %all-gather.11.cloned.1.call-done, bf16[4096,512]{1,0:T(8,128)(2,1)} %get-tuple-element.105), kind=kOutput, calls=%fused_computation.95 | convolution fusion | flops 16110059520 | bytes 47448064 | tf_op jit(solution)/shard_map/dot_general | solution.py:23
  1248.5 4.3 fusion.74
  1255.5 24.9 %fusion.2 = f32[512,3840,1]{1,0,2:T(8,128)} fusion(bf16[8,512,512]{2,1,0:T(8,128)(2,1)} %all-to-all-done.3, bf16[480,8,8,512]{3,2,1,0:T(8,128)(2,1)} %bitcast.131), kind=kOutput, calls=%fused_computation.2 | convolution fusion | flops 16106127360 | bytes 43515904 | tf_op jit(solution)/shard_map/gtn,dgn->td/dot_general | solution.py:442
  1280.4 3.5 all-to-all-start.6
  1283.9 25.2 %fusion = f32[512,3840,1]{1,0,2:T(8,128)} fusion(bf16[8,512,512]{2,1,0:T(8,128)(2,1)} %all-to-all-done.4, bf16[480,8,8,512]{3,2,1,0:T(8,128)(2,1)} %bitcast.132), kind=kOutput, calls=%fused_computation | convolution fusion | flops 16106127360 | bytes 43515904 | tf_op jit(solution)/shard_map/gtn,dgn->td/dot_general | solution.py:442
  1309.1 26.0 %place.3 = bf16[4096,3840]{1,0:T(8,128)(2,1)} custom-call(bf16[4096,3840]{1,0:T(8,128)(2,1)} %all-gather.17.cloned.1.call-done.x_ref), custom_call_target="tpu_custom_call" | custom-call | flops 251658240 | bytes 62914560 | tf_op jit(solution)/shard_map/place/pallas_call | solution.py:135
  1335.1 14.8 fusion.8
  1350.0 25.1 %all-to-all-done.6 = bf16[8,512,512]{2,1,0:T(8,128)(2,1)} async-done(((bf16[8,512,512]{2,1,0:T(8,128)(2,1)}), bf16[8,512,512]{2,1,0:T(8,128)(2,1)}, u32[]{:S(2)}, u32[]{:S(2)}) %all-to-all-start.6) | async-done | bytes 4194336 | tf_op jit(solution)/shard_map/all_to_all | solution.py:349
  1375.1 14.9 fusion.6
  1390.0 18.4 %fusion.52 = bf16[512,3840]{1,0:T(8,128)(2,1)} fusion(f32[512,3840,1]{1,0,2:T(8,128)} %fusion.6, f32[512,3840,1]{1,0,2:T(8,128)} %fusion, bf16[480,8,8,256]{3,2,1,0:T(8,128)(2,1)} %bitcast.137, bf16[8,512,512]{2,1,0:T(8,128)(2,1)} %all-to-all-done.6), kind=kOutput, calls=%fused_computation.88 | convolution fusion | flops 8058961920 | bytes 37486592 | tf_op jit(solution)/shard_map/gtn,dgn->td/dot_general | solution.py:442
  1408.5 22.3 %fusion.28 = (f32[3840]{0:T(1024)S(1)}, f32[512]{0:T(512)S(1)}, f32[512]{0:T(512)S(1)}, f32[3840]{0:T(1024)S(1)}, bf16[512,3840]{1,0:T(8,128)(2,1)}) fusion(f32[512]{0:T(512)S(1)} %copy-done.20, bf16[1,1024,3840]{2,1,0:T(8,128)(2,1)} %param.11, f32[3840]{0:T(1024)S(1)} %copy-done.9, bf16[512,3840]{1,0:T(8,128)(2,1)} %fusion.52, f32[512]{0:T(512)S(1)} %copy-done.22, ...), kind=kOutput, calls=%fused_computation.61 | convolution fusion | flops 8090409984 | bytes 49337344 | tf_op jit(solution)/shard_map/gtn,dgn->td/dot_general | solution.py:442
  1430.8 24.7 %all-reduce = (f32[3840]{0:T(1024)}, f32[3840]{0:T(1024)}, f32[256]{0:T(256)}, f32[256]{0:T(256)}) all-reduce(f32[3840]{0:T(1024)S(1)} %add.128, f32[3840]{0:T(1024)S(1)} %copy-done.12, f32[256]{0:T(256)S(1)} %copy-done.30, f32[256]{0:T(256)S(1)} %add_reduce_fusion), channel_id=1, replica_groups=mesh['dp'=1,'sp'=8] {'sp'}, use_global_device_ids=true, to_apply=%region_10.0 | all-reduce | flops 8192 | bytes 65536 | tf_op jit(solution)/shard_map/psum | solution.py:454
  1455.5 17.3 %fusion.34 = (bf16[512,3840]{1,0:T(8,128)(2,1)}, bf16[512,3840]{1,0:T(8,128)(2,1)}, bf16[512,3840]{1,0:T(8,128)(2,1)}) fusion(bf16[512,3840]{1,0:T(8,128)(2,1)} %get-tuple-element.147, f32[512]{0:T(512)S(1)} %multiply_multiply_fusion.1, f32[3840]{0:T(1024)S(1)} %copy-done.9, f32[512]{0:T(512)S(1)} %copy-done.20, bf16[1,1024,3840]{2,1,0:T(8,128)(2,1)} %param.12, ...), kind=kLoop, calls=%fused_computation.67 | loop fusion | flops 49152000 | bytes 39362560 | tf_op jit(solution)/shard_map/convert_element_type | solution.py:451
  1472.8 8.5 maximum_bitcast_fusion.2
  1481.2 7.3 maximum_bitcast_fusion.1
  1488.6 17.1 %place.5 = bf16[3840,2048]{1,0:T(8,128)(2,1)} custom-call(bf16[3840,2048]{1,0:T(8,128)(2,1)} %all-gather.21.cloned.1.call-done.x_ref), custom_call_target="tpu_custom_call" | custom-call | flops 125829120 | bytes 31457280 | tf_op jit(solution)/shard_map/place/pallas_call | solution.py:135
  1505.7 114.5 %all-gather.19.cloned.1.call-done.x_ref = bf16[3840,4096]{1,0:T(8,128)(2,1)} async-done(((bf16[3840,512]{1,0:T(8,128)(2,1)}), bf16[3840,4096]{1,0:T(8,128)(2,1)}) %all-gather.19.cloned.1.call-update) | async-done | bytes 31457296 | tf_op jit(solution)/shard_map/all_gather | solution.py:346
  1620.1 26.5 %place.4 = bf16[3840,4096]{1,0:T(8,128)(2,1)} custom-call(bf16[3840,4096]{1,0:T(8,128)(2,1)} %all-gather.19.cloned.1.call-done.x_ref), custom_call_target="tpu_custom_call" | custom-call | flops 251658240 | bytes 62914560 | tf_op jit(solution)/shard_map/place/pallas_call | solution.py:135
  1646.6 13.5 copy.84
  (122 shorter events, 16.9 us)
Async XLA Ops:
  7.2 7.7 copy-start.23
  7.2 269.4 %all-gather.9.cloned.1.call-start = ((), (), s32[]{:S(2)}) async-start(), calls=%async_computation.7 | async-start | bytes 35389440 | tf_op jit(solution)/shard_map/all_gather | solution.py:346
  7.2 8.3 copy-start.3
  10.3 4.6 copy-start.15
  14.9 7.5 copy-start.8
  15.0 0.6 copy-start.19
  21.9 0.6 copy-start.17
  22.5 0.6 copy-start.21
  52.5 2.1 copy-start.4
  52.5 14.2 slice-start.2
  54.6 12.1 slice-start.3
  54.6 12.1 slice-start.4
  54.6 12.1 slice-start.5
  80.1 246.6 %all-to-all-start = ((bf16[8,512,1024]{2,1,0:T(8,128)(2,1)}), bf16[8,512,1024]{2,1,0:T(8,128)(2,1)}, u32[]{:S(2)}, u32[]{:S(2)}) async-start(bf16[8,512,1024]{2,1,0:T(8,128)(2,1)} %maximum_bitcast_fusion), calls=%async_computation | async-start | bytes 16777216 | tf_op jit(solution)/shard_map/all_to_all | solution.py:380
  85.3 486.1 %all-gather.11.cloned.1.call-start = ((), (), s32[]{:S(2)}) async-start(), calls=%async_computation.8 | async-start | bytes 35389440 | tf_op jit(solution)/shard_map/all_gather | solution.py:346
  85.4 8.0 copy-start.29
  404.8 8.0 copy-start.24
  404.8 98.0 %all-to-all-start.1 = ((bf16[8,512,512]{2,1,0:T(8,128)(2,1)}), bf16[8,512,512]{2,1,0:T(8,128)(2,1)}, u32[]{:S(2)}, u32[]{:S(2)}) async-start(bf16[8,512,512]{2,1,0:T(8,128)(2,1)} %bitcast.123), calls=%async_computation.1 | async-start | bytes 8388608 | tf_op jit(solution)/shard_map/all_to_all | solution.py:349
  412.8 189.0 %copy-start.6 = (f32[3840]{0:T(1024)}, f32[3840]{0:T(1024)S(1)}, u32[]{:S(2)}) copy-start(f32[3840]{0:T(1024)S(1)} %broadcast_add_fusion) | copy-start | bytes 46084
  502.9 68.5 %all-to-all-start.2 = ((bf16[8,512,512]{2,1,0:T(8,128)(2,1)}), bf16[8,512,512]{2,1,0:T(8,128)(2,1)}, u32[]{:S(2)}, u32[]{:S(2)}) async-start(bf16[8,512,512]{2,1,0:T(8,128)(2,1)} %bitcast.122), calls=%async_computation.2 | async-start | bytes 8388608 | tf_op jit(solution)/shard_map/all_to_all | solution.py:349
  506.2 210.8 %all-gather.15.cloned.1.call-start = ((), (), s32[]{:S(2)}) async-start(), calls=%async_computation.10 | async-start | bytes 35389440 | tf_op jit(solution)/shard_map/all_gather | solution.py:346
  506.2 30.6 %slice-start = ((s8[7864320]{0:T(1024)(128)(4,1)}), s8[4194304]{0:T(1024)(128)(4,1)S(1)}, s32[]{:S(2)}) async-start(s8[7864320]{0:T(1024)(128)(4,1)} %bitcast.119), calls=%async_computation.15 | async-start | bytes 8388608
  506.2 30.6 %slice-start.1 = ((s8[7864320]{0:T(1024)(128)(4,1)}), s8[3670016]{0:T(1024)(128)(4,1)S(1)}, s32[]{:S(2)}) async-start(s8[7864320]{0:T(1024)(128)(4,1)} %bitcast.119), calls=%async_computation.16 | async-start | bytes 7340032
  528.6 8.3 copy-start.2
  528.6 8.2 copy-start.13
  571.4 341.6 %all-gather.13.cloned.1.call-start = ((), (), s32[]{:S(2)}) async-start(), calls=%async_computation.9 | async-start | bytes 35389440 | tf_op jit(solution)/shard_map/all_gather | solution.py:346
  571.5 25.0 %copy-start.1 = (bf16[512,3840]{1,0:T(8,128)(2,1)S(1)}, bf16[512,3840]{1,0:T(8,128)(2,1)}, u32[]{:S(2)}) copy-start(bf16[512,3840]{1,0:T(8,128)(2,1)} %slice_bitcast_fusion) | copy-start | bytes 11796484
  596.5 5.3 copy-start
  885.6 75.2 %all-to-all-start.3 = ((bf16[8,512,512]{2,1,0:T(8,128)(2,1)}), bf16[8,512,512]{2,1,0:T(8,128)(2,1)}, u32[]{:S(2)}, u32[]{:S(2)}) async-start(bf16[8,512,512]{2,1,0:T(8,128)(2,1)} %bitcast.125), calls=%async_computation.3 | async-start | bytes 8388608 | tf_op jit(solution)/shard_map/all_to_all | solution.py:349
  888.9 290.1 %all-gather.17.cloned.1.call-start = ((), (), s32[]{:S(2)}) async-start(), calls=%async_computation.11 | async-start | bytes 35389440 | tf_op jit(solution)/shard_map/all_gather | solution.py:346
  1126.0 52.9 %all-to-all-start.4 = ((bf16[8,512,512]{2,1,0:T(8,128)(2,1)}), bf16[8,512,512]{2,1,0:T(8,128)(2,1)}, u32[]{:S(2)}, u32[]{:S(2)}) async-start(bf16[8,512,512]{2,1,0:T(8,128)(2,1)} %bitcast.127), calls=%async_computation.4 | async-start | bytes 8388608 | tf_op jit(solution)/shard_map/all_to_all | solution.py:349
  1129.8 21.4 %copy-start.5 = (bf16[4096,512]{1,0:T(8,128)(2,1)S(1)}, bf16[4096,512]{1,0:T(8,128)(2,1)}, u32[]{:S(2)}) copy-start(bf16[4096,512]{1,0:T(8,128)(2,1)} %get-tuple-element.95) | copy-start | bytes 12582916
  1187.9 60.6 %all-to-all-start.5 = ((bf16[8,512,512]{2,1,0:T(8,128)(2,1)}), bf16[8,512,512]{2,1,0:T(8,128)(2,1)}, u32[]{:S(2)}, u32[]{:S(2)}) async-start(bf16[8,512,512]{2,1,0:T(8,128)(2,1)} %bitcast.126), calls=%async_computation.5 | async-start | bytes 8388608 | tf_op jit(solution)/shard_map/all_to_all | solution.py:349
  1191.2 297.4 %all-gather.23.cloned.1.call-start = ((), (), s32[]{:S(2)}) async-start(), calls=%async_computation.14 | async-start | bytes 17694720 | tf_op jit(solution)/shard_map/all_gather | solution.py:346
  1248.4 5.8 copy-start.10
  1248.4 5.8 copy-start.11
  1248.4 6.5 copy-start.25
  1248.5 6.5 copy-start.26
  1252.8 235.8 %all-gather.21.cloned.1.call-start = ((), (), s32[]{:S(2)}) async-start(), calls=%async_computation.13 | async-start | bytes 17694720 | tf_op jit(solution)/shard_map/all_gather | solution.py:346
  1253.5 366.6 %all-gather.19.cloned.1.call-start = ((), (), s32[]{:S(2)}) async-start(), calls=%async_computation.12 | async-start | bytes 35389440 | tf_op jit(solution)/shard_map/all_gather | solution.py:346
  1280.4 94.7 %all-to-all-start.6 = ((bf16[8,512,512]{2,1,0:T(8,128)(2,1)}), bf16[8,512,512]{2,1,0:T(8,128)(2,1)}, u32[]{:S(2)}, u32[]{:S(2)}) async-start(bf16[8,512,512]{2,1,0:T(8,128)(2,1)} %bitcast.124), calls=%async_computation.6 | async-start | bytes 8388608 | tf_op jit(solution)/shard_map/all_to_all | solution.py:349
  1309.1 26.0 %copy-start.27 = (f32[8,256]{1,0:T(8,128)S(1)}, f32[8,256]{1,0:T(8,128)}, u32[]{:S(2)}) copy-start(f32[8,256]{1,0:T(8,128)} %get-tuple-element.111) | copy-start | bytes 24580
  1309.1 26.0 %copy-start.28 = (f32[8,256]{1,0:T(8,128)S(1)}, f32[8,256]{1,0:T(8,128)}, u32[]{:S(2)}) copy-start(f32[8,256]{1,0:T(8,128)} %get-tuple-element.112) | copy-start | bytes 24580
  1390.0 18.4 %copy-start.9 = (f32[3840]{0:T(1024)S(1)}, f32[3840]{0:T(1024)}, u32[]{:S(2)}) copy-start(f32[3840]{0:T(1024)} %copy-done.8) | copy-start | bytes 46084
  1390.0 18.4 %copy-start.20 = (f32[512]{0:T(512)S(1)}, f32[512]{0:T(512)}, u32[]{:S(2)}) copy-start(f32[512]{0:T(512)} %copy-done.19) | copy-start | bytes 6148
  1390.0 18.4 %copy-start.22 = (f32[512]{0:T(512)S(1)}, f32[512]{0:T(512)}, u32[]{:S(2)}) copy-start(f32[512]{0:T(512)} %copy-done.21) | copy-start | bytes 6148
  1408.4 22.3 %copy-start.12 = (f32[3840]{0:T(1024)S(1)}, f32[3840]{0:T(1024)}, u32[]{:S(2)}) copy-start(f32[3840]{0:T(1024)} %add.129) | copy-start | bytes 46084
  1408.4 22.3 %copy-start.30 = (f32[256]{0:T(256)S(1)}, f32[256]{0:T(256)}, u32[]{:S(2)}) copy-start(f32[256]{0:T(256)} %add_reduce_fusion.1) | copy-start | bytes 3076
  1408.4 47.0 %copy-start.18 = (f32[512]{0:T(512)S(1)}, f32[512]{0:T(512)}, u32[]{:S(2)}) copy-start(f32[512]{0:T(512)} %copy-done.17) | copy-start | bytes 6148
  1408.5 47.0 %copy-start.16 = (f32[512]{0:T(512)S(1)}, f32[512]{0:T(512)}, u32[]{:S(2)}) copy-start(f32[512]{0:T(512)} %copy-done.15) | copy-start | bytes 6148
  1408.5 47.0 %copy-start.7 = (f32[3840]{0:T(1024)S(1)}, f32[3840]{0:T(1024)}, u32[]{:S(2)}) copy-start(f32[3840]{0:T(1024)} %copy-done.6) | copy-start | bytes 46084
  1408.5 47.0 %copy-start.14 = (f32[512]{0:T(512)S(1)}, f32[512]{0:T(512)}, u32[]{:S(2)}) copy-start(f32[512]{0:T(512)} %copy-done.13) | copy-start | bytes 6148
Sparse Core Ops, SparseCore 0:
  19.0 223.4 all-gather.8
  337.7 218.6 all-gather.10
  571.5 145.3 all-gather.14
  718.6 146.2 all-gather.12
  960.9 147.5 all-gather.16
  1252.9 125.3 all-gather.22
  1380.1 85.6 all-gather.20
  1467.6 152.4 all-gather.18

commit v4 on v3

--- a/solution.py
+++ b/solution.py
@@ -44,7 +44,7 @@
 
 
 def rope_fwd_kernel(n_q, n_k, head, x_ref, cos_ref, sin_ref, wq_ref, wk_ref, *refs):
-    q_ref, k_ref, v_ref = refs[-3:]
+    q_ref, k_ref, v_ref, kt_ref, vt_ref = refs[-5:]
     half = head // 2
     cosines = cos_ref[...]
     sines = sin_ref[...]
@@ -57,6 +57,8 @@
         out_ref[:, at * head:at * head + half] = (first * cosines - second * sines).astype(BF16)
         out_ref[:, at * head + half:(at + 1) * head] = (second * cosines + first * sines).astype(BF16)
     v_ref[...] = x_ref[:, (n_q + n_k) * head:]
+    kt_ref[...] = k_ref[...].T
+    vt_ref[...] = v_ref[...].T
 
 
 def rope_fwd(z, qkv, cosines, sines, w_qn, w_kn, n_q, n_k, head, kv_so_far):
@@ -67,14 +69,16 @@
     placed = lambda width: pl.BlockSpec((blk, width), lambda i: (2 * i + z, 0))
     whole = pl.BlockSpec((1, head), lambda i: (0, 0))
     kv_shape = jax.ShapeDtypeStruct((seq, n_k * head), BF16)
+    t_shape = jax.ShapeDtypeStruct((n_k * head, seq), BF16)
+    t_placed = pl.BlockSpec((n_k * head, blk), lambda i: (0, 2 * i + z))
     return pl.pallas_call(
         functools.partial(rope_fwd_kernel, n_q, n_k, head),
         name='rope_fwd',
         grid=(qkv.shape[0] // blk,),
         in_specs=[row((n_q + 2 * n_k) * head), placed(half), placed(half), whole, whole] + [pl.BlockSpec(memory_space=pl.ANY)] * len(kv_so_far),
-        out_specs=[row(n_q * head), placed(n_k * head), placed(n_k * head)],
-        out_shape=[jax.ShapeDtypeStruct((qkv.shape[0], n_q * head), BF16), kv_shape, kv_shape],
-        input_output_aliases={5: 1, 6: 2} if kv_so_far else {},
+        out_specs=[row(n_q * head), placed(n_k * head), placed(n_k * head), t_placed, t_placed],
+        out_shape=[jax.ShapeDtypeStruct((qkv.shape[0], n_q * head), BF16), kv_shape, kv_shape, t_shape, t_shape],
+        input_output_aliases={5: 1, 6: 2, 7: 3, 8: 4} if kv_so_far else {},
         compiler_params=pltpu.CompilerParams(dimension_semantics=('arbitrary',)),
         cost_estimate=pl.CostEstimate(flops=qkv.size * 40, bytes_accessed=qkv.size * 4 + seq * head * 2, transcendentals=0),
     )(qkv, cosines, sines, w_qn, w_kn, *kv_so_far)
@@ -144,10 +148,34 @@
     )(x)
 
 
+def split_kernel(x_ref, *refs):
+    a_ref, b_ref = refs[-2:]
+    a_ref[...] = x_ref[:, :a_ref.shape[1]]
+    b_ref[...] = x_ref[:, a_ref.shape[1]:]
+
+
+def split_pairs(x, lanes, out_rows, first_row, so_far):
+    rows = x.shape[0] // 3
+    parts = x.shape[1] // (2 * lanes)
+    out = pl.BlockSpec((rows, lanes), lambda i, g: (i + first_row // rows, g))
+    shape = jax.ShapeDtypeStruct((out_rows, parts * lanes), x.dtype)
+    return pl.pallas_call(
+        split_kernel,
+        name='split_pairs',
+        grid=(3, parts),
+        in_specs=[pl.BlockSpec((rows, 2 * lanes), lambda i, g: (i, g))] + [pl.BlockSpec(memory_space=pl.ANY)] * len(so_far),
+        out_specs=[out, out],
+        out_shape=[shape, shape],
+        input_output_aliases={1: 0, 2: 1} if so_far else {},
+        compiler_params=pltpu.CompilerParams(dimension_semantics=('arbitrary', 'arbitrary')),
+        cost_estimate=pl.CostEstimate(flops=x.size * 16, bytes_accessed=4 * x.size, transcendentals=0),
+    )(x, *so_far)
+
+
 BLK = 512
 
 
-def attn_fwd_kernel(z, per, head, blk, q_ref, k_ref, v_ref, o_ref, lse_ref, m_sc, l_sc, acc_sc, s_even, s_odd):
+def attn_fwd_kernel(z, per, head, blk, q_ref, k_ref, vt_ref, o_ref, lse_ref, m_sc, l_sc, acc_sc, s_even, s_odd):
     i = pl.program_id(0)
     c = LOG2E * head ** -0.5
     m_sc[...] = jnp.full_like(m_sc, -jnp.inf)
@@ -157,27 +185,24 @@
     def scores(j, s_ref):
         k = k_ref[pl.ds(pl.multiple_of(j * blk, blk), blk), :]
         for h in range(per):
-            s_ref[h] = dot(q_ref[:, h * head:(h + 1) * head], k, NT)
+            s_ref[h] = dot(k, q_ref[:, h * head:(h + 1) * head], NT)
 
     def update(j, s_ref, masked):
-        v = v_ref[pl.ds(pl.multiple_of(j * blk, blk), blk), :]
+        v_t = vt_ref[:, pl.ds(pl.multiple_of(j * blk, blk), blk)]
         for h in range(per):
             s = s_ref[h]
             if masked:
-                rows = lax.broadcasted_iota(jnp.int32, s.shape, 0)
-                cols = lax.broadcasted_iota(jnp.int32, s.shape, 1)
-                s = jnp.where(rows >= cols, s, NEG_BIG)
+                kv_ids = lax.broadcasted_iota(jnp.int32, s.shape, 0)
+                q_ids = lax.broadcasted_iota(jnp.int32, s.shape, 1)
+                s = jnp.where(q_ids >= kv_ids, s, NEG_BIG)
             t = s * c
             m_prev = m_sc[h]
-            m_new = jnp.maximum(m_prev, jnp.max(t, axis=1, keepdims=True))
+            m_new = jnp.maximum(m_prev, jnp.max(t, axis=0, keepdims=True))
             m_sc[h] = m_new
-            p = jnp.exp2(t - jnp.tile(m_new, (1, blk // 128)))
+            p = jnp.exp2(t - m_new)
             alpha = jnp.exp2(m_prev - m_new)
-            part = p[:, :128]
-            for y in range(1, blk // 128):
-                part = part + p[:, y * 128:(y + 1) * 128]
-            l_sc[h] = l_sc[h] * alpha + part
-            acc_sc[h] = acc_sc[h] * jnp.tile(alpha, (1, head // 128)) + dot(p.astype(BF16), v, NN)
+            l_sc[h] = l_sc[h] * alpha + jnp.sum(p.reshape(blk // 8, 8, blk), axis=0)
+            acc_sc[h] = acc_sc[h] * alpha + dot(v_t, p.astype(BF16), NN)
 
     scores(0, s_even)
 
@@ -195,13 +220,12 @@
         update(2 * i, s_even, False)
         update(2 * i + 1, s_odd, True)
     for h in range(per):
-        total = jnp.sum(l_sc[h], axis=1, keepdims=True)
-        o_ref[:, h * head:(h + 1) * head] = (acc_sc[h] / total).astype(BF16)
-        lse = m_sc[h] + jnp.log2(jnp.broadcast_to(total, (blk, 128)))
-        lse_ref[h:h + 1, :] = lse.T[0:1, :]
-
-
-def attn_fwd(z, q, k, v, per, head):
+        total = jnp.sum(l_sc[h], axis=0, keepdims=True)
+        o_ref[:, h * head:(h + 1) * head] = (acc_sc[h] / total).T.astype(BF16)
+        lse_ref[h:h + 1, :] = m_sc[h] + jnp.log2(total)
+
+
+def attn_fwd(z, q, k, v_t, per, head):
     rows = q.shape[0]
     seq = k.shape[0]
     blk = BLK
@@ -212,17 +236,17 @@
         functools.partial(attn_fwd_kernel, z, per, head, blk),
         name='attn_fwd',
         grid=(rows // blk,),
-        in_specs=[row, whole, whole],
+        in_specs=[row, whole, pl.BlockSpec((head, seq), lambda i: (0, 0), pipeline_mode=pl.Buffered(1))],
         out_specs=[row, pl.BlockSpec((per, blk), lambda i: (0, i))],
         out_shape=[jax.ShapeDtypeStruct((rows, per * head), BF16), jax.ShapeDtypeStruct((per, rows), F32)],
-        scratch_shapes=[pltpu.VMEM((per, blk, 128), F32), pltpu.VMEM((per, blk, 128), F32), pltpu.VMEM((per, blk, head), F32),
+        scratch_shapes=[pltpu.VMEM((per, 1, blk), F32), pltpu.VMEM((per, 8, blk), F32), pltpu.VMEM((per, head, blk), F32),
                         pltpu.VMEM((per, blk, blk), F32), pltpu.VMEM((per, blk, blk), F32)],
         compiler_params=pltpu.CompilerParams(dimension_semantics=('arbitrary',), vmem_limit_bytes=VMEM_LIMIT),
         cost_estimate=pl.CostEstimate(flops=4 * pairs * head, bytes_accessed=rows * head * 4 * per + seq * head * 4, transcendentals=pairs),
-    )(q, k, v)
-
-
-def attn_bwd_kernel(z, per, head, blk, q_ref, do_ref, o_ref, lse_ref, k_ref, v_ref, *refs):
+    )(q, k, v_t)
+
+
+def attn_bwd_kernel(z, per, head, blk, q_ref, do_ref, o_ref, lse_ref, k_ref, v_ref, kt_ref, *refs):
     if z == 0:
         dq_ref, dk_ref, dv_ref, dk_acc, dv_acc, dq_acc, q_sc, do_sc, delta_sc, sems = refs
     else:
@@ -257,6 +281,7 @@
         at = pl.ds(pl.multiple_of(j * blk, blk), blk)
         k = k_ref[at, :]
         v = v_ref[at, :]
+        k_t = kt_ref[:, at]
         dvs = []
         dks = []
         dqs = []
@@ -274,15 +299,14 @@
             ds = (p * (dp - delta_sc[:, rows])).astype(BF16)
             dvs.append(dot(p.astype(BF16), d_out, NN))
             dks.append(dot(ds, q, NN))
-            dqs.append(dot(ds, k, TN))
+            dqs.append(dot(k_t, ds, NN))
         dv_acc[at, :] += functools.reduce(jnp.add, dvs)
         dk_acc[at, :] += functools.reduce(jnp.add, dks)
         for h in range(per):
-            rows = slice(h * blk, (h + 1) * blk)
             if diag:
-                dq_acc[rows, :] = dqs[h]
+                dq_acc[h] = dqs[h]
             else:
-                dq_acc[rows, :] += dqs[h]
+                dq_acc[h] += dqs[h]
 
     step(2 * i + z, True)
 
@@ -291,7 +315,7 @@
         step(j, False)
 
     for h in range(per):
-        dq_ref[:, h * head:(h + 1) * head] = (dq_acc[h * blk:(h + 1) * blk, :] * scale).astype(BF16)
+        dq_ref[:, h * head:(h + 1) * head] = (dq_acc[h] * scale).T.astype(BF16)
 
     @pl.when(i == last)
     def _():
@@ -309,7 +333,7 @@
                 dv_ref[at, :] = dv_acc[at, :].astype(BF16)
 
 
-def attn_bwd(z, q, d_out, o, lse, k, v, per, head, partial):
+def attn_bwd(z, q, d_out, o, lse, k, v, k_t, per, head, partial):
     rows = q.shape[0]
     seq = k.shape[0]
     blk = BLK
@@ -328,15 +352,16 @@
         functools.partial(attn_bwd_kernel, z, per, head, blk),
         name='attn_bwd',
         grid=(rows // blk,),
-        in_specs=[row, row, row, pl.BlockSpec((per, blk), lambda i: (0, i)), once(seq), once(seq)] + [anywhere] * len(partial),
+        in_specs=[row, row, row, pl.BlockSpec((per, blk), lambda i: (0, i)), once(seq), once(seq),
+                  pl.BlockSpec((head, seq), lambda i: (0, 0), pipeline_mode=pl.Buffered(1))] + [anywhere] * len(partial),
         out_specs=out_specs,
         out_shape=out_shape,
-        scratch_shapes=[pltpu.VMEM((seq, head), F32), pltpu.VMEM((seq, head), F32), pltpu.VMEM((per * blk, head), F32),
+        scratch_shapes=[pltpu.VMEM((seq, head), F32), pltpu.VMEM((seq, head), F32), pltpu.VMEM((per, head, blk), F32),
                         pltpu.VMEM((per * blk, head), BF16), pltpu.VMEM((per * blk, head), BF16), pltpu.VMEM((1, per * blk), F32),
                         pltpu.SemaphoreType.DMA((2,))],
         compiler_params=pltpu.CompilerParams(dimension_semantics=('arbitrary',), vmem_limit_bytes=VMEM_LIMIT),
         cost_estimate=pl.CostEstimate(flops=10 * pairs * head, bytes_accessed=rows * head * 8 * per + seq * head * 16, transcendentals=pairs),
-    )(q, d_out, o, lse, k, v, *partial)
+    )(q, d_out, o, lse, k, v, k_t, *partial)
 
 
 def solution(mesh):
@@ -371,25 +396,30 @@
             out, pull = jax.vjp(pre_norm, x_f32[z], w_pre)
             normed.append(out)
             pre_pull.append(pull)
-        cosines, sines = rope_tables(gather(positions), head)
+        normed[0], positions = lax.optimization_barrier((normed[0], positions))
+        normed[1], pos_all = lax.optimization_barrier((normed[1], gather(positions)))
+        cosines, sines = rope_tables(pos_all, head)
         w_mine = jnp.concatenate([mine(w_q, n_q, 1), mine(w_k, n_k, 1), mine(w_v, n_k, 1)], axis=1)
         qn = q_norm[None, :]
         kn = k_norm[None, :]
         local = [dot(normed[1], w, NN).astype(BF16).reshape(BLK, group, -1) for w in (w_k, w_v, w_q)]
         local = jnp.concatenate([local[2], local[0], local[1]], axis=2).swapaxes(0, 1)
         local = lax.all_to_all(local, 'sp', 0, 0, tiled=True)
-        qkv = [dot(normed_all[0], w_mine, NN).astype(BF16), local.reshape(group * BLK, -1)]
+        w_mine, cosines, sines = lax.optimization_barrier((w_mine, cosines, sines))
+        qkv_0 = dot(normed_all[0], w_mine, NN).astype(BF16)
+        local, qkv_0, to_gather = lax.optimization_barrier((local, qkv_0, normed[1]))
+        qkv = [qkv_0, local.reshape(group * BLK, -1)]
         q_all, kv = [], ()
         for z in range(2):
             q, *kv = rope_fwd(z, qkv[z], cosines, sines, qn, kn, n_q, n_k, head, kv)
             q_all.append(q)
-        k_all, v_all, to_gather = lax.optimization_barrier((*kv, normed[1]))
+        k_all, v_all, k_t, v_t = kv
         normed_all.append(gather(to_gather))
 
         w_o3 = w_o.reshape(group, n_q * head, width)
         o_all, lse, y_out, dy_f32, d_proj_all, dw_post = [], [], [], [], [], []
         for z in range(2):
-            o, row_lse = attn_fwd(z, q_all[z], k_all, v_all, per, head)
+            o, row_lse = attn_fwd(z, q_all[z], k_all, v_t, per, head)
             o_all.append(o)
             lse.append(row_lse)
         o_mine = [exchange(o_all[0])]
@@ -408,14 +438,14 @@
 
         wo_mine = mine(w_o, n_q, 0)
         do_0 = dot(d_proj_all[0], wo_mine, NT).astype(BF16)
-        dq_0, *partial = attn_bwd(0, q_all[0], do_0, o_all[0], lse[0], k_all, v_all, per, head, ())
+        dq_0, *partial = attn_bwd(0, q_all[0], do_0, o_all[0], lse[0], k_all, v_all, k_t, per, head, ())
         dq_proj_0, gq_0 = rope_bwd(0, dq_0, (), qkv[0], 0, cosines, sines, qn, n_q, head)
         do_1 = dot(d_proj_all[1], wo_mine, NT).astype(BF16)
         dw_o = (dot(o_all[0], d_proj_all[0], TN) + dot(o_all[1], d_proj_all[1], TN)).astype(BF16)
         dq_flat_0 = exchange(dq_proj_0)
         do_1, dw_o, dq_flat_0, partial = lax.optimization_barrier((do_1, dw_o, dq_flat_0, partial))
         dw_o = gather(dw_o)
-        dq_1, dk_all, dv_all = attn_bwd(1, q_all[1], do_1, o_all[1], lse[1], k_all, v_all, per, head, partial)
+        dq_1, dk_all, dv_all = attn_bwd(1, q_all[1], do_1, o_all[1], lse[1], k_all, v_all, k_t, per, head, partial)
         dq_proj_1, gq_1 = rope_bwd(1, dq_1, (), qkv[1], 0, cosines, sines, qn, n_q, head)
         dq_flat = [dq_flat_0, exchange(dq_proj_1)]
 
@@ -433,8 +463,9 @@
         dkv_flat = [exchange(dkv[0])]
         dw_kv = weight_grad(dkv)
         dw_kv, dkv_flat[0], dkv[1] = lax.optimization_barrier((dw_kv, dkv_flat[0], dkv[1]))
-        dw_k = gather(dw_kv[:, :n_k * head], 1)
-        dw_v = gather(dw_kv[:, n_k * head:], 1)
+        top = width // 2
+        dw_kv_top = gather(dw_kv[:top], 1)
+        dw_kv_rest = gather(dw_kv[top:], 1)
         dkv_flat.append(exchange(dkv[1]))
         dw_o = place(dw_o)
 
@@ -453,7 +484,8 @@
         dw_pre, dw_o = lax.optimization_barrier((dw_pre, dw_o))
         sums = lax.psum((dw_pre, dw_post[0] + dw_post[1], jnp.sum(gq_0 + gq_1, axis=0), jnp.sum(gk[0] + gk[1], axis=0)), 'sp')
         dw_q, sums = lax.optimization_barrier((dw_q, sums))
-        return (jnp.concatenate(y_out)[None], jnp.concatenate(dx_out)[None], place(dw_q), place(dw_k), dw_v, dw_o, sums[0], sums[1], sums[2], sums[3])
+        dw_k, dw_v = split_pairs(dw_kv_rest, n_k * head, width, top, split_pairs(dw_kv_top, n_k * head, width, 0, ()))
+        return (jnp.concatenate(y_out)[None], jnp.concatenate(dx_out)[None], place(dw_q), dw_k, dw_v, dw_o, sums[0], sums[1], sums[2], sums[3])
 
     token_spec = P('dp', 'sp', None)
     return jax.shard_map(device_step, mesh=mesh,

time: 1670 us -> 1600 us (0.958)
  blocking collectives: 190 us -> 37.7 us
  waiting for transfers between devices: 300 us -> 378 us
  starting transfers between devices: 26.3 us -> 44.8 us
  local copies, waits for them, and re-layouts: 39.1 us -> 21.2 us
    all_gather x1, blocking collectives: 165 us -> 12.5 us  [gather(): return lax.all_gather(arr, 'sp', axis=axis, tiled=True)]
    all_gather x8, waiting for transfers between devices: 224 us -> 316 us  [gather(): return lax.all_gather(arr, 'sp', axis=axis, tiled=True)]
    pallas_call x0 -> x2, Pallas kernels: none -> 40 us  [split_pairs(): pl.pallas_call(split_kernel, name='split_pairs', grid=(3, parts), in_spec...]
    pallas_call x2, Pallas kernels: 289 us -> 264 us  [attn_bwd(): pl.pallas_call(functools.partial(attn_bwd_kernel, z, per, head, blk), nam...]
    all_to_all x6, starting transfers between devices: 20.8 us -> 40.1 us  [exchange(): lax.all_to_all(arr.reshape(group, -1, arr.shape[1]), 'sp', 0, 0, tiled=True)]
    pallas_call x3 -> x2, Pallas kernels: 69.5 us -> 52.5 us  [place(): pl.pallas_call(copy_kernel, name='place', grid=(x.shape[0] // rows,), in_...]
  transfers between devices with their start and end apart: 15 -> 15, of which waited for: 6 -> 7; matrix products, arithmetic and copies ran while one was open for 32% -> 34% of each run, Pallas kernels for 31% -> 33%
where the time goes in v4:
time: 1600 us
  Pallas kernels  565 us (35%)
  matrix products  437 us (27%)
  waiting for transfers between devices  378 us (24%)
  other arithmetic  99.4 us (6%)
  starting transfers between devices  44.8 us (3%)
  blocking collectives  37.7 us (2%)
  local copies, waits for them, and re-layouts  21.2 us (1%)
    all_gather x8, waiting for transfers between devices, gather(): return lax.all_gather(arr, 'sp', axis=axis, tiled=True)  316 us
    dot_general x12, matrix products, dot(): return lax.dot_general(a, b, dims, preferred_element_type=F32)  270 us
    pallas_call x2, Pallas kernels, attn_bwd(): pl.pallas_call(functools.partial(attn_bwd_kernel, z, per, head, blk), nam...  264 us
    pallas_call x2, Pallas kernels, attn_fwd(): pl.pallas_call(functools.partial(attn_fwd_kernel, z, per, head, blk), nam...  142 us
    dot_general x6, matrix products, back(): jnp.einsum('gtn,dgn->td', flat, w.reshape(width, group, -1), preferred_el...  120 us
    all_to_all x6, waiting for transfers between devices, exchange(): lax.all_to_all(arr.reshape(group, -1, arr.shape[1]), 'sp', 0, 0, tiled=True)  60.5 us
    pallas_call x2, Pallas kernels, place(): pl.pallas_call(copy_kernel, name='place', grid=(x.shape[0] // rows,), in_...  52.5 us
    dot_general x2, matrix products, device_step(): jnp.einsum('gtn,gnd->td', o_mine[z], w_o3, preferred_element_type=F32)  46.7 us
  transfers between devices with their start and end apart: 15, of which 7 were waited for; matrix products, arithmetic and copies ran while one was open for 34% of the time, Pallas kernels for 33%

profile of v4, /device:TPU:0, one launch (start us, length us, event | category | flops | bytes accessed | tf_op | source)
XLA Modules:
  0.0 1597.2 jit_solution(12026842906753196758)
XLA Ops:
  10.4 4.6 slice_bitcast_fusion.1
  15.6 3.3 fusion.26
  19.0 12.5 all_gather.27
  31.5 3.8 fusion.40
  35.4 5.3 fusion.27
  40.7 21.3 %convolution_convert_fusion.3 = bf16[512,4096]{1,0:T(8,128)(2,1)S(1)} fusion(bf16[512,3840]{1,0:T(8,128)(2,1)} %fusion.27, bf16[3840,4096]{1,0:T(8,128)(2,1)} %param.14), kind=kOutput, calls=%fused_computation.98 | convolution fusion | flops 16108224512 | bytes 39583744 | tf_op jit(solution)/shard_map/dot_general | solution.py:23
  64.2 12.1 convolution_convert_fusion.5
  76.3 8.5 convolution_convert_fusion.4
  85.2 3.9 maximum_bitcast_fusion
  89.1 3.7 all-to-all-start
  95.9 18.0 %multiply_sine_fusion = (f32[8192,128]{1,0:T(8,128)}, f32[8192,128]{1,0:T(8,128)}) fusion(f32[128]{0:T(128)S(1)} %multiply_power_fusion, f32[8192]{0:T(1024)S(1)} %convert_multiply_fusion.24), kind=kLoop, calls=%fused_computation.94 | loop fusion | flops 1048576 | bytes 8421888 | tf_op jit(solution)/shard_map/sin | solution.py:43
  116.3 3.8 pad_maximum_fusion
  120.0 115.7 %all-gather.9.cloned.1.call-done = bf16[4096,3840]{1,0:T(8,128)(2,1)} async-done(((bf16[512,3840]{1,0:T(8,128)(2,1)}), bf16[4096,3840]{1,0:T(8,128)(2,1)}) %all-gather.9.cloned.1.call-update) | async-done | bytes 31457296 | tf_op jit(solution)/shard_map/all_gather | solution.py:371
  235.7 39.7 %convolution_convert_fusion.x_ref = bf16[4096,1024]{1,0:T(8,128)(2,1)} fusion(bf16[4096,3840]{1,0:T(8,128)(2,1)} %all-gather.9.cloned.1.call-done, bf16[3840,1024]{1,0:T(8,128)(2,1)} %pad_maximum_fusion), kind=kOutput, calls=%fused_computation.93 | convolution fusion | flops 32216449024 | bytes 47710208 | tf_op jit(solution)/shard_map/dot_general | solution.py:23
  275.5 13.0 rope_fwd.2
  288.5 13.0 rope_fwd.3
  301.5 73.7 %attn_fwd.2 = (bf16[4096,512]{1,0:T(8,128)(2,1)}, f32[2,4096]{1,0:T(2,128)}) custom-call(bf16[4096,512]{1,0:T(8,128)(2,1)} %get-tuple-element.88.q_ref, bf16[8192,256]{1,0:T(8,128)(2,1)} %get-tuple-element.94.k_ref, bf16[256,8192]{1,0:T(8,128)(2,1)} %get-tuple-element.95.vt_ref), custom_call_target="tpu_custom_call" | custom-call | flops 36507222016 | bytes 16777216 | tf_op jit(solution)/shard_map/attn_fwd/pallas_call | solution.py:235
  375.1 23.0 %all-to-all-start.1 = ((bf16[8,512,512]{2,1,0:T(8,128)(2,1)}), bf16[8,512,512]{2,1,0:T(8,128)(2,1)}, u32[]{:S(2)}, u32[]{:S(2)}) async-start(bf16[8,512,512]{2,1,0:T(8,128)(2,1)} %bitcast.124), calls=%async_computation.1 | async-start | bytes 8388608 | tf_op jit(solution)/shard_map/all_to_all | solution.py:374
  398.1 4.3 slice_bitcast_fusion
  402.4 68.6 %attn_fwd.3 = (bf16[4096,512]{1,0:T(8,128)(2,1)}, f32[2,4096]{1,0:T(2,128)}) custom-call(bf16[4096,512]{1,0:T(8,128)(2,1)} %get-tuple-element.97.q_ref, bf16[8192,256]{1,0:T(8,128)(2,1)} %get-tuple-element.94.k_ref, bf16[256,8192]{1,0:T(8,128)(2,1)} %get-tuple-element.95.vt_ref), custom_call_target="tpu_custom_call" | custom-call | flops 36507222016 | bytes 16777216 | tf_op jit(solution)/shard_map/attn_fwd/pallas_call | solution.py:235
  471.0 15.7 all-to-all-done.1
  486.7 3.3 all-to-all-start.2
  490.1 22.3 %fusion.36 = (f32[512]{0:T(512)S(1)}, bf16[512,3840]{1,0:T(8,128)(2,1)S(1)}) fusion(bf16[8,512,512]{2,1,0:T(8,128)(2,1)} %all-to-all-done.1, bf16[8,512,3840]{2,1,0:T(8,128)(2,1)} %bitcast.148), kind=kOutput, calls=%fused_computation.69 | convolution fusion | flops 16113991680 | bytes 39585792 | tf_op jit(solution)/shard_map/gtn,gnd->td/dot_general | solution.py:429
  512.4 8.2 fusion.35
  520.7 3.9 fusion.30
  524.6 14.5 all-to-all-done.2
  539.4 24.4 %fusion.38 = (f32[512]{0:T(512)S(1)}, bf16[512,3840]{1,0:T(8,128)(2,1)S(1)}) fusion(bf16[8,512,512]{2,1,0:T(8,128)(2,1)} %all-to-all-done.2, bf16[8,512,3840]{2,1,0:T(8,128)(2,1)} %bitcast.149), kind=kOutput, calls=%fused_computation.71 | convolution fusion | flops 16113991680 | bytes 39585792 | tf_op jit(solution)/shard_map/gtn,gnd->td/dot_general | solution.py:429
  563.8 5.3 fusion.32
  569.2 6.0 fusion.33
  575.2 109.4 %all-gather.15.cloned.1.call-done = bf16[4096,3840]{1,0:T(8,128)(2,1)} async-done(((bf16[512,3840]{1,0:T(8,128)(2,1)}), bf16[4096,3840]{1,0:T(8,128)(2,1)}) %all-gather.15.cloned.1.call-update) | async-done | bytes 31457296 | tf_op jit(solution)/shard_map/all_gather | solution.py:371
  684.6 23.9 %convolution_convert_fusion.1.do_ref = bf16[4096,512]{1,0:T(8,128)(2,1)} fusion(bf16[4096,3840]{1,0:T(8,128)(2,1)} %all-gather.15.cloned.1.call-done, bf16[4096,3840]{1,0:T(8,128)(2,1)} %param.17, s32[]{:T(128)S(6)} %select_n.8), kind=kOutput, calls=%fused_computation.96 | convolution fusion | flops 16108224512 | bytes 39583748 | tf_op jit(solution)/shard_map/dot_general | solution.py:23
  708.5 122.7 %attn_bwd.2 = (bf16[4096,512]{1,0:T(8,128)(2,1)}, f32[8192,256]{1,0:T(8,128)}, f32[8192,256]{1,0:T(8,128)}) custom-call(bf16[4096,512]{1,0:T(8,128)(2,1)} %get-tuple-element.88.q_ref, bf16[4096,512]{1,0:T(8,128)(2,1)} %convolution_convert_fusion.1.do_ref, bf16[4096,512]{1,0:T(8,128)(2,1)} %get-tuple-element.96.o_ref, f32[2,4096]{1,0:T(2,128)} %get-tuple-element.105.lse_ref, ...), custom_call_target="tpu_custom_call" | custom-call | flops 91268055040 | bytes 50331648 | tf_op jit(solution)/shard_map/attn_bwd/pallas_call | solution.py:351
  831.2 10.6 rope_bwd.4
  845.1 24.1 %fusion.65 = f32[512,3840]{1,0:T(8,128)} fusion(bf16[4096,512]{1,0:T(8,128)(2,1)} %get-tuple-element.96.o_ref, bf16[4096,3840]{1,0:T(8,128)(2,1)} %all-gather.15.cloned.1.call-done), kind=kOutput, calls=%fused_computation.136 | convolution fusion | flops 16106127360 | bytes 43515904 | tf_op jit(solution)/shard_map/dot_general | solution.py:23
  869.3 24.3 %add_convert_fusion.2 = bf16[512,3840]{1,0:T(8,128)(2,1)} fusion(f32[512,3840]{1,0:T(8,128)} %fusion.65, bf16[4096,512]{1,0:T(8,128)(2,1)} %get-tuple-element.100.o_ref, bf16[4096,3840]{1,0:T(8,128)(2,1)} %all-gather.13.cloned.1.call-done), kind=kOutput, calls=%fused_computation.92 | convolution fusion | flops 16110059520 | bytes 47448064 | tf_op jit(solution)/shard_map/dot_general | solution.py:23
  893.6 23.5 %convolution_convert_fusion.2.do_ref = bf16[4096,512]{1,0:T(8,128)(2,1)} fusion(bf16[4096,3840]{1,0:T(8,128)(2,1)} %all-gather.13.cloned.1.call-done, bf16[4096,3840]{1,0:T(8,128)(2,1)} %param.17, s32[]{:T(128)S(6)} %select_n.8), kind=kOutput, calls=%fused_computation.97 | convolution fusion | flops 16108224512 | bytes 39583748 | tf_op jit(solution)/shard_map/dot_general | solution.py:23
  917.0 141.6 %attn_bwd.3 = (bf16[4096,512]{1,0:T(8,128)(2,1)}, bf16[8192,256]{1,0:T(8,128)(2,1)}, bf16[8192,256]{1,0:T(8,128)(2,1)}) custom-call(bf16[4096,512]{1,0:T(8,128)(2,1)} %get-tuple-element.97.q_ref, bf16[4096,512]{1,0:T(8,128)(2,1)} %convolution_convert_fusion.2.do_ref, bf16[4096,512]{1,0:T(8,128)(2,1)} %get-tuple-element.100.o_ref, ...), custom_call_target="tpu_custom_call" | custom-call | flops 91268055040 | bytes 50331648 | tf_op jit(solution)/shard_map/attn_bwd/pallas_call | solution.py:351
  1058.7 10.9 rope_bwd.5
  1069.6 3.7 all-to-all-start.4
  1073.3 21.4 %fusion.66 = f32[3840,512]{1,0:T(8,128)S(1)} fusion(bf16[4096,3840]{1,0:T(8,128)(2,1)} %all-gather.9.cloned.1.call-done, bf16[4096,512]{1,0:T(8,128)(2,1)} %get-tuple-element.109), kind=kOutput, calls=%fused_computation.137 | convolution fusion | flops 16106127360 | bytes 43515904 | tf_op jit(solution)/shard_map/dot_general | solution.py:23
  1094.7 22.5 %add_convert_fusion.1 = bf16[3840,512]{1,0:T(8,128)(2,1)} fusion(f32[3840,512]{1,0:T(8,128)S(1)} %fusion.66, bf16[4096,3840]{1,0:T(8,128)(2,1)} %all-gather.11.cloned.1.call-done, bf16[4096,512]{1,0:T(8,128)(2,1)S(1)} %copy-done.5), kind=kOutput, calls=%fused_computation.91 | convolution fusion | flops 16110059520 | bytes 47448064 | tf_op jit(solution)/shard_map/dot_general | solution.py:23
  1117.3 5.2 all-to-all-done.4
  1122.4 9.0 rope_bwd.6
  1134.8 24.0 %fusion.67 = f32[3840,512]{1,0:T(8,128)} fusion(bf16[4096,3840]{1,0:T(8,128)(2,1)} %all-gather.9.cloned.1.call-done, bf16[4096,512]{1,0:T(8,128)(2,1)} %get-tuple-element.125), kind=kOutput, calls=%fused_computation.138 | convolution fusion | flops 16106127360 | bytes 43515904 | tf_op jit(solution)/shard_map/dot_general | solution.py:23
  1158.7 9.0 rope_bwd.7
  1167.8 24.2 %add_convert_fusion = bf16[3840,512]{1,0:T(8,128)(2,1)} fusion(f32[3840,512]{1,0:T(8,128)} %fusion.67, bf16[4096,3840]{1,0:T(8,128)(2,1)} %all-gather.11.cloned.1.call-done, bf16[4096,512]{1,0:T(8,128)(2,1)} %get-tuple-element.129), kind=kOutput, calls=%fused_computation.90 | convolution fusion | flops 16110059520 | bytes 47448064 | tf_op jit(solution)/shard_map/dot_general | solution.py:23
  1192.0 4.3 fusion.64
  1199.1 24.9 %fusion.2 = f32[512,3840,1]{1,0,2:T(8,128)} fusion(bf16[8,512,512]{2,1,0:T(8,128)(2,1)} %all-to-all-done.3, bf16[480,8,8,512]{3,2,1,0:T(8,128)(2,1)} %bitcast.132), kind=kOutput, calls=%fused_computation.2 | convolution fusion | flops 16106127360 | bytes 43515904 | tf_op jit(solution)/shard_map/gtn,dgn->td/dot_general | solution.py:473
  1224.0 3.5 all-to-all-start.6
  1227.5 25.2 %fusion = f32[512,3840,1]{1,0,2:T(8,128)} fusion(bf16[8,512,512]{2,1,0:T(8,128)(2,1)} %all-to-all-done.4, bf16[480,8,8,512]{3,2,1,0:T(8,128)(2,1)} %bitcast.133), kind=kOutput, calls=%fused_computation | convolution fusion | flops 16106127360 | bytes 43515904 | tf_op jit(solution)/shard_map/gtn,dgn->td/dot_general | solution.py:473
  1252.7 26.0 %place.2 = bf16[4096,3840]{1,0:T(8,128)(2,1)} custom-call(bf16[4096,3840]{1,0:T(8,128)(2,1)} %all-gather.17.cloned.1.call-done.x_ref), custom_call_target="tpu_custom_call" | custom-call | flops 251658240 | bytes 62914560 | tf_op jit(solution)/shard_map/place/pallas_call | solution.py:139
  1278.7 14.8 fusion.8
  1293.5 25.1 %all-to-all-done.6 = bf16[8,512,512]{2,1,0:T(8,128)(2,1)} async-done(((bf16[8,512,512]{2,1,0:T(8,128)(2,1)}), bf16[8,512,512]{2,1,0:T(8,128)(2,1)}, u32[]{:S(2)}, u32[]{:S(2)}) %all-to-all-start.6) | async-done | bytes 4194336 | tf_op jit(solution)/shard_map/all_to_all | solution.py:374
  1318.7 14.9 fusion.6
  1333.6 18.4 %fusion.46 = bf16[512,3840]{1,0:T(8,128)(2,1)} fusion(f32[512,3840,1]{1,0,2:T(8,128)} %fusion.6, f32[512,3840,1]{1,0,2:T(8,128)} %fusion, bf16[480,8,8,256]{3,2,1,0:T(8,128)(2,1)} %bitcast.138, bf16[8,512,512]{2,1,0:T(8,128)(2,1)} %all-to-all-done.6), kind=kOutput, calls=%fused_computation.83 | convolution fusion | flops 8058961920 | bytes 37486592 | tf_op jit(solution)/shard_map/gtn,dgn->td/dot_general | solution.py:473
  1352.0 22.2 %fusion.28 = (f32[3840]{0:T(1024)S(1)}, f32[512]{0:T(512)S(1)}, f32[512]{0:T(512)S(1)}, f32[3840]{0:T(1024)S(1)}, bf16[512,3840]{1,0:T(8,128)(2,1)}) fusion(f32[512]{0:T(512)S(1)} %copy-done.20, bf16[1,1024,3840]{2,1,0:T(8,128)(2,1)} %param.11, f32[3840]{0:T(1024)S(1)} %copy-done.9, bf16[512,3840]{1,0:T(8,128)(2,1)} %fusion.46, f32[512]{0:T(512)S(1)} %copy-done.22, ...), kind=kOutput, calls=%fused_computation.61 | convolution fusion | flops 8090409984 | bytes 49337344 | tf_op jit(solution)/shard_map/gtn,dgn->td/dot_general | solution.py:473
  1374.3 25.2 %all-reduce = (f32[3840]{0:T(1024)}, f32[3840]{0:T(1024)}, f32[256]{0:T(256)}, f32[256]{0:T(256)}) all-reduce(f32[3840]{0:T(1024)S(1)} %add.128, f32[3840]{0:T(1024)S(1)} %copy-done.12, f32[256]{0:T(256)S(1)} %copy-done.30, f32[256]{0:T(256)S(1)} %add_reduce_fusion), channel_id=1, replica_groups=mesh['dp'=1,'sp'=8] {'sp'}, use_global_device_ids=true, to_apply=%region_10.0 | all-reduce | flops 8192 | bytes 65536 | tf_op jit(solution)/shard_map/psum | solution.py:485
  1399.5 18.0 %fusion.34 = (bf16[512,3840]{1,0:T(8,128)(2,1)}, bf16[512,3840]{1,0:T(8,128)(2,1)}, bf16[512,3840]{1,0:T(8,128)(2,1)}) fusion(bf16[512,3840]{1,0:T(8,128)(2,1)} %get-tuple-element.175, f32[512]{0:T(512)S(1)} %multiply_multiply_fusion.1, f32[3840]{0:T(1024)S(1)} %copy-done.9, f32[512]{0:T(512)S(1)} %copy-done.20, bf16[1,1024,3840]{2,1,0:T(8,128)(2,1)} %param.12, ...), kind=kLoop, calls=%fused_computation.67 | loop fusion | flops 49152000 | bytes 39362560 | tf_op jit(solution)/shard_map/convert_element_type | solution.py:482
  1417.5 8.1 maximum_bitcast_fusion.2
  1425.6 7.3 maximum_bitcast_fusion.1
  1433.0 19.0 %split_pairs.2 = (bf16[3840,2048]{1,0:T(8,128)(2,1)}, bf16[3840,2048]{1,0:T(8,128)(2,1)}) custom-call(bf16[1920,4096]{1,0:T(8,128)(2,1)} %all-gather.23.cloned.1.call-done.x_ref), custom_call_target="tpu_custom_call" | custom-call | flops 125829120 | bytes 31457280 | tf_op jit(solution)/shard_map/split_pairs/pallas_call | solution.py:162
  1452.0 21.0 %split_pairs.3 = (bf16[3840,2048]{1,0:T(8,128)(2,1)}, bf16[3840,2048]{1,0:T(8,128)(2,1)}) custom-call(bf16[1920,4096]{1,0:T(8,128)(2,1)} %all-gather.21.cloned.1.call-done.x_ref, bf16[3840,2048]{1,0:T(8,128)(2,1)} %get-tuple-element.139.refs_0_, bf16[3840,2048]{1,0:T(8,128)(2,1)} %get-tuple-element.140.refs_1_), custom_call_target="tpu_custom_call", output_to_operand_aliasing={{0}: (1, {}), {1}: (2, {})} | custom-call | flops 125829120 | bytes 31457280 | tf_op jit(solution)/shard_map/split_pairs/pallas_call | solution.py:162
  1473.0 90.7 %all-gather.19.cloned.1.call-done.x_ref = bf16[3840,4096]{1,0:T(8,128)(2,1)} async-done(((bf16[3840,512]{1,0:T(8,128)(2,1)}), bf16[3840,4096]{1,0:T(8,128)(2,1)}) %all-gather.19.cloned.1.call-update) | async-done | bytes 31457296 | tf_op jit(solution)/shard_map/all_gather | solution.py:371
  1563.7 26.5 %place.3 = bf16[3840,4096]{1,0:T(8,128)(2,1)} custom-call(bf16[3840,4096]{1,0:T(8,128)(2,1)} %all-gather.19.cloned.1.call-done.x_ref), custom_call_target="tpu_custom_call" | custom-call | flops 251658240 | bytes 62914560 | tf_op jit(solution)/shard_map/place/pallas_call | solution.py:139
  (123 shorter events, 21.6 us)
Async XLA Ops:
  7.2 7.8 copy-start.23
  7.2 228.5 %all-gather.9.cloned.1.call-start = ((), (), s32[]{:S(2)}) async-start(), calls=%async_computation.7 | async-start | bytes 35389440 | tf_op jit(solution)/shard_map/all_gather | solution.py:371
  7.2 8.4 copy-start.3
  10.3 4.7 copy-start.15
  15.0 4.0 copy-start.29
  15.0 20.3 %copy-start.8 = (f32[3840]{0:T(1024)}, f32[3840]{0:T(1024)S(1)}, u32[]{:S(2)}) copy-start(f32[3840]{0:T(1024)S(1)} %broadcast_add_fusion.1) | copy-start | bytes 46084
  15.0 0.6 copy-start.19
  35.3 26.7 %copy-start.17 = (f32[512]{0:T(512)}, f32[512]{0:T(512)S(1)}, u32[]{:S(2)}) copy-start(f32[512]{0:T(512)S(1)} %fusion.40) | copy-start | bytes 6148
  35.4 26.7 %copy-start.21 = (f32[512]{0:T(512)}, f32[512]{0:T(512)S(1)}, u32[]{:S(2)}) copy-start(f32[512]{0:T(512)S(1)} %fusion.59) | copy-start | bytes 6148
  62.1 2.1 copy-start.4
  62.1 14.2 slice-start.2
  64.2 12.1 slice-start.3
  64.2 12.1 slice-start.4
  64.2 12.1 slice-start.5
  89.1 186.3 %all-to-all-start = ((bf16[8,512,1024]{2,1,0:T(8,128)(2,1)}), bf16[8,512,1024]{2,1,0:T(8,128)(2,1)}, u32[]{:S(2)}, u32[]{:S(2)}) async-start(bf16[8,512,1024]{2,1,0:T(8,128)(2,1)} %maximum_bitcast_fusion), calls=%async_computation | async-start | bytes 16777216 | tf_op jit(solution)/shard_map/all_to_all | solution.py:407
  92.9 446.2 %all-gather.11.cloned.1.call-start = ((), (), s32[]{:S(2)}) async-start(), calls=%async_computation.8 | async-start | bytes 35389440 | tf_op jit(solution)/shard_map/all_gather | solution.py:371
  375.1 27.3 %copy-start.24 = (f32[3840]{0:T(1024)S(1)}, f32[3840]{0:T(1024)}, u32[]{:S(2)}) copy-start(f32[3840]{0:T(1024)} %param.19) | copy-start | bytes 46084
  375.1 111.5 %all-to-all-start.1 = ((bf16[8,512,512]{2,1,0:T(8,128)(2,1)}), bf16[8,512,512]{2,1,0:T(8,128)(2,1)}, u32[]{:S(2)}, u32[]{:S(2)}) async-start(bf16[8,512,512]{2,1,0:T(8,128)(2,1)} %bitcast.124), calls=%async_computation.1 | async-start | bytes 8388608 | tf_op jit(solution)/shard_map/all_to_all | solution.py:374
  402.4 166.8 %copy-start.6 = (f32[3840]{0:T(1024)}, f32[3840]{0:T(1024)S(1)}, u32[]{:S(2)}) copy-start(f32[3840]{0:T(1024)S(1)} %broadcast_add_fusion) | copy-start | bytes 46084
  486.7 52.4 %all-to-all-start.2 = ((bf16[8,512,512]{2,1,0:T(8,128)(2,1)}), bf16[8,512,512]{2,1,0:T(8,128)(2,1)}, u32[]{:S(2)}, u32[]{:S(2)}) async-start(bf16[8,512,512]{2,1,0:T(8,128)(2,1)} %bitcast.123), calls=%async_computation.2 | async-start | bytes 8388608 | tf_op jit(solution)/shard_map/all_to_all | solution.py:374
  490.0 194.6 %all-gather.15.cloned.1.call-start = ((), (), s32[]{:S(2)}) async-start(), calls=%async_computation.10 | async-start | bytes 35389440 | tf_op jit(solution)/shard_map/all_gather | solution.py:371
  490.0 30.6 %slice-start = ((s8[7864320]{0:T(1024)(128)(4,1)}), s8[4194304]{0:T(1024)(128)(4,1)S(1)}, s32[]{:S(2)}) async-start(s8[7864320]{0:T(1024)(128)(4,1)} %bitcast.120), calls=%async_computation.15 | async-start | bytes 8388608
  490.0 30.6 %slice-start.1 = ((s8[7864320]{0:T(1024)(128)(4,1)}), s8[3670016]{0:T(1024)(128)(4,1)S(1)}, s32[]{:S(2)}) async-start(s8[7864320]{0:T(1024)(128)(4,1)} %bitcast.120), calls=%async_computation.16 | async-start | bytes 7340032
  512.4 8.3 copy-start.2
  512.4 8.3 copy-start.13
  539.1 330.2 %all-gather.13.cloned.1.call-start = ((), (), s32[]{:S(2)}) async-start(), calls=%async_computation.9 | async-start | bytes 35389440 | tf_op jit(solution)/shard_map/all_gather | solution.py:371
  539.4 24.5 %copy-start.1 = (bf16[512,3840]{1,0:T(8,128)(2,1)S(1)}, bf16[512,3840]{1,0:T(8,128)(2,1)}, u32[]{:S(2)}) copy-start(bf16[512,3840]{1,0:T(8,128)(2,1)} %slice_bitcast_fusion) | copy-start | bytes 11796484
  563.8 5.3 copy-start
  841.8 75.2 %all-to-all-start.3 = ((bf16[8,512,512]{2,1,0:T(8,128)(2,1)}), bf16[8,512,512]{2,1,0:T(8,128)(2,1)}, u32[]{:S(2)}, u32[]{:S(2)}) async-start(bf16[8,512,512]{2,1,0:T(8,128)(2,1)} %bitcast.126), calls=%async_computation.3 | async-start | bytes 8388608 | tf_op jit(solution)/shard_map/all_to_all | solution.py:374
  845.1 277.3 %all-gather.17.cloned.1.call-start = ((), (), s32[]{:S(2)}) async-start(), calls=%async_computation.11 | async-start | bytes 35389440 | tf_op jit(solution)/shard_map/all_gather | solution.py:371
  1069.6 52.8 %all-to-all-start.4 = ((bf16[8,512,512]{2,1,0:T(8,128)(2,1)}), bf16[8,512,512]{2,1,0:T(8,128)(2,1)}, u32[]{:S(2)}, u32[]{:S(2)}) async-start(bf16[8,512,512]{2,1,0:T(8,128)(2,1)} %bitcast.128), calls=%async_computation.4 | async-start | bytes 8388608 | tf_op jit(solution)/shard_map/all_to_all | solution.py:374
  1073.3 21.4 %copy-start.5 = (bf16[4096,512]{1,0:T(8,128)(2,1)S(1)}, bf16[4096,512]{1,0:T(8,128)(2,1)}, u32[]{:S(2)}) copy-start(bf16[4096,512]{1,0:T(8,128)(2,1)} %get-tuple-element.119) | copy-start | bytes 12582916
  1131.4 60.6 %all-to-all-start.5 = ((bf16[8,512,512]{2,1,0:T(8,128)(2,1)}), bf16[8,512,512]{2,1,0:T(8,128)(2,1)}, u32[]{:S(2)}, u32[]{:S(2)}) async-start(bf16[8,512,512]{2,1,0:T(8,128)(2,1)} %bitcast.127), calls=%async_computation.5 | async-start | bytes 8388608 | tf_op jit(solution)/shard_map/all_to_all | solution.py:374
  1134.7 298.3 %all-gather.23.cloned.1.call-start = ((), (), s32[]{:S(2)}) async-start(), calls=%async_computation.14 | async-start | bytes 17694720 | tf_op jit(solution)/shard_map/all_gather | solution.py:371
  1192.0 5.8 copy-start.10
  1192.0 5.8 copy-start.11
  1192.0 6.4 copy-start.25
  1192.0 6.4 copy-start.26
  1196.3 255.7 %all-gather.21.cloned.1.call-start = ((), (), s32[]{:S(2)}) async-start(), calls=%async_computation.13 | async-start | bytes 17694720 | tf_op jit(solution)/shard_map/all_gather | solution.py:371
  1197.1 366.6 %all-gather.19.cloned.1.call-start = ((), (), s32[]{:S(2)}) async-start(), calls=%async_computation.12 | async-start | bytes 35389440 | tf_op jit(solution)/shard_map/all_gather | solution.py:371
  1224.0 94.7 %all-to-all-start.6 = ((bf16[8,512,512]{2,1,0:T(8,128)(2,1)}), bf16[8,512,512]{2,1,0:T(8,128)(2,1)}, u32[]{:S(2)}, u32[]{:S(2)}) async-start(bf16[8,512,512]{2,1,0:T(8,128)(2,1)} %bitcast.125), calls=%async_computation.6 | async-start | bytes 8388608 | tf_op jit(solution)/shard_map/all_to_all | solution.py:374
  1252.7 26.0 %copy-start.27 = (f32[8,256]{1,0:T(8,128)S(1)}, f32[8,256]{1,0:T(8,128)}, u32[]{:S(2)}) copy-start(f32[8,256]{1,0:T(8,128)} %get-tuple-element.135) | copy-start | bytes 24580
  1252.7 26.0 %copy-start.28 = (f32[8,256]{1,0:T(8,128)S(1)}, f32[8,256]{1,0:T(8,128)}, u32[]{:S(2)}) copy-start(f32[8,256]{1,0:T(8,128)} %get-tuple-element.136) | copy-start | bytes 24580
  1333.5 18.4 %copy-start.9 = (f32[3840]{0:T(1024)S(1)}, f32[3840]{0:T(1024)}, u32[]{:S(2)}) copy-start(f32[3840]{0:T(1024)} %copy-done.8) | copy-start | bytes 46084
  1333.5 18.4 %copy-start.20 = (f32[512]{0:T(512)S(1)}, f32[512]{0:T(512)}, u32[]{:S(2)}) copy-start(f32[512]{0:T(512)} %copy-done.19) | copy-start | bytes 6148
  1333.6 18.4 %copy-start.22 = (f32[512]{0:T(512)S(1)}, f32[512]{0:T(512)}, u32[]{:S(2)}) copy-start(f32[512]{0:T(512)} %copy-done.21) | copy-start | bytes 6148
  1352.0 22.3 %copy-start.12 = (f32[3840]{0:T(1024)S(1)}, f32[3840]{0:T(1024)}, u32[]{:S(2)}) copy-start(f32[3840]{0:T(1024)} %add.129) | copy-start | bytes 46084
  1352.0 22.3 %copy-start.30 = (f32[256]{0:T(256)S(1)}, f32[256]{0:T(256)}, u32[]{:S(2)}) copy-start(f32[256]{0:T(256)} %add_reduce_fusion.1) | copy-start | bytes 3076
  1352.0 47.4 %copy-start.18 = (f32[512]{0:T(512)S(1)}, f32[512]{0:T(512)}, u32[]{:S(2)}) copy-start(f32[512]{0:T(512)} %copy-done.17) | copy-start | bytes 6148
  1352.0 47.5 %copy-start.16 = (f32[512]{0:T(512)S(1)}, f32[512]{0:T(512)}, u32[]{:S(2)}) copy-start(f32[512]{0:T(512)} %copy-done.15) | copy-start | bytes 6148
  1352.0 47.5 %copy-start.7 = (f32[3840]{0:T(1024)S(1)}, f32[3840]{0:T(1024)}, u32[]{:S(2)}) copy-start(f32[3840]{0:T(1024)} %copy-done.6) | copy-start | bytes 46084
  1352.0 47.5 %copy-start.14 = (f32[512]{0:T(512)S(1)}, f32[512]{0:T(512)}, u32[]{:S(2)}) copy-start(f32[512]{0:T(512)} %copy-done.13) | copy-start | bytes 6148
Sparse Core Ops, SparseCore 0:
  19.1 216.5 all-gather.8
  275.6 206.3 all-gather.10
  539.2 145.3 all-gather.14
  686.3 146.2 all-gather.12
  917.2 147.5 all-gather.16
  1196.5 125.3 all-gather.22
  1323.7 85.6 all-gather.20
  1411.2 152.4 all-gather.18

commit v5 on v4

--- a/solution.py
+++ b/solution.py
@@ -414,7 +414,8 @@
             q, *kv = rope_fwd(z, qkv[z], cosines, sines, qn, kn, n_q, n_k, head, kv)
             q_all.append(q)
         k_all, v_all, k_t, v_t = kv
-        normed_all.append(gather(to_gather))
+        top = width // 2
+        normed_left = gather(to_gather[:, :top])
 
         w_o3 = w_o.reshape(group, n_q * head, width)
         o_all, lse, y_out, dy_f32, d_proj_all, dw_post = [], [], [], [], [], []
@@ -433,24 +434,28 @@
             d_proj, dw = post_pull(dy_f32[z])
             dw_post.append(dw)
             if z == 0:
-                dy_half[1], d_proj, o_mine[1], normed_all[1] = lax.optimization_barrier((dy_half[1], d_proj, o_mine[1], normed_all[1]))
+                dy_half[1], d_proj, o_mine[1], normed_left = lax.optimization_barrier((dy_half[1], d_proj, o_mine[1], normed_left))
             d_proj_all.append(gather(d_proj))
 
         wo_mine = mine(w_o, n_q, 0)
         do_0 = dot(d_proj_all[0], wo_mine, NT).astype(BF16)
         dq_0, *partial = attn_bwd(0, q_all[0], do_0, o_all[0], lse[0], k_all, v_all, k_t, per, head, ())
+        dq_0, to_gather = lax.optimization_barrier((dq_0, to_gather))
+        normed_right = gather(to_gather[:, top:])
         dq_proj_0, gq_0 = rope_bwd(0, dq_0, (), qkv[0], 0, cosines, sines, qn, n_q, head)
         do_1 = dot(d_proj_all[1], wo_mine, NT).astype(BF16)
         dw_o = (dot(o_all[0], d_proj_all[0], TN) + dot(o_all[1], d_proj_all[1], TN)).astype(BF16)
         dq_flat_0 = exchange(dq_proj_0)
-        do_1, dw_o, dq_flat_0, partial = lax.optimization_barrier((do_1, dw_o, dq_flat_0, partial))
+        do_1, dw_o, partial = lax.optimization_barrier((do_1, dw_o, partial))
         dw_o = gather(dw_o)
         dq_1, dk_all, dv_all = attn_bwd(1, q_all[1], do_1, o_all[1], lse[1], k_all, v_all, k_t, per, head, partial)
+        dq_1, normed_right, dq_flat_0 = lax.optimization_barrier((dq_1, normed_right, dq_flat_0))
         dq_proj_1, gq_1 = rope_bwd(1, dq_1, (), qkv[1], 0, cosines, sines, qn, n_q, head)
         dq_flat = [dq_flat_0, exchange(dq_proj_1)]
 
         def weight_grad(grads):
-            return (dot(normed_all[0], grads[0], TN) + dot(normed_all[1], grads[1], TN)).astype(BF16)
+            half_1 = jnp.concatenate([dot(normed_left, grads[1], TN), dot(normed_right, grads[1], TN)])
+            return (dot(normed_all[0], grads[0], TN) + half_1).astype(BF16)
 
         dw_q = weight_grad((dq_proj_0, dq_proj_1))
         dw_q, dw_o, dq_flat[1], dk_all, dv_all = lax.optimization_barrier((dw_q, dw_o, dq_flat[1], dk_all, dv_all))
@@ -463,7 +468,6 @@
         dkv_flat = [exchange(dkv[0])]
         dw_kv = weight_grad(dkv)
         dw_kv, dkv_flat[0], dkv[1] = lax.optimization_barrier((dw_kv, dkv_flat[0], dkv[1]))
-        top = width // 2
         dw_kv_top = gather(dw_kv[:top], 1)
         dw_kv_rest = gather(dw_kv[top:], 1)
         dkv_flat.append(exchange(dkv[1]))

time: 1600 us -> 1630 us (1.019)
    dot_general x12 -> x14, matrix products: 270 us -> 284 us  [dot(): return lax.dot_general(a, b, dims, preferred_element_type=F32)]
    all_gather x8 -> x9, waiting for transfers between devices: 316 us -> 316 us  [gather(): return lax.all_gather(arr, 'sp', axis=axis, tiled=True)]
  transfers between devices with their start and end apart: 15 -> 16, of which waited for: 7 -> 7; matrix products, arithmetic and copies ran while one was open for 34% -> 33% of each run, Pallas kernels for 33% -> 32%
where the time goes in v5:
time: 1630 us; the launch traced here: 1620 us
  Pallas kernels  564 us (35%)
  matrix products  451 us (28%)
  waiting for transfers between devices  388 us (24%)
  other arithmetic  97.2 us (6%)
  starting transfers between devices  45.6 us (3%)
  blocking collectives  37.6 us (2%)
  local copies, waits for them, and re-layouts  24.9 us (2%)
    all_gather x9, waiting for transfers between devices, gather(): return lax.all_gather(arr, 'sp', axis=axis, tiled=True)  316 us
    dot_general x14, matrix products, dot(): return lax.dot_general(a, b, dims, preferred_element_type=F32)  284 us
    pallas_call x2, Pallas kernels, attn_bwd(): pl.pallas_call(functools.partial(attn_bwd_kernel, z, per, head, blk), nam...  265 us
    pallas_call x2, Pallas kernels, attn_fwd(): pl.pallas_call(functools.partial(attn_fwd_kernel, z, per, head, blk), nam...  142 us
    dot_general x6, matrix products, back(): jnp.einsum('gtn,dgn->td', flat, w.reshape(width, group, -1), preferred_el...  121 us
    all_to_all x6, waiting for transfers between devices, exchange(): lax.all_to_all(arr.reshape(group, -1, arr.shape[1]), 'sp', 0, 0, tiled=True)  70.4 us
    pallas_call x2, Pallas kernels, place(): pl.pallas_call(copy_kernel, name='place', grid=(x.shape[0] // rows,), in_...  52.5 us
    dot_general x2, matrix products, device_step(): jnp.einsum('gtn,gnd->td', o_mine[z], w_o3, preferred_element_type=F32)  46.3 us
  transfers between devices with their start and end apart: 16, of which 7 were waited for; matrix products, arithmetic and copies ran while one was open for 33% of the time, Pallas kernels for 32%

profile of v5, /device:TPU:0, one launch (start us, length us, event | category | flops | bytes accessed | tf_op | source)
XLA Modules:
  0.0 1622.6 jit_solution(1334579622975863505)
XLA Ops:
  10.4 4.6 slice_bitcast_fusion.1
  15.5 3.3 fusion.26
  18.9 12.5 all_gather.30
  31.4 3.8 fusion.40
  36.4 3.4 fusion.27
  39.8 22.1 %convolution_convert_fusion.3 = bf16[512,4096]{1,0:T(8,128)(2,1)S(1)} fusion(bf16[512,3840]{1,0:T(8,128)(2,1)S(1)} %fusion.27, bf16[3840,4096]{1,0:T(8,128)(2,1)} %param.14), kind=kOutput, calls=%fused_computation.100 | convolution fusion | flops 16108224512 | bytes 39583744 | tf_op jit(solution)/shard_map/dot_general | solution.py:23
  62.2 11.9 convolution_convert_fusion.5
  74.2 11.9 convolution_convert_fusion.4
  86.6 3.9 maximum_bitcast_fusion
  90.5 3.7 all-to-all-start
  97.2 18.0 %multiply_sine_fusion = (f32[8192,128]{1,0:T(8,128)}, f32[8192,128]{1,0:T(8,128)}) fusion(f32[128]{0:T(128)S(1)} %multiply_power_fusion, f32[8192]{0:T(1024)S(1)} %convert_multiply_fusion.24), kind=kLoop, calls=%fused_computation.96 | loop fusion | flops 1048576 | bytes 8421888 | tf_op jit(solution)/shard_map/sin | solution.py:43
  117.6 3.8 pad_maximum_fusion
  121.4 114.1 %all-gather.10.cloned.1.call-done = bf16[4096,3840]{1,0:T(8,128)(2,1)} async-done(((bf16[512,3840]{1,0:T(8,128)(2,1)}), bf16[4096,3840]{1,0:T(8,128)(2,1)}) %all-gather.10.cloned.1.call-update) | async-done | bytes 31457296 | tf_op jit(solution)/shard_map/all_gather | solution.py:371
  235.5 39.7 %convolution_convert_fusion.x_ref = bf16[4096,1024]{1,0:T(8,128)(2,1)} fusion(bf16[4096,3840]{1,0:T(8,128)(2,1)} %all-gather.10.cloned.1.call-done, bf16[3840,1024]{1,0:T(8,128)(2,1)} %pad_maximum_fusion), kind=kOutput, calls=%fused_computation.95 | convolution fusion | flops 32216449024 | bytes 47710208 | tf_op jit(solution)/shard_map/dot_general | solution.py:23
  278.2 13.0 rope_fwd.2
  291.2 13.0 rope_fwd.3
  304.2 73.1 %attn_fwd.2 = (bf16[4096,512]{1,0:T(8,128)(2,1)}, f32[2,4096]{1,0:T(2,128)}) custom-call(bf16[4096,512]{1,0:T(8,128)(2,1)} %get-tuple-element.92.q_ref, bf16[8192,256]{1,0:T(8,128)(2,1)} %get-tuple-element.98.k_ref, bf16[256,8192]{1,0:T(8,128)(2,1)} %get-tuple-element.99.vt_ref), custom_call_target="tpu_custom_call" | custom-call | flops 36507222016 | bytes 16777216 | tf_op jit(solution)/shard_map/attn_fwd/pallas_call | solution.py:235
  377.3 23.3 %all-to-all-start.1 = ((bf16[8,512,512]{2,1,0:T(8,128)(2,1)}), bf16[8,512,512]{2,1,0:T(8,128)(2,1)}, u32[]{:S(2)}, u32[]{:S(2)}) async-start(bf16[8,512,512]{2,1,0:T(8,128)(2,1)} %bitcast.128), calls=%async_computation.1 | async-start | bytes 8388608 | tf_op jit(solution)/shard_map/all_to_all | solution.py:374
  400.6 4.4 slice_bitcast_fusion
  405.0 68.6 %attn_fwd.3 = (bf16[4096,512]{1,0:T(8,128)(2,1)}, f32[2,4096]{1,0:T(2,128)}) custom-call(bf16[4096,512]{1,0:T(8,128)(2,1)} %get-tuple-element.101.q_ref, bf16[8192,256]{1,0:T(8,128)(2,1)} %get-tuple-element.98.k_ref, bf16[256,8192]{1,0:T(8,128)(2,1)} %get-tuple-element.99.vt_ref), custom_call_target="tpu_custom_call" | custom-call | flops 36507222016 | bytes 16777216 | tf_op jit(solution)/shard_map/attn_fwd/pallas_call | solution.py:235
  477.0 22.3 %fusion.36 = (f32[512]{0:T(512)S(1)}, bf16[512,3840]{1,0:T(8,128)(2,1)S(1)}) fusion(bf16[8,512,512]{2,1,0:T(8,128)(2,1)} %all-to-all-done.1, bf16[8,512,3840]{2,1,0:T(8,128)(2,1)} %bitcast.150), kind=kOutput, calls=%fused_computation.69 | convolution fusion | flops 16113991680 | bytes 39585792 | tf_op jit(solution)/shard_map/gtn,gnd->td/dot_general | solution.py:430
  499.4 8.2 fusion.35
  507.6 3.9 fusion.30
  511.5 15.0 all-to-all-done.2
  526.8 23.9 %fusion.38 = (f32[512]{0:T(512)S(1)}, bf16[512,3840]{1,0:T(8,128)(2,1)S(1)}) fusion(bf16[8,512,512]{2,1,0:T(8,128)(2,1)} %all-to-all-done.2, bf16[8,512,3840]{2,1,0:T(8,128)(2,1)} %bitcast.151), kind=kOutput, calls=%fused_computation.71 | convolution fusion | flops 16113991680 | bytes 39585792 | tf_op jit(solution)/shard_map/gtn,gnd->td/dot_general | solution.py:430
  550.8 5.3 fusion.32
  556.1 6.0 fusion.33
  562.6 110.3 %all-gather.16.cloned.1.call-done = bf16[4096,3840]{1,0:T(8,128)(2,1)} async-done(((bf16[512,3840]{1,0:T(8,128)(2,1)}), bf16[4096,3840]{1,0:T(8,128)(2,1)}) %all-gather.16.cloned.1.call-update) | async-done | bytes 31457296 | tf_op jit(solution)/shard_map/all_gather | solution.py:371
  672.9 23.3 %convolution_convert_fusion.1.do_ref = bf16[4096,512]{1,0:T(8,128)(2,1)} fusion(bf16[4096,3840]{1,0:T(8,128)(2,1)} %all-gather.16.cloned.1.call-done, bf16[4096,3840]{1,0:T(8,128)(2,1)} %param.17, s32[]{:T(128)S(6)} %select_n.8), kind=kOutput, calls=%fused_computation.98 | convolution fusion | flops 16108224512 | bytes 39583748 | tf_op jit(solution)/shard_map/dot_general | solution.py:23
  696.2 122.8 %attn_bwd.2 = (bf16[4096,512]{1,0:T(8,128)(2,1)}, f32[8192,256]{1,0:T(8,128)}, f32[8192,256]{1,0:T(8,128)}) custom-call(bf16[4096,512]{1,0:T(8,128)(2,1)} %get-tuple-element.92.q_ref, bf16[4096,512]{1,0:T(8,128)(2,1)} %convolution_convert_fusion.1.do_ref, bf16[4096,512]{1,0:T(8,128)(2,1)} %get-tuple-element.100.o_ref, f32[2,4096]{1,0:T(2,128)} %get-tuple-element.109.lse_ref, ...), custom_call_target="tpu_custom_call" | custom-call | flops 91268055040 | bytes 50331648 | tf_op jit(solution)/shard_map/attn_bwd/pallas_call | solution.py:351
  820.7 23.8 %fusion.67 = f32[512,3840]{1,0:T(8,128)} fusion(bf16[4096,512]{1,0:T(8,128)(2,1)} %get-tuple-element.100.o_ref, bf16[4096,3840]{1,0:T(8,128)(2,1)} %all-gather.16.cloned.1.call-done), kind=kOutput, calls=%fused_computation.138 | convolution fusion | flops 16106127360 | bytes 43515904 | tf_op jit(solution)/shard_map/dot_general | solution.py:23
  844.5 24.5 %add_convert_fusion = bf16[512,3840]{1,0:T(8,128)(2,1)} fusion(f32[512,3840]{1,0:T(8,128)} %fusion.67, bf16[4096,512]{1,0:T(8,128)(2,1)} %get-tuple-element.104.o_ref, bf16[4096,3840]{1,0:T(8,128)(2,1)} %all-gather.14.cloned.1.call-done), kind=kOutput, calls=%fused_computation.94 | convolution fusion | flops 16110059520 | bytes 47448064 | tf_op jit(solution)/shard_map/dot_general | solution.py:23
  869.0 23.5 %convolution_convert_fusion.2.do_ref = bf16[4096,512]{1,0:T(8,128)(2,1)} fusion(bf16[4096,3840]{1,0:T(8,128)(2,1)} %all-gather.14.cloned.1.call-done, bf16[4096,3840]{1,0:T(8,128)(2,1)} %param.17, s32[]{:T(128)S(6)} %select_n.8), kind=kOutput, calls=%fused_computation.99 | convolution fusion | flops 16108224512 | bytes 39583748 | tf_op jit(solution)/shard_map/dot_general | solution.py:23
  892.5 10.8 rope_bwd.4
  906.7 142.0 %attn_bwd.3 = (bf16[4096,512]{1,0:T(8,128)(2,1)}, bf16[8192,256]{1,0:T(8,128)(2,1)}, bf16[8192,256]{1,0:T(8,128)(2,1)}) custom-call(bf16[4096,512]{1,0:T(8,128)(2,1)} %get-tuple-element.101.q_ref, bf16[4096,512]{1,0:T(8,128)(2,1)} %convolution_convert_fusion.2.do_ref, bf16[4096,512]{1,0:T(8,128)(2,1)} %get-tuple-element.104.o_ref, ...), custom_call_target="tpu_custom_call" | custom-call | flops 91268055040 | bytes 50331648 | tf_op jit(solution)/shard_map/attn_bwd/pallas_call | solution.py:351
  1048.7 10.6 rope_bwd.5
  1059.2 3.7 all-to-all-start.4
  1063.0 12.6 fusion.68
  1075.6 13.9 fusion.69
  1089.5 23.2 %fusion.46 = bf16[3840,512]{1,0:T(8,128)(2,1)} fusion(f32[1920,512]{1,0:T(8,128)} %fusion.69, f32[1920,512]{1,0:T(8,128)S(1)} %fusion.68, bf16[4096,3840]{1,0:T(8,128)(2,1)} %all-gather.10.cloned.1.call-done, bf16[4096,512]{1,0:T(8,128)(2,1)S(1)} %copy-done.6), kind=kOutput, calls=%fused_computation.82 | convolution fusion | flops 16112025600 | bytes 47448064 | tf_op jit(solution)/shard_map/dot_general | solution.py:23
  1112.7 19.7 %all-to-all-done.4 = bf16[8,512,512]{2,1,0:T(8,128)(2,1)} async-done(((bf16[8,512,512]{2,1,0:T(8,128)(2,1)}), bf16[8,512,512]{2,1,0:T(8,128)(2,1)}, u32[]{:S(2)}, u32[]{:S(2)}) %all-to-all-start.4) | async-done | bytes 4194336 | tf_op jit(solution)/shard_map/all_to_all | solution.py:374
  1132.4 9.0 rope_bwd.6
  1141.4 9.0 rope_bwd.7
  1150.4 15.1 fusion.70
  1168.8 15.0 fusion.71
  1183.8 23.2 %fusion.47 = bf16[3840,512]{1,0:T(8,128)(2,1)} fusion(f32[1920,512]{1,0:T(8,128)} %fusion.71, f32[1920,512]{1,0:T(8,128)S(1)} %copy-done.34, bf16[4096,3840]{1,0:T(8,128)(2,1)} %all-gather.10.cloned.1.call-done, bf16[4096,512]{1,0:T(8,128)(2,1)S(1)} %copy-done.7), kind=kOutput, calls=%fused_computation.84 | convolution fusion | flops 16112025600 | bytes 47448064 | tf_op jit(solution)/shard_map/dot_general | solution.py:23
  1207.0 10.8 all-to-all-done.5
  1217.8 4.3 fusion.66
  1224.9 25.0 %fusion.2 = f32[512,3840,1]{1,0,2:T(8,128)} fusion(bf16[8,512,512]{2,1,0:T(8,128)(2,1)} %all-to-all-done.3, bf16[480,8,8,512]{3,2,1,0:T(8,128)(2,1)} %bitcast.136), kind=kOutput, calls=%fused_computation.2 | convolution fusion | flops 16106127360 | bytes 43515904 | tf_op jit(solution)/shard_map/gtn,dgn->td/dot_general | solution.py:477
  1253.2 25.5 %fusion = f32[512,3840,1]{1,0,2:T(8,128)} fusion(bf16[8,512,512]{2,1,0:T(8,128)(2,1)} %all-to-all-done.4, bf16[480,8,8,512]{3,2,1,0:T(8,128)(2,1)} %bitcast.137), kind=kOutput, calls=%fused_computation | convolution fusion | flops 16106127360 | bytes 43515904 | tf_op jit(solution)/shard_map/gtn,dgn->td/dot_general | solution.py:477
  1278.7 26.0 %place.2 = bf16[4096,3840]{1,0:T(8,128)(2,1)} custom-call(bf16[4096,3840]{1,0:T(8,128)(2,1)} %all-gather.20.cloned.1.call-done.x_ref), custom_call_target="tpu_custom_call" | custom-call | flops 251658240 | bytes 62914560 | tf_op jit(solution)/shard_map/place/pallas_call | solution.py:139
  1304.7 14.8 fusion.8
  1319.5 24.8 %all-to-all-done.6 = bf16[8,512,512]{2,1,0:T(8,128)(2,1)} async-done(((bf16[8,512,512]{2,1,0:T(8,128)(2,1)}), bf16[8,512,512]{2,1,0:T(8,128)(2,1)}, u32[]{:S(2)}, u32[]{:S(2)}) %all-to-all-start.6) | async-done | bytes 4194336 | tf_op jit(solution)/shard_map/all_to_all | solution.py:374
  1344.4 14.8 fusion.6
  1359.2 18.4 %fusion.48 = bf16[512,3840]{1,0:T(8,128)(2,1)} fusion(f32[512,3840,1]{1,0,2:T(8,128)} %fusion.6, f32[512,3840,1]{1,0,2:T(8,128)} %fusion, bf16[480,8,8,256]{3,2,1,0:T(8,128)(2,1)} %bitcast.140, bf16[8,512,512]{2,1,0:T(8,128)(2,1)} %all-to-all-done.6), kind=kOutput, calls=%fused_computation.87 | convolution fusion | flops 8058961920 | bytes 37486592 | tf_op jit(solution)/shard_map/gtn,dgn->td/dot_general | solution.py:477
  1377.7 22.2 %fusion.28 = (f32[3840]{0:T(1024)S(1)}, f32[512]{0:T(512)S(1)}, f32[512]{0:T(512)S(1)}, f32[3840]{0:T(1024)S(1)}, bf16[512,3840]{1,0:T(8,128)(2,1)}) fusion(f32[512]{0:T(512)S(1)} %copy-done.23, bf16[1,1024,3840]{2,1,0:T(8,128)(2,1)} %param.11, f32[3840]{0:T(1024)S(1)} %copy-done.12, bf16[512,3840]{1,0:T(8,128)(2,1)} %fusion.48, f32[512]{0:T(512)S(1)} %copy-done.25, ...), kind=kOutput, calls=%fused_computation.61 | convolution fusion | flops 8090409984 | bytes 49337344 | tf_op jit(solution)/shard_map/gtn,dgn->td/dot_general | solution.py:477
  1399.9 25.0 %all-reduce = (f32[3840]{0:T(1024)}, f32[3840]{0:T(1024)}, f32[256]{0:T(256)}, f32[256]{0:T(256)}) all-reduce(f32[3840]{0:T(1024)S(1)} %add.128, f32[3840]{0:T(1024)S(1)} %copy-done.15, f32[256]{0:T(256)S(1)} %copy-done.33, f32[256]{0:T(256)S(1)} %add_reduce_fusion), channel_id=1, replica_groups=mesh['dp'=1,'sp'=8] {'sp'}, use_global_device_ids=true, to_apply=%region_10.0 | all-reduce | flops 8192 | bytes 65536 | tf_op jit(solution)/shard_map/psum | solution.py:489
  1424.9 17.5 %fusion.34 = (bf16[512,3840]{1,0:T(8,128)(2,1)}, bf16[512,3840]{1,0:T(8,128)(2,1)}, bf16[512,3840]{1,0:T(8,128)(2,1)}) fusion(bf16[512,3840]{1,0:T(8,128)(2,1)} %get-tuple-element.183, f32[512]{0:T(512)S(1)} %multiply_multiply_fusion.1, f32[3840]{0:T(1024)S(1)} %copy-done.12, f32[512]{0:T(512)S(1)} %copy-done.23, bf16[1,1024,3840]{2,1,0:T(8,128)(2,1)} %param.12, ...), kind=kLoop, calls=%fused_computation.67 | loop fusion | flops 49152000 | bytes 39362560 | tf_op jit(solution)/shard_map/convert_element_type | solution.py:486
  1442.4 8.4 maximum_bitcast_fusion.2
  1450.8 7.3 maximum_bitcast_fusion.1
  1458.2 19.0 %split_pairs.2 = (bf16[3840,2048]{1,0:T(8,128)(2,1)}, bf16[3840,2048]{1,0:T(8,128)(2,1)}) custom-call(bf16[1920,4096]{1,0:T(8,128)(2,1)} %all-gather.26.cloned.1.call-done.x_ref), custom_call_target="tpu_custom_call" | custom-call | flops 125829120 | bytes 31457280 | tf_op jit(solution)/shard_map/split_pairs/pallas_call | solution.py:162
  1477.2 21.0 %split_pairs.3 = (bf16[3840,2048]{1,0:T(8,128)(2,1)}, bf16[3840,2048]{1,0:T(8,128)(2,1)}) custom-call(bf16[1920,4096]{1,0:T(8,128)(2,1)} %all-gather.24.cloned.1.call-done.x_ref, bf16[3840,2048]{1,0:T(8,128)(2,1)} %get-tuple-element.147.refs_0_, bf16[3840,2048]{1,0:T(8,128)(2,1)} %get-tuple-element.148.refs_1_), custom_call_target="tpu_custom_call", output_to_operand_aliasing={{0}: (1, {}), {1}: (2, {})} | custom-call | flops 125829120 | bytes 31457280 | tf_op jit(solution)/shard_map/split_pairs/pallas_call | solution.py:162
  1498.2 91.2 %all-gather.22.cloned.1.call-done.x_ref = bf16[3840,4096]{1,0:T(8,128)(2,1)} async-done(((bf16[3840,512]{1,0:T(8,128)(2,1)}), bf16[3840,4096]{1,0:T(8,128)(2,1)}) %all-gather.22.cloned.1.call-update) | async-done | bytes 31457296 | tf_op jit(solution)/shard_map/all_gather | solution.py:371
  1589.4 26.5 %place.3 = bf16[3840,4096]{1,0:T(8,128)(2,1)} custom-call(bf16[3840,4096]{1,0:T(8,128)(2,1)} %all-gather.22.cloned.1.call-done.x_ref), custom_call_target="tpu_custom_call" | custom-call | flops 251658240 | bytes 62914560 | tf_op jit(solution)/shard_map/place/pallas_call | solution.py:139
  (129 shorter events, 32.5 us)
Async XLA Ops:
  7.2 7.7 copy-start.26
  7.2 228.3 %all-gather.10.cloned.1.call-start = ((), (), s32[]{:S(2)}) async-start(), calls=%async_computation.7 | async-start | bytes 35389440 | tf_op jit(solution)/shard_map/all_gather | solution.py:371
  7.2 8.3 copy-start.3
  10.3 4.6 copy-start.18
  14.9 4.0 copy-start.32
  14.9 20.3 %copy-start.11 = (f32[3840]{0:T(1024)}, f32[3840]{0:T(1024)S(1)}, u32[]{:S(2)}) copy-start(f32[3840]{0:T(1024)S(1)} %broadcast_add_fusion.1) | copy-start | bytes 46084
  15.0 0.6 copy-start.22
  35.2 0.6 copy-start.20
  35.8 0.5 copy-start.24
  39.8 34.4 %copy-start.4 = (bf16[512,3840]{1,0:T(8,128)(2,1)}, bf16[512,3840]{1,0:T(8,128)(2,1)S(1)}, u32[]{:S(2)}) copy-start(bf16[512,3840]{1,0:T(8,128)(2,1)S(1)} %fusion.27) | copy-start | bytes 11796484
  90.5 184.8 %all-to-all-start = ((bf16[8,512,1024]{2,1,0:T(8,128)(2,1)}), bf16[8,512,1024]{2,1,0:T(8,128)(2,1)}, u32[]{:S(2)}, u32[]{:S(2)}) async-start(bf16[8,512,1024]{2,1,0:T(8,128)(2,1)} %maximum_bitcast_fusion), calls=%async_computation | async-start | bytes 16777216 | tf_op jit(solution)/shard_map/all_to_all | solution.py:407
  94.2 432.3 %all-gather.12.cloned.1.call-start = ((), (), s32[]{:S(2)}) async-start(), calls=%async_computation.8 | async-start | bytes 17694720 | tf_op jit(solution)/shard_map/all_gather | solution.py:371
  377.3 27.7 %copy-start.27 = (f32[3840]{0:T(1024)S(1)}, f32[3840]{0:T(1024)}, u32[]{:S(2)}) copy-start(f32[3840]{0:T(1024)} %param.19) | copy-start | bytes 46084
  377.3 96.3 %all-to-all-start.1 = ((bf16[8,512,512]{2,1,0:T(8,128)(2,1)}), bf16[8,512,512]{2,1,0:T(8,128)(2,1)}, u32[]{:S(2)}, u32[]{:S(2)}) async-start(bf16[8,512,512]{2,1,0:T(8,128)(2,1)} %bitcast.128), calls=%async_computation.1 | async-start | bytes 8388608 | tf_op jit(solution)/shard_map/all_to_all | solution.py:374
  405.0 151.1 %copy-start.9 = (f32[3840]{0:T(1024)}, f32[3840]{0:T(1024)S(1)}, u32[]{:S(2)}) copy-start(f32[3840]{0:T(1024)S(1)} %broadcast_add_fusion) | copy-start | bytes 46084
  473.6 52.9 %all-to-all-start.2 = ((bf16[8,512,512]{2,1,0:T(8,128)(2,1)}), bf16[8,512,512]{2,1,0:T(8,128)(2,1)}, u32[]{:S(2)}, u32[]{:S(2)}) async-start(bf16[8,512,512]{2,1,0:T(8,128)(2,1)} %bitcast.127), calls=%async_computation.2 | async-start | bytes 8388608 | tf_op jit(solution)/shard_map/all_to_all | solution.py:374
  476.9 196.0 %all-gather.16.cloned.1.call-start = ((), (), s32[]{:S(2)}) async-start(), calls=%async_computation.10 | async-start | bytes 35389440 | tf_op jit(solution)/shard_map/all_gather | solution.py:371
  477.0 30.6 %slice-start = ((s8[7864320]{0:T(1024)(128)(4,1)}), s8[4194304]{0:T(1024)(128)(4,1)S(1)}, s32[]{:S(2)}) async-start(s8[7864320]{0:T(1024)(128)(4,1)} %bitcast.124), calls=%async_computation.16 | async-start | bytes 8388608
  477.0 30.6 %slice-start.1 = ((s8[7864320]{0:T(1024)(128)(4,1)}), s8[3670016]{0:T(1024)(128)(4,1)S(1)}, s32[]{:S(2)}) async-start(s8[7864320]{0:T(1024)(128)(4,1)} %bitcast.124), calls=%async_computation.17 | async-start | bytes 7340032
  499.3 8.3 copy-start.2
  499.4 8.3 copy-start.16
  526.5 318.0 %all-gather.14.cloned.1.call-start = ((), (), s32[]{:S(2)}) async-start(), calls=%async_computation.9 | async-start | bytes 35389440 | tf_op jit(solution)/shard_map/all_gather | solution.py:371
  526.8 24.0 %copy-start.1 = (bf16[512,3840]{1,0:T(8,128)(2,1)S(1)}, bf16[512,3840]{1,0:T(8,128)(2,1)}, u32[]{:S(2)}) copy-start(bf16[512,3840]{1,0:T(8,128)(2,1)} %slice_bitcast_fusion) | copy-start | bytes 11796484
  550.8 5.3 copy-start
  562.1 486.5 %all-gather.18.cloned.1.call-start = ((), (), s32[]{:S(2)}) async-start(), calls=%async_computation.11 | async-start | bytes 17694720 | tf_op jit(solution)/shard_map/all_gather | solution.py:371
  696.2 122.8 %copy-start.5 = (bf16[512,3840]{1,0:T(8,128)(2,1)S(1)}, bf16[512,3840]{1,0:T(8,128)(2,1)}, u32[]{:S(2)}) copy-start(bf16[512,3840]{1,0:T(8,128)(2,1)} %copy-done.4) | copy-start | bytes 11796484
  820.5 311.9 %all-gather.20.cloned.1.call-start = ((), (), s32[]{:S(2)}) async-start(), calls=%async_computation.12 | async-start | bytes 35389440 | tf_op jit(solution)/shard_map/all_gather | solution.py:371
  903.4 145.3 %all-to-all-start.3 = ((bf16[8,512,512]{2,1,0:T(8,128)(2,1)}), bf16[8,512,512]{2,1,0:T(8,128)(2,1)}, u32[]{:S(2)}, u32[]{:S(2)}) async-start(bf16[8,512,512]{2,1,0:T(8,128)(2,1)} %bitcast.130), calls=%async_computation.3 | async-start | bytes 8388608 | tf_op jit(solution)/shard_map/all_to_all | solution.py:374
  1059.2 73.2 %all-to-all-start.4 = ((bf16[8,512,512]{2,1,0:T(8,128)(2,1)}), bf16[8,512,512]{2,1,0:T(8,128)(2,1)}, u32[]{:S(2)}, u32[]{:S(2)}) async-start(bf16[8,512,512]{2,1,0:T(8,128)(2,1)} %bitcast.132), calls=%async_computation.4 | async-start | bytes 8388608 | tf_op jit(solution)/shard_map/all_to_all | solution.py:374
  1062.9 12.7 copy-start.8
  1075.6 13.9 copy-start.6
  1165.4 52.4 %all-to-all-start.5 = ((bf16[8,512,512]{2,1,0:T(8,128)(2,1)}), bf16[8,512,512]{2,1,0:T(8,128)(2,1)}, u32[]{:S(2)}, u32[]{:S(2)}) async-start(bf16[8,512,512]{2,1,0:T(8,128)(2,1)} %bitcast.131), calls=%async_computation.5 | async-start | bytes 8388608 | tf_op jit(solution)/shard_map/all_to_all | solution.py:374
  1168.7 289.4 %all-gather.26.cloned.1.call-start = ((), (), s32[]{:S(2)}) async-start(), calls=%async_computation.15 | async-start | bytes 17694720 | tf_op jit(solution)/shard_map/all_gather | solution.py:371
  1168.8 15.0 copy-start.7
  1168.8 15.0 copy-start.34
  1207.0 16.6 %copy-start.13 = (f32[3840]{0:T(1024)S(1)}, f32[3840]{0:T(1024)}, u32[]{:S(2)}) copy-start(f32[3840]{0:T(1024)} %get-tuple-element.156) | copy-start | bytes 46084
  1207.0 16.6 %copy-start.14 = (f32[3840]{0:T(1024)S(1)}, f32[3840]{0:T(1024)}, u32[]{:S(2)}) copy-start(f32[3840]{0:T(1024)} %get-tuple-element.160) | copy-start | bytes 46084
  1207.0 17.3 %copy-start.28 = (f32[8,256]{1,0:T(8,128)S(1)}, f32[8,256]{1,0:T(8,128)}, u32[]{:S(2)}) copy-start(f32[8,256]{1,0:T(8,128)} %get-tuple-element.141) | copy-start | bytes 24580
  1207.0 17.3 %copy-start.29 = (f32[8,256]{1,0:T(8,128)S(1)}, f32[8,256]{1,0:T(8,128)}, u32[]{:S(2)}) copy-start(f32[8,256]{1,0:T(8,128)} %get-tuple-element.142) | copy-start | bytes 24580
  1222.2 255.0 %all-gather.24.cloned.1.call-start = ((), (), s32[]{:S(2)}) async-start(), calls=%async_computation.14 | async-start | bytes 17694720 | tf_op jit(solution)/shard_map/all_gather | solution.py:371
  1222.9 366.5 %all-gather.22.cloned.1.call-start = ((), (), s32[]{:S(2)}) async-start(), calls=%async_computation.13 | async-start | bytes 35389440 | tf_op jit(solution)/shard_map/all_gather | solution.py:371
  1249.9 94.5 %all-to-all-start.6 = ((bf16[8,512,512]{2,1,0:T(8,128)(2,1)}), bf16[8,512,512]{2,1,0:T(8,128)(2,1)}, u32[]{:S(2)}, u32[]{:S(2)}) async-start(bf16[8,512,512]{2,1,0:T(8,128)(2,1)} %bitcast.129), calls=%async_computation.6 | async-start | bytes 8388608 | tf_op jit(solution)/shard_map/all_to_all | solution.py:374
  1278.7 26.0 %copy-start.30 = (f32[8,256]{1,0:T(8,128)S(1)}, f32[8,256]{1,0:T(8,128)}, u32[]{:S(2)}) copy-start(f32[8,256]{1,0:T(8,128)} %get-tuple-element.143) | copy-start | bytes 24580
  1278.7 26.0 %copy-start.31 = (f32[8,256]{1,0:T(8,128)S(1)}, f32[8,256]{1,0:T(8,128)}, u32[]{:S(2)}) copy-start(f32[8,256]{1,0:T(8,128)} %get-tuple-element.144) | copy-start | bytes 24580
  1359.2 18.4 %copy-start.12 = (f32[3840]{0:T(1024)S(1)}, f32[3840]{0:T(1024)}, u32[]{:S(2)}) copy-start(f32[3840]{0:T(1024)} %copy-done.11) | copy-start | bytes 46084
  1359.2 18.4 %copy-start.23 = (f32[512]{0:T(512)S(1)}, f32[512]{0:T(512)}, u32[]{:S(2)}) copy-start(f32[512]{0:T(512)} %copy-done.22) | copy-start | bytes 6148
  1359.2 18.4 %copy-start.25 = (f32[512]{0:T(512)S(1)}, f32[512]{0:T(512)}, u32[]{:S(2)}) copy-start(f32[512]{0:T(512)} %copy-done.24) | copy-start | bytes 6148
  1377.6 22.2 %copy-start.15 = (f32[3840]{0:T(1024)S(1)}, f32[3840]{0:T(1024)}, u32[]{:S(2)}) copy-start(f32[3840]{0:T(1024)} %add.129) | copy-start | bytes 46084
  1377.6 22.2 %copy-start.33 = (f32[256]{0:T(256)S(1)}, f32[256]{0:T(256)}, u32[]{:S(2)}) copy-start(f32[256]{0:T(256)} %add_reduce_fusion.1) | copy-start | bytes 3076
  1377.6 47.2 %copy-start.21 = (f32[512]{0:T(512)S(1)}, f32[512]{0:T(512)}, u32[]{:S(2)}) copy-start(f32[512]{0:T(512)} %copy-done.20) | copy-start | bytes 6148
  1377.6 47.2 %copy-start.19 = (f32[512]{0:T(512)S(1)}, f32[512]{0:T(512)}, u32[]{:S(2)}) copy-start(f32[512]{0:T(512)} %copy-done.18) | copy-start | bytes 6148
  1377.7 47.3 %copy-start.10 = (f32[3840]{0:T(1024)S(1)}, f32[3840]{0:T(1024)}, u32[]{:S(2)}) copy-start(f32[3840]{0:T(1024)} %copy-done.9) | copy-start | bytes 46084
  1377.7 47.3 %copy-start.17 = (f32[512]{0:T(512)S(1)}, f32[512]{0:T(512)}, u32[]{:S(2)}) copy-start(f32[512]{0:T(512)} %copy-done.16) | copy-start | bytes 6148
Sparse Core Ops, SparseCore 0:
  19.0 216.4 all-gather.9
  278.3 102.1 all-gather.11
  526.7 146.1 all-gather.15
  674.6 146.2 all-gather.13
  822.5 79.7 all-gather.17
  903.9 217.6 all-gather.19
  1222.3 123.2 all-gather.25
  1347.4 87.6 all-gather.23
  1436.9 152.4 all-gather.21
